TPU v7x, 32 devices: a whole 2x2x4 slice. The times are simulated.
32 devices in a mesh: member: 2 (over y), tile: 4 (over z), lev: 2 (over x), sub: 2 (over core).
Axes of the slice: x: 2, y: 2, z: 4, core: 2. Of those that a mesh axis runs over, the one named last changes fastest.
Arguments:
- increment: float32 [4, 1024, 128], P(('member', 'lev'), ('tile', 'sub')), parts along dimension 0, may hold values from -6 to 6
- residual: float32 [4, 1024, 128], P(('member', 'lev'), ('tile', 'sub')), parts along dimension 0, may hold values from -6 to 6
- direction: float32 [4, 1024, 128], P(('member', 'lev'), ('tile', 'sub')), parts along dimension 0, may hold values from -6 to 6
- wind_u: bfloat16 [4, 1024, 128], P(('member', 'lev'), ('tile', 'sub')), parts along dimension 0, may hold values from -0.3984375 to 0.3984375
- wind_v: bfloat16 [4, 1024, 128], P(('member', 'lev'), ('tile', 'sub')), parts along dimension 0, may hold values from -0.3984375 to 0.3984375
- diffusion: float32 [2], replicated, may hold values from 0.03 to 0.12
- vertical: float32 [2], replicated, may hold values from 0.02 to 0.1
- background_inv: float32 [2], replicated, may hold values from 0.5 to 2
- side_pair: int32 [8, 4], replicated, may hold values from 0 to 31, as said below
- side_flip: int32 [8, 4], replicated, may hold values from 0 to 1, as said below
- obs_column: int32 [512], P(('tile', 'sub')), may hold values from 0 to 131071, as said below
- obs_time: int32 [512], P(('tile', 'sub')), may hold values from 1 to 4
- obs_count: int32 [8], P(('tile', 'sub')), may hold values from 48 to 64, as said below
- jacobian: bfloat16 [512, 2, 616], P(('tile', 'sub'), 'lev'), may hold values from -4 to 4
- error_inv: float32 [616], replicated, may hold values from 0.2 to 5
Outputs:
- increment_new: float32 [4, 1024, 128], P(('member', 'lev'), ('tile', 'sub')), parts along dimension 0
- residual_new: float32 [4, 1024, 128], P(('member', 'lev'), ('tile', 'sub')), parts along dimension 0
- direction_new: float32 [4, 1024, 128], P(('member', 'lev'), ('tile', 'sub')), parts along dimension 0
There are 2 independent parts, one for each index of `member`. A program takes and returns all parts, laid end to end along the dimension named above; an argument that names none is the same for every part. Nothing has to cross between parts.
Inputs may be any that keep to these rules, and one draw needn't show every extreme that they name: side_pair[side_pair[k]] == k for every side k, and side_pair[k] is a side of another panel, so the panels close into one surface joined edge to edge. side_flip is equal on both sides of a pair. `obs_column`: among the live slots of one owner at most 16 name columns of one panel, and every owner reaches 16 for some panel. `obs_count`: some owner has all 64 slots live.
All inputs are finite; a program needn't handle non-finite values.
Results may differ from a plain program's by a relative error of at most 0.0003.
Values sent between devices are 32-bit elements; how exact they have to be, the bound alone decides.
No kernel may reach another device: no remote copies, remote signals or barrier semaphores. Data moves between devices by JAX's collectives and lax.ppermute only.
A program may use at most 64 MiB of HBM per device.

v0:
```python
import jax
import jax.numpy as jnp
from jax import lax
from jax.sharding import PartitionSpec as P

STEPS = 4


def with_halo(block, sides, width):
    for axis, dim in sides:
        count = lax.axis_size(axis)
        forward = [(i, i + 1) for i in range(count - 1)]
        backward = [(target, source) for source, target in forward]
        low = lax.ppermute(
            lax.slice_in_dim(block, block.shape[dim] - width, None, axis=dim), axis, forward
        )
        high = lax.ppermute(lax.slice_in_dim(block, 0, width, axis=dim), axis, backward)
        block = jnp.concatenate([low, block, high], axis=dim)
    return block


def neighbours(strips, pair_rows, flip_rows):
    everyone = lax.all_gather(strips, ("tile", "sub"), axis=0, tiled=True)
    picked = everyone[pair_rows]
    return jnp.where(flip_rows[:, None, None] == 1, picked[:, :, ::-1], picked)


def level_padded(field):
    return with_halo(field, (("lev", 0),), 1)


def body(
    increment,
    residual,
    direction,
    wind_u,
    wind_v,
    diffusion,
    vertical,
    background_inv,
    side_pair,
    side_flip,
    obs_column,
    obs_time,
    obs_count,
    jacobian,
    error_inv,
):
    depth = increment.shape[0]
    width = increment.shape[2]
    slots = obs_column.shape[0]
    panels = lax.axis_size(("tile", "sub"))
    capacity = max(2, (2 * slots + panels - 1) // panels)
    panel = lax.axis_index(("tile", "sub"))
    first_level = lax.axis_index("lev") * depth
    mixing = lax.dynamic_slice_in_dim(diffusion, first_level, depth)[:, None, None]
    blending = lax.dynamic_slice_in_dim(vertical, first_level, depth)[:, None, None]
    prior = lax.dynamic_slice_in_dim(background_inv, first_level, depth)[:, None, None]
    pair_rows = lax.dynamic_index_in_dim(side_pair, panel, 0, keepdims=False)
    flip_rows = lax.dynamic_index_in_dim(side_flip, panel, 0, keepdims=False)
    speed_u = wind_u.astype(jnp.float32)
    speed_v = wind_v.astype(jnp.float32)
    coefs = (
        mixing + 0.5 * speed_u,
        mixing - 0.5 * speed_u,
        mixing + 0.5 * speed_v,
        mixing - 0.5 * speed_v,
    )
    center = 1.0 - 4.0 * mixing - 2.0 * blending

    def forward(field):
        strips = jnp.stack([field[:, 0, :], field[:, -1, :], field[:, :, 0], field[:, :, -1]])
        halos = neighbours(strips, pair_rows, flip_rows)
        north = jnp.concatenate([halos[0][:, None, :], field[:, :-1, :]], axis=1)
        south = jnp.concatenate([field[:, 1:, :], halos[1][:, None, :]], axis=1)
        west = jnp.concatenate([halos[2][:, :, None], field[:, :, :-1]], axis=2)
        east = jnp.concatenate([field[:, :, 1:], halos[3][:, :, None]], axis=2)
        padded = level_padded(field)
        return (
            center * field
            + coefs[0] * north
            + coefs[1] * south
            + coefs[2] * west
            + coefs[3] * east
            + blending * (padded[:-2] + padded[2:])
        )

    def adjoint(field):
        prods = [c * field for c in coefs]
        strips = jnp.stack(
            [prods[0][:, 0, :], prods[1][:, -1, :], prods[2][:, :, 0], prods[3][:, :, -1]]
        )
        halos = neighbours(strips, pair_rows, flip_rows)
        rows_term = jnp.concatenate([prods[0][:, 1:, :], halos[1][:, None, :]], axis=1)
        rows_term = rows_term + jnp.concatenate([halos[0][:, None, :], prods[1][:, :-1, :]], axis=1)
        cols_term = jnp.concatenate([prods[2][:, :, 1:], halos[3][:, :, None]], axis=2)
        cols_term = cols_term + jnp.concatenate([halos[2][:, :, None], prods[3][:, :, :-1]], axis=2)
        padded = level_padded(blending * field)
        return center * field + rows_term + cols_term + padded[:-2] + padded[2:]

    state = direction
    states = []
    for step in range(STEPS):
        state = forward(state)
        states.append(state.reshape(depth, width * width))
    history = jnp.stack(states, axis=0)
    area = width * width
    alive = jnp.arange(slots, dtype=jnp.int32) < obs_count[0]
    targets = obs_column // area
    cells = obs_column % area
    owned = (
        (targets[:, None] == jnp.arange(panels, dtype=jnp.int32)[None, :]) & alive[:, None]
    ).astype(jnp.int32)
    rank = jnp.sum((jnp.cumsum(owned, axis=0) - owned) * owned, axis=1)
    position = jnp.where(alive, targets * capacity + rank, panels * capacity)
    want_cell = (
        jnp.zeros((panels * capacity,), jnp.int32)
        .at[position]
        .set(cells, mode="drop")
        .reshape(panels, capacity)
    )
    want_time = (
        jnp.ones((panels * capacity,), jnp.int32)
        .at[position]
        .set(obs_time, mode="drop")
        .reshape(panels, capacity)
    )
    asked_cell = lax.all_to_all(want_cell, ("tile", "sub"), split_axis=0, concat_axis=0, tiled=True)
    asked_time = lax.all_to_all(want_time, ("tile", "sub"), split_axis=0, concat_axis=0, tiled=True)
    values = history[asked_time - 1, :, asked_cell]
    sent = lax.all_to_all(values, ("tile", "sub"), split_axis=0, concat_axis=0, tiled=True)
    gathered = sent.reshape(panels * capacity, depth)[jnp.minimum(position, panels * capacity - 1)]
    wide = jacobian.astype(jnp.float32)
    partial_value = jnp.einsum("olc,ol->oc", wide, gathered, precision=lax.Precision.HIGHEST)
    departure = lax.psum(partial_value, "lev")
    weighted = departure * error_inv[None, :]
    back = jnp.einsum("olc,oc->ol", wide, weighted, precision=lax.Precision.HIGHEST)
    back = back * alive.astype(jnp.float32)[:, None]
    outgoing = (
        jnp.zeros((panels * capacity, depth), jnp.float32)
        .at[position]
        .set(back, mode="drop")
        .reshape(panels, capacity, depth)
    )
    incoming = lax.all_to_all(outgoing, ("tile", "sub"), split_axis=0, concat_axis=0, tiled=True)
    flat_cell = asked_cell.reshape(panels * capacity)
    flat_time = asked_time.reshape(panels * capacity) - 1
    forcing = (
        jnp.zeros((STEPS, depth, area), jnp.float32)
        .at[flat_time, :, flat_cell]
        .add(incoming.reshape(panels * capacity, depth))
    )
    forcing = forcing.reshape(STEPS, depth, width, width)
    sensitivity = forcing[STEPS - 1]
    for step in range(STEPS - 1, 0, -1):
        sensitivity = adjoint(sensitivity) + forcing[step - 1]
    sensitivity = adjoint(sensitivity)
    image = prior * direction + sensitivity
    norm_old, curvature, cross, square = lax.psum(
        (
            jnp.sum(residual * residual),
            jnp.sum(direction * image),
            jnp.sum(residual * image),
            jnp.sum(image * image),
        ),
        ("tile", "lev", "sub"),
    )
    alpha = norm_old / curvature
    increment_new = increment + alpha * direction
    residual_new = residual - alpha * image
    norm_new = norm_old - 2.0 * alpha * cross + alpha * alpha * square
    direction_new = residual_new + norm_new / norm_old * direction
    return (increment_new, residual_new, direction_new)


def solution(mesh):
    placed = (
        P(("member", "lev"), ("tile", "sub"), None),
        P(("member", "lev"), ("tile", "sub"), None),
        P(("member", "lev"), ("tile", "sub"), None),
        P(("member", "lev"), ("tile", "sub"), None),
        P(("member", "lev"), ("tile", "sub"), None),
        P(),
        P(),
        P(),
        P(),
        P(),
        P(("tile", "sub")),
        P(("tile", "sub")),
        P(("tile", "sub")),
        P(("tile", "sub"), "lev", None),
        P(),
    )
    return jax.shard_map(
        body,
        mesh=mesh,
        in_specs=placed,
        out_specs=(
            P(("member", "lev"), ("tile", "sub"), None),
            P(("member", "lev"), ("tile", "sub"), None),
            P(("member", "lev"), ("tile", "sub"), None),
        ),
        check_vma=False,
    )
```

profile of v0, /device:TPU:0, one launch (start us, length us, event | category | flops | bytes accessed | tf_op | source)
XLA Modules:
  0.0 299.5 jit_solution(5029368264383714935)
XLA Ops:
  7.2 1.3 collective-permute-start.1
  8.5 4.9 %collective-permute-start = (f32[1,128,128]{2,1,0:T(8,128)}, f32[1,128,128]{2,1,0:T(8,128)S(1)}, u32[]{:S(2)}, u32[]{:S(2)}) collective-permute-start(f32[1,128,128]{2,1,0:T(8,128)} %param.17), channel_id=1, source_target_pairs={{0,2},{1,3},{4,6},{5,7},{8,10},{9,11},{12,14},{13,15},{16,18},{17,... | collective-permute-start | bytes 196616 | tf_op jit(solution)/shard_map/ppermute | solution.py:14
  16.5 6.0 %all-to-all-start.1 = ((s32[8,1,16]{2,1,0:T(1,128)}), s32[8,1,16]{2,1,0:T(1,128)S(1)}, u32[]{:S(2)}, u32[]{:S(2)}) async-start(s32[8,1,16]{2,1,0:T(1,128)} %bitcast.6), calls=%async_computation.1 | async-start | bytes 8192 | tf_op jit(solution)/shard_map/all_to_all | solution.py:128
  24.0 13.3 %all_gather.24 = f32[32,1,128]{2,1,0:T(1,128)S(1)} all-gather(f32[4,1,128]{2,1,0:T(1,128)S(1)} %pad_maximum_fusion), channel_id=1, replica_groups=mesh['member'=2,'tile'=4,'lev'=2,'sub'=2] {'tile','sub'}, dimensions={0}, use_global_device_ids=true | all-gather | bytes 18432 | tf_op jit(solution)/shard_map/all_gather | solution.py:23
  38.0 0.9 scatter_custom_fusion
  39.6 3.3 %all-to-all-start = ((s32[8,1,16]{2,1,0:T(1,128)}), s32[8,1,16]{2,1,0:T(1,128)S(1)}, u32[]{:S(2)}, u32[]{:S(2)}) async-start(s32[8,1,16]{2,1,0:T(1,128)} %bitcast.3), calls=%async_computation | async-start | bytes 8192 | tf_op jit(solution)/shard_map/all_to_all | solution.py:129
  46.4 2.0 all-to-all-done
  48.5 1.4 fusion.5
  50.1 1.3 collective-permute-start.3
  51.4 4.5 %collective-permute-start.2 = (f32[1,128,128]{2,1,0:T(8,128)S(1)}, f32[1,128,128]{2,1,0:T(8,128)S(1)}, u32[]{:S(2)}, u32[]{:S(2)}) collective-permute-start(f32[1,128,128]{2,1,0:T(8,128)S(1)} %fusion.5), channel_id=1, source_target_pairs={{0,2},{1,3},{4,6},{5,7},{8,10},{9,11},{12,14},{13,15},{16,18},{17,... | collective-permute-start | bytes 196616 | tf_op jit(solution)/shard_map/ppermute | solution.py:14
  56.1 12.8 %all_gather.25 = f32[32,1,128]{2,1,0:T(1,128)S(1)} all-gather(f32[4,1,128]{2,1,0:T(1,128)S(1)} %pad_maximum_fusion.1), channel_id=1, replica_groups=mesh['member'=2,'tile'=4,'lev'=2,'sub'=2] {'tile','sub'}, dimensions={0}, use_global_device_ids=true | all-gather | bytes 18432 | tf_op jit(solution)/shard_map/all_gather | solution.py:23
  69.8 1.4 fusion.10
  71.4 1.3 collective-permute-start.5
  72.7 4.5 %collective-permute-start.4 = (f32[1,128,128]{2,1,0:T(8,128)S(1)}, f32[1,128,128]{2,1,0:T(8,128)S(1)}, u32[]{:S(2)}, u32[]{:S(2)}) collective-permute-start(f32[1,128,128]{2,1,0:T(8,128)S(1)} %fusion.10), channel_id=1, source_target_pairs={{0,2},{1,3},{4,6},{5,7},{8,10},{9,11},{12,14},{13,15},{16,18},{17,... | collective-permute-start | bytes 196616 | tf_op jit(solution)/shard_map/ppermute | solution.py:14
  77.4 12.8 %all_gather.26 = f32[32,1,128]{2,1,0:T(1,128)S(1)} all-gather(f32[4,1,128]{2,1,0:T(1,128)S(1)} %pad_maximum_fusion.2), channel_id=1, replica_groups=mesh['member'=2,'tile'=4,'lev'=2,'sub'=2] {'tile','sub'}, dimensions={0}, use_global_device_ids=true | all-gather | bytes 18432 | tf_op jit(solution)/shard_map/all_gather | solution.py:23
  91.1 1.4 fusion.15
  92.7 1.3 collective-permute-start.7
  94.0 4.5 %collective-permute-start.6 = (f32[1,128,128]{2,1,0:T(8,128)S(1)}, f32[1,128,128]{2,1,0:T(8,128)S(1)}, u32[]{:S(2)}, u32[]{:S(2)}) collective-permute-start(f32[1,128,128]{2,1,0:T(8,128)S(1)} %fusion.15), channel_id=1, source_target_pairs={{0,2},{1,3},{4,6},{5,7},{8,10},{9,11},{12,14},{13,15},{16,18},{17,... | collective-permute-start | bytes 196616 | tf_op jit(solution)/shard_map/ppermute | solution.py:14
  98.7 12.8 %all_gather.27 = f32[32,1,128]{2,1,0:T(1,128)S(1)} all-gather(f32[4,1,128]{2,1,0:T(1,128)S(1)} %pad_maximum_fusion.3), channel_id=1, replica_groups=mesh['member'=2,'tile'=4,'lev'=2,'sub'=2] {'tile','sub'}, dimensions={0}, use_global_device_ids=true | all-gather | bytes 18432 | tf_op jit(solution)/shard_map/all_gather | solution.py:23
  112.4 1.4 fusion.20
  114.1 1.5 gather_fusion.4
  116.3 3.3 %all-to-all-start.2 = ((f32[8,16,1]{1,2,0:T(1,128)}), f32[8,16,1]{1,2,0:T(1,128)S(1)}, u32[]{:S(2)}, u32[]{:S(2)}) async-start(f32[8,16,1]{1,2,0:T(1,128)} %bitcast.47), calls=%async_computation.2 | async-start | bytes 8192 | tf_op jit(solution)/shard_map/all_to_all | solution.py:131
  122.2 2.9 all-to-all-done.2
  126.3 0.8 gather_fusion.5
  128.1 19.5 %all-reduce.3.cloned.1.call-done = f32[64,616]{1,0:T(8,128)} async-done(((f32[64,616]{1,0:T(8,128)}), f32[64,616]{1,0:T(8,128)}) %all-reduce.3.cloned.1.call-update) | async-done | bytes 157712 | tf_op jit(solution)/shard_map/psum | solution.py:135
  147.6 1.0 fusion
  148.7 0.8 scatter_custom_fusion.2
  150.1 4.6 %all-to-all-start.3 = ((f32[8,16,1]{1,2,0:T(1,128)}), f32[8,16,1]{1,2,0:T(1,128)S(1)}, u32[]{:S(2)}, u32[]{:S(2)}) async-start(f32[8,16,1]{1,2,0:T(1,128)} %bitcast.49), calls=%async_computation.3 | async-start | bytes 8192 | tf_op jit(solution)/shard_map/all_to_all | solution.py:145
  154.8 5.5 %all-to-all-done.3 = f32[8,16,1]{1,2,0:T(1,128)S(1)} async-done(((f32[8,16,1]{1,2,0:T(1,128)}), f32[8,16,1]{1,2,0:T(1,128)S(1)}, u32[]{:S(2)}, u32[]{:S(2)}) %all-to-all-start.3) | async-done | bytes 544 | tf_op jit(solution)/shard_map/all_to_all | solution.py:145
  161.0 6.8 %scatter_fusion = f32[4,16384]{1,0:T(4,128)S(1)} fusion(f32[4,16384]{1,0:T(4,128)S(1)} %broadcast.219, s32[128]{0:T(128)S(1)} %fusion.71, f32[128]{0:T(128)S(1)} %reshape.842), kind=kCustom, calls=%fused_computation.13 | custom fusion | flops 128 | bytes 2560 | tf_op jit(solution)/shard_map/scatter-add | solution.py:151
  168.0 1.3 fusion.56
  169.4 1.3 collective-permute-start.9
  170.7 4.5 %collective-permute-start.8 = (f32[1,128,128]{2,1,0:T(8,128)S(1)}, f32[1,128,128]{2,1,0:T(8,128)S(1)}, u32[]{:S(2)}, u32[]{:S(2)}) collective-permute-start(f32[1,128,128]{2,1,0:T(8,128)S(1)} %get-tuple-element.57), channel_id=1, source_target_pairs={{0,2},{1,3},{4,6},{5,7},{8,10},{9,11},{12,14},{13,15},{16,18},{17,... | collective-permute-start | bytes 196616 | tf_op jit(solution)/shard_map/ppermute | solution.py:14
  175.4 12.8 %all_gather.28 = f32[32,1,128]{2,1,0:T(1,128)S(1)} all-gather(f32[4,1,128]{2,1,0:T(1,128)S(1)} %pad_maximum_fusion.4), channel_id=1, replica_groups=mesh['member'=2,'tile'=4,'lev'=2,'sub'=2] {'tile','sub'}, dimensions={0}, use_global_device_ids=true | all-gather | bytes 18432 | tf_op jit(solution)/shard_map/all_gather | solution.py:23
  190.0 1.3 fusion.45
  191.3 1.3 collective-permute-start.11
  192.6 4.5 %collective-permute-start.10 = (f32[1,128,128]{2,1,0:T(8,128)S(1)}, f32[1,128,128]{2,1,0:T(8,128)S(1)}, u32[]{:S(2)}, u32[]{:S(2)}) collective-permute-start(f32[1,128,128]{2,1,0:T(8,128)S(1)} %get-tuple-element.56), channel_id=1, source_target_pairs={{0,2},{1,3},{4,6},{5,7},{8,10},{9,11},{12,14},{13,15},{16,18},{17,... | collective-permute-start | bytes 196616 | tf_op jit(solution)/shard_map/ppermute | solution.py:14
  197.5 12.8 %all_gather.29 = f32[32,1,128]{2,1,0:T(1,128)S(1)} all-gather(f32[4,1,128]{2,1,0:T(1,128)S(1)} %pad_maximum_fusion.5), channel_id=1, replica_groups=mesh['member'=2,'tile'=4,'lev'=2,'sub'=2] {'tile','sub'}, dimensions={0}, use_global_device_ids=true | all-gather | bytes 18432 | tf_op jit(solution)/shard_map/all_gather | solution.py:23
  212.1 1.3 fusion.44
  213.5 1.3 collective-permute-start.13
  214.8 4.5 %collective-permute-start.12 = (f32[1,128,128]{2,1,0:T(8,128)S(1)}, f32[1,128,128]{2,1,0:T(8,128)S(1)}, u32[]{:S(2)}, u32[]{:S(2)}) collective-permute-start(f32[1,128,128]{2,1,0:T(8,128)S(1)} %get-tuple-element.54), channel_id=1, source_target_pairs={{0,2},{1,3},{4,6},{5,7},{8,10},{9,11},{12,14},{13,15},{16,18},{17,... | collective-permute-start | bytes 196616 | tf_op jit(solution)/shard_map/ppermute | solution.py:14
  219.6 12.8 %all_gather.30 = f32[32,1,128]{2,1,0:T(1,128)S(1)} all-gather(f32[4,1,128]{2,1,0:T(1,128)S(1)} %pad_maximum_fusion.6), channel_id=1, replica_groups=mesh['member'=2,'tile'=4,'lev'=2,'sub'=2] {'tile','sub'}, dimensions={0}, use_global_device_ids=true | all-gather | bytes 18432 | tf_op jit(solution)/shard_map/all_gather | solution.py:23
  234.3 1.3 fusion.43
  235.6 1.3 collective-permute-start.15
  236.9 4.5 %collective-permute-start.14 = (f32[1,128,128]{2,1,0:T(8,128)S(1)}, f32[1,128,128]{2,1,0:T(8,128)S(1)}, u32[]{:S(2)}, u32[]{:S(2)}) collective-permute-start(f32[1,128,128]{2,1,0:T(8,128)S(1)} %get-tuple-element.52), channel_id=1, source_target_pairs={{0,2},{1,3},{4,6},{5,7},{8,10},{9,11},{12,14},{13,15},{16,18},{17,... | collective-permute-start | bytes 196616 | tf_op jit(solution)/shard_map/ppermute | solution.py:14
  241.8 12.8 %all_gather.31 = f32[32,1,128]{2,1,0:T(1,128)S(1)} all-gather(f32[4,1,128]{2,1,0:T(1,128)S(1)} %pad_maximum_fusion.7), channel_id=1, replica_groups=mesh['member'=2,'tile'=4,'lev'=2,'sub'=2] {'tile','sub'}, dimensions={0}, use_global_device_ids=true | all-gather | bytes 18432 | tf_op jit(solution)/shard_map/all_gather | solution.py:23
  256.2 1.4 multiply_reduce_fusion
  257.6 30.5 %all-reduce = (f32[]{:T(128)}, f32[]{:T(128)}, f32[]{:T(128)}, f32[]{:T(128)}) all-reduce(f32[]{:T(128)} %get-tuple-element.11, f32[]{:T(128)} %get-tuple-element.12, f32[]{:T(128)} %get-tuple-element.10, f32[]{:T(128)} %get-tuple-element.9), channel_id=1, replica_groups=mesh['member'=2,'tile'=4,'lev'=2,'sub'=2] {'tile','lev','sub'}, use_global_device_ids=true, to_apply=%region_1.2 | all-reduce | flops 4 | bytes 32 | tf_op jit(solution)/shard_map/psum | solution.py:159
  (183 shorter events, 27.4 us)
Async XLA Ops:
  7.2 16.6 %copy-start = (s32[8,4]{0,1:T(4,128)S(1)}, s32[8,4]{0,1:T(4,128)}, u32[]{:S(2)}) copy-start(s32[8,4]{0,1:T(4,128)} %param.23) | copy-start | bytes 388
  7.2 41.3 %collective-permute-start.1 = (f32[1,128,128]{2,1,0:T(8,128)}, f32[1,128,128]{2,1,0:T(8,128)S(1)}, u32[]{:S(2)}, u32[]{:S(2)}) collective-permute-start(f32[1,128,128]{2,1,0:T(8,128)} %param.17), channel_id=1, source_target_pairs={{2,0},{3,1},{6,4},{7,5},{10,8},{11,9},{14,12},{15,13},{18,16},{19,... | collective-permute-start | bytes 196616 | tf_op jit(solution)/shard_map/ppermute | solution.py:17
  8.5 40.0 %collective-permute-start = (f32[1,128,128]{2,1,0:T(8,128)}, f32[1,128,128]{2,1,0:T(8,128)S(1)}, u32[]{:S(2)}, u32[]{:S(2)}) collective-permute-start(f32[1,128,128]{2,1,0:T(8,128)} %param.17), channel_id=1, source_target_pairs={{0,2},{1,3},{4,6},{5,7},{8,10},{9,11},{12,14},{13,15},{16,18},{17,... | collective-permute-start | bytes 196616 | tf_op jit(solution)/shard_map/ppermute | solution.py:14
  14.0 0.7 copy-start.9
  14.8 7.8 %copy-start.1 = (f32[1,128,128]{2,1,0:T(8,128)S(1)}, f32[1,128,128]{2,1,0:T(8,128)}, u32[]{:S(2)}) copy-start(f32[1,128,128]{2,1,0:T(8,128)} %param.17) | copy-start | bytes 196612
  16.5 23.1 %all-to-all-start.1 = ((s32[8,1,16]{2,1,0:T(1,128)}), s32[8,1,16]{2,1,0:T(1,128)S(1)}, u32[]{:S(2)}, u32[]{:S(2)}) async-start(s32[8,1,16]{2,1,0:T(1,128)} %bitcast.6), calls=%async_computation.1 | async-start | bytes 8192 | tf_op jit(solution)/shard_map/all_to_all | solution.py:128
  22.9 0.7 copy-start.8
  39.6 8.8 %all-to-all-start = ((s32[8,1,16]{2,1,0:T(1,128)}), s32[8,1,16]{2,1,0:T(1,128)S(1)}, u32[]{:S(2)}, u32[]{:S(2)}) async-start(s32[8,1,16]{2,1,0:T(1,128)} %bitcast.3), calls=%async_computation | async-start | bytes 8192 | tf_op jit(solution)/shard_map/all_to_all | solution.py:129
  42.9 0.7 copy-start.10
  43.6 0.7 copy-start.11
  45.0 3.5 %copy-start.3 = (bf16[1,128,128]{2,1,0:T(8,128)(2,1)S(1)}, bf16[1,128,128]{2,1,0:T(8,128)(2,1)}, u32[]{:S(2)}) copy-start(bf16[1,128,128]{2,1,0:T(8,128)(2,1)} %param.19) | copy-start | bytes 98308
  45.1 3.4 %copy-start.2 = (bf16[1,128,128]{2,1,0:T(8,128)(2,1)S(1)}, bf16[1,128,128]{2,1,0:T(8,128)(2,1)}, u32[]{:S(2)}) copy-start(bf16[1,128,128]{2,1,0:T(8,128)(2,1)} %param.18) | copy-start | bytes 98308
  50.1 19.7 %collective-permute-start.3 = (f32[1,128,128]{2,1,0:T(8,128)S(1)}, f32[1,128,128]{2,1,0:T(8,128)S(1)}, u32[]{:S(2)}, u32[]{:S(2)}) collective-permute-start(f32[1,128,128]{2,1,0:T(8,128)S(1)} %fusion.5), channel_id=1, source_target_pairs={{2,0},{3,1},{6,4},{7,5},{10,8},{11,9},{14,12},{15,13},{18,16},{19,... | collective-permute-start | bytes 196616 | tf_op jit(solution)/shard_map/ppermute | solution.py:17
  51.4 18.4 %collective-permute-start.2 = (f32[1,128,128]{2,1,0:T(8,128)S(1)}, f32[1,128,128]{2,1,0:T(8,128)S(1)}, u32[]{:S(2)}, u32[]{:S(2)}) collective-permute-start(f32[1,128,128]{2,1,0:T(8,128)S(1)} %fusion.5), channel_id=1, source_target_pairs={{0,2},{1,3},{4,6},{5,7},{8,10},{9,11},{12,14},{13,15},{16,18},{17,... | collective-permute-start | bytes 196616 | tf_op jit(solution)/shard_map/ppermute | solution.py:14
  71.4 19.7 %collective-permute-start.5 = (f32[1,128,128]{2,1,0:T(8,128)S(1)}, f32[1,128,128]{2,1,0:T(8,128)S(1)}, u32[]{:S(2)}, u32[]{:S(2)}) collective-permute-start(f32[1,128,128]{2,1,0:T(8,128)S(1)} %fusion.10), channel_id=1, source_target_pairs={{2,0},{3,1},{6,4},{7,5},{10,8},{11,9},{14,12},{15,13},{18,16},{19,... | collective-permute-start | bytes 196616 | tf_op jit(solution)/shard_map/ppermute | solution.py:17
  72.7 18.4 %collective-permute-start.4 = (f32[1,128,128]{2,1,0:T(8,128)S(1)}, f32[1,128,128]{2,1,0:T(8,128)S(1)}, u32[]{:S(2)}, u32[]{:S(2)}) collective-permute-start(f32[1,128,128]{2,1,0:T(8,128)S(1)} %fusion.10), channel_id=1, source_target_pairs={{0,2},{1,3},{4,6},{5,7},{8,10},{9,11},{12,14},{13,15},{16,18},{17,... | collective-permute-start | bytes 196616 | tf_op jit(solution)/shard_map/ppermute | solution.py:14
  92.7 19.7 %collective-permute-start.7 = (f32[1,128,128]{2,1,0:T(8,128)S(1)}, f32[1,128,128]{2,1,0:T(8,128)S(1)}, u32[]{:S(2)}, u32[]{:S(2)}) collective-permute-start(f32[1,128,128]{2,1,0:T(8,128)S(1)} %fusion.15), channel_id=1, source_target_pairs={{2,0},{3,1},{6,4},{7,5},{10,8},{11,9},{14,12},{15,13},{18,16},{19,... | collective-permute-start | bytes 196616 | tf_op jit(solution)/shard_map/ppermute | solution.py:17
  94.0 18.4 %collective-permute-start.6 = (f32[1,128,128]{2,1,0:T(8,128)S(1)}, f32[1,128,128]{2,1,0:T(8,128)S(1)}, u32[]{:S(2)}, u32[]{:S(2)}) collective-permute-start(f32[1,128,128]{2,1,0:T(8,128)S(1)} %fusion.15), channel_id=1, source_target_pairs={{0,2},{1,3},{4,6},{5,7},{8,10},{9,11},{12,14},{13,15},{16,18},{17,... | collective-permute-start | bytes 196616 | tf_op jit(solution)/shard_map/ppermute | solution.py:14
  116.3 8.8 %all-to-all-start.2 = ((f32[8,16,1]{1,2,0:T(1,128)}), f32[8,16,1]{1,2,0:T(1,128)S(1)}, u32[]{:S(2)}, u32[]{:S(2)}) async-start(f32[8,16,1]{1,2,0:T(1,128)} %bitcast.47), calls=%async_computation.2 | async-start | bytes 8192 | tf_op jit(solution)/shard_map/all_to_all | solution.py:131
  119.6 28.0 %all-reduce.3.cloned.1.call-start = ((), (), s32[]{:S(2)}) async-start(), calls=%async_computation.4 | async-start | bytes 327680 | tf_op jit(solution)/shard_map/psum | solution.py:135
  119.7 0.7 copy-start.12
  126.3 0.9 copy-start.4
  128.1 19.6 %copy-start.7 = (f32[616]{0:T(1024)S(1)}, f32[616]{0:T(1024)}, u32[]{:S(2)}) copy-start(f32[616]{0:T(1024)} %param.29) | copy-start | bytes 7396
  150.1 10.1 %all-to-all-start.3 = ((f32[8,16,1]{1,2,0:T(1,128)}), f32[8,16,1]{1,2,0:T(1,128)S(1)}, u32[]{:S(2)}, u32[]{:S(2)}) async-start(f32[8,16,1]{1,2,0:T(1,128)} %bitcast.49), calls=%async_computation.3 | async-start | bytes 8192 | tf_op jit(solution)/shard_map/all_to_all | solution.py:145
  169.4 19.9 %collective-permute-start.9 = (f32[1,128,128]{2,1,0:T(8,128)S(1)}, f32[1,128,128]{2,1,0:T(8,128)S(1)}, u32[]{:S(2)}, u32[]{:S(2)}) collective-permute-start(f32[1,128,128]{2,1,0:T(8,128)S(1)} %get-tuple-element.57), channel_id=1, source_target_pairs={{2,0},{3,1},{6,4},{7,5},{10,8},{11,9},{14,12},{15,13},{18,16},{19,... | collective-permute-start | bytes 196616 | tf_op jit(solution)/shard_map/ppermute | solution.py:17
  170.7 18.6 %collective-permute-start.8 = (f32[1,128,128]{2,1,0:T(8,128)S(1)}, f32[1,128,128]{2,1,0:T(8,128)S(1)}, u32[]{:S(2)}, u32[]{:S(2)}) collective-permute-start(f32[1,128,128]{2,1,0:T(8,128)S(1)} %get-tuple-element.57), channel_id=1, source_target_pairs={{0,2},{1,3},{4,6},{5,7},{8,10},{9,11},{12,14},{13,15},{16,18},{17,... | collective-permute-start | bytes 196616 | tf_op jit(solution)/shard_map/ppermute | solution.py:14
  191.3 20.0 %collective-permute-start.11 = (f32[1,128,128]{2,1,0:T(8,128)S(1)}, f32[1,128,128]{2,1,0:T(8,128)S(1)}, u32[]{:S(2)}, u32[]{:S(2)}) collective-permute-start(f32[1,128,128]{2,1,0:T(8,128)S(1)} %get-tuple-element.56), channel_id=1, source_target_pairs={{2,0},{3,1},{6,4},{7,5},{10,8},{11,9},{14,12},{15,13},{18,16},{19,... | collective-permute-start | bytes 196616 | tf_op jit(solution)/shard_map/ppermute | solution.py:17
  192.6 18.7 %collective-permute-start.10 = (f32[1,128,128]{2,1,0:T(8,128)S(1)}, f32[1,128,128]{2,1,0:T(8,128)S(1)}, u32[]{:S(2)}, u32[]{:S(2)}) collective-permute-start(f32[1,128,128]{2,1,0:T(8,128)S(1)} %get-tuple-element.56), channel_id=1, source_target_pairs={{0,2},{1,3},{4,6},{5,7},{8,10},{9,11},{12,14},{13,15},{16,18},{17,... | collective-permute-start | bytes 196616 | tf_op jit(solution)/shard_map/ppermute | solution.py:14
  213.5 20.0 %collective-permute-start.13 = (f32[1,128,128]{2,1,0:T(8,128)S(1)}, f32[1,128,128]{2,1,0:T(8,128)S(1)}, u32[]{:S(2)}, u32[]{:S(2)}) collective-permute-start(f32[1,128,128]{2,1,0:T(8,128)S(1)} %get-tuple-element.54), channel_id=1, source_target_pairs={{2,0},{3,1},{6,4},{7,5},{10,8},{11,9},{14,12},{15,13},{18,16},{19,... | collective-permute-start | bytes 196616 | tf_op jit(solution)/shard_map/ppermute | solution.py:17
  214.8 18.7 %collective-permute-start.12 = (f32[1,128,128]{2,1,0:T(8,128)S(1)}, f32[1,128,128]{2,1,0:T(8,128)S(1)}, u32[]{:S(2)}, u32[]{:S(2)}) collective-permute-start(f32[1,128,128]{2,1,0:T(8,128)S(1)} %get-tuple-element.54), channel_id=1, source_target_pairs={{0,2},{1,3},{4,6},{5,7},{8,10},{9,11},{12,14},{13,15},{16,18},{17,... | collective-permute-start | bytes 196616 | tf_op jit(solution)/shard_map/ppermute | solution.py:14
  235.6 20.0 %collective-permute-start.15 = (f32[1,128,128]{2,1,0:T(8,128)S(1)}, f32[1,128,128]{2,1,0:T(8,128)S(1)}, u32[]{:S(2)}, u32[]{:S(2)}) collective-permute-start(f32[1,128,128]{2,1,0:T(8,128)S(1)} %get-tuple-element.52), channel_id=1, source_target_pairs={{2,0},{3,1},{6,4},{7,5},{10,8},{11,9},{14,12},{15,13},{18,16},{19,... | collective-permute-start | bytes 196616 | tf_op jit(solution)/shard_map/ppermute | solution.py:17
  236.9 18.7 %collective-permute-start.14 = (f32[1,128,128]{2,1,0:T(8,128)S(1)}, f32[1,128,128]{2,1,0:T(8,128)S(1)}, u32[]{:S(2)}, u32[]{:S(2)}) collective-permute-start(f32[1,128,128]{2,1,0:T(8,128)S(1)} %get-tuple-element.52), channel_id=1, source_target_pairs={{0,2},{1,3},{4,6},{5,7},{8,10},{9,11},{12,14},{13,15},{16,18},{17,... | collective-permute-start | bytes 196616 | tf_op jit(solution)/shard_map/ppermute | solution.py:14
  255.4 0.8 copy-start.5
  256.2 35.7 %copy-start.6 = (f32[1,128,128]{2,1,0:T(8,128)S(1)}, f32[1,128,128]{2,1,0:T(8,128)}, u32[]{:S(2)}) copy-start(f32[1,128,128]{2,1,0:T(8,128)} %param.15) | copy-start | bytes 196612
Sparse Core Ops, SparseCore 0:
  128.1 19.4 all-reduce.2
where the time goes:
time: 301 us; the launch traced here: 299 us
  blocking collectives  133 us (44%)
  starting transfers between devices  64.3 us (21%)
  waiting for transfers between devices  30 us (10%)
  other arithmetic  27.2 us (9%)
  local copies, waits for them, and re-layouts  24.1 us (8%)
  between operations  20.7 us (7%)
    all_gather x8, blocking collectives, neighbours(): everyone = lax.all_gather(strips, ('tile', 'sub'), axis=0, tiled=True)  103 us
    ppermute x8, starting transfers between devices, with_halo(): lax.ppermute(lax.slice_in_dim(block, block.shape[dim] - width, None, axis...  36.7 us
    psum x1, blocking collectives, body(): lax.psum((jnp.sum(residual * residual), jnp.sum(direction * image), jnp.s...  30.5 us
    psum x1, waiting for transfers between devices, body(): departure = lax.psum(partial_value, 'lev')  19.5 us
    ppermute x8, starting transfers between devices, with_halo(): lax.ppermute(lax.slice_in_dim(block, 0, width, axis=dim), axis, backward)  10.3 us
    mul x7, other arithmetic, adjoint(): prods = [c * field for c in coefs]  7.49 us
    scatter-add x1, other arithmetic, body(): forcing = jnp.zeros((STEPS, depth, area), jnp.float32).at[flat_time, :, f...  6.81 us
    all_to_all x1, starting transfers between devices, body(): lax.all_to_all(want_cell, ('tile', 'sub'), split_axis=0, concat_axis=0, t...  6.03 us
  transfers between devices with their start and end apart: 21, of which 4 were waited for; matrix products, arithmetic and copies ran while one was open for 5% of the time, Pallas kernels for 0%

commit v1 on v0

v1 whole, which is shorter than its diff:
```python
import jax
import jax.numpy as jnp
from jax import lax
from jax.experimental import pallas as pl
from jax.experimental.pallas import tpu as pltpu
from jax.sharding import PartitionSpec as P

STEPS = 4
DEEP = 2 * STEPS
SIDES = 4
FIELDS = 3
BAND = SIDES * FIELDS * DEEP
LANES = 128
SHEETS = LANES // DEEP
CHUNK = 512
F32 = jnp.float32
BF16 = jnp.bfloat16
NT = (((1,), (1,)), ((), ()))
WHOLE = pl.BlockSpec(memory_space=pltpu.VMEM)
SCALAR = pl.BlockSpec(memory_space=pltpu.SMEM)
CORNERS = ((0, 2), (0, 3), (1, 2), (1, 3))
NW, NE, SW, SE = range(4)


def iota(shape, axis):
    return lax.broadcasted_iota(jnp.int32, shape, axis)


def level_pairs(levels):
    return [(low, high) for low in range(levels) for high in range(low, levels)]


def record_rows(levels):
    return -(-(4 + len(level_pairs(levels))) // 8) * 8


def rotated(levels, k):
    return lax.rem(lax.axis_index("lev") + (levels - k), levels)


def prepare(direction, wind_u, wind_v, jacobian, bands, winds, wide):
    x = direction[...]
    u = 0.5 * wind_u[...].astype(F32)
    v = 0.5 * wind_v[...].astype(F32)
    width = x.shape[0]
    winds[0] = u
    winds[1] = v
    wide[...] = jacobian[...].astype(F32)
    first = lambda a: a[:DEEP]
    last = lambda a: jnp.concatenate([a[width - 1 - d : width - d] for d in range(DEEP)], axis=0)
    xt, ut, vt = x.T, u.T, v.T
    parts = [
        (first(x), first(u), first(v)),
        (last(x), -last(u), last(v)),
        (first(xt), first(vt), first(ut)),
        (last(xt), -last(vt), last(ut)),
    ]
    for side in range(SIDES):
        for field in range(FIELDS):
            row = (side * FIELDS + field) * DEEP
            bands[row : row + DEEP, :] = parts[side][field]


def compose(levels, *refs):
    bands = refs[:levels]
    jacobians = refs[levels : 2 * levels]
    error_inv, places, message, ordered = refs[2 * levels :]
    for k in range(levels):
        level = rotated(levels, k)
        message[pl.ds(pl.multiple_of(level * BAND, 8), BAND), :] = bands[k][...]
        ordered[level] = jacobians[k][...].astype(F32)
    slots = ordered.shape[1]
    base = levels * BAND
    place = places[...]
    ones = jnp.ones((8, ordered.shape[2]), F32)
    weights = error_inv[...]
    pairs = level_pairs(levels)
    rows = [place[:4, :]]
    for low, high in pairs:
        product = ordered[low] * weights * ordered[high]
        total = lax.dot_general(ones, product, NT, precision=lax.Precision.HIGHEST, preferred_element_type=F32)
        row = total[:1]
        if slots < LANES:
            row = jnp.concatenate([row, jnp.zeros((1, LANES - slots), F32)], axis=1)
        rows.append(row)
    spare = record_rows(levels) - 4 - len(pairs)
    if spare:
        rows.append(jnp.zeros((spare, LANES), F32))
    message[base : base + record_rows(levels), :] = jnp.concatenate(rows, axis=0)


def roll(a, shift, axis):
    return pltpu.roll(a, shift % a.shape[axis], axis)


class Geometry:
    def __init__(self, width):
        last = width - 1
        self.last = last
        row, lane = iota((width, LANES), 0), iota((width, LANES), 1)
        self.top, self.bottom = row == 0, row == last
        self.left, self.right = lane == 0, lane == last
        self.half = lane == LANES // 2
        brow, blane = iota((DEEP, LANES), 0), iota((DEEP, LANES), 1)
        self.band_first = brow == 0
        self.band_left, self.band_right = blane == 0, blane == last
        crow, clane = iota((SIDES * DEEP, LANES), 0), iota((SIDES * DEEP, LANES), 1)
        self.chain_top = crow % DEEP == 0
        self.chain_left = clane % DEEP == 0
        self.even = (clane // DEEP) % 2 == 0
        self.seventh = clane // DEEP == DEEP - 1
        self.near = iota((1, LANES), 1) < LANES // 2

    def chain(self, a, corner):
        return a[corner * DEEP : (corner + 1) * DEEP]

    def main_up(self, a, north):
        return jnp.where(self.top, north[:1], roll(a, 1, 0))

    def main_down(self, a, south):
        return jnp.where(self.bottom, south[:1], roll(a, -1, 0))

    def main_west(self, a, ew):
        return jnp.where(self.left, roll(ew, LANES // 2, 1), roll(a, 1, 1))

    def main_east(self, a, ew):
        return jnp.where(self.right, roll(ew, -1, 1), roll(a, -1, 1))

    def band_toward(self, a, main_row):
        return jnp.where(self.band_first, main_row, roll(a, 1, 0))

    def band_west(self, a, chain_block):
        return jnp.where(self.band_left, roll(chain_block, -2 * DEEP, 1), roll(a, 1, 1))

    def band_east(self, a, chain_block):
        return jnp.where(self.band_right, roll(chain_block, self.last - 2 * DEEP, 1), roll(a, -1, 1))

    def ew_toward(self, a, main_east, main_west):
        inner = jnp.where(self.half, roll(main_west, LANES // 2, 1), roll(a, 1, 1))
        return jnp.where(self.left, roll(main_east, 1, 1), inner)

    def ew_fill(self, east, west):
        return jnp.where(self.near, roll(east, 2 * DEEP, 1)[:1], roll(west, 2 * DEEP + LANES // 2, 1)[:1])

    def ew_up(self, a, chain):
        fill = self.ew_fill(self.chain(chain, NE), self.chain(chain, NW))
        return jnp.where(self.top, fill, roll(a, 1, 0))

    def ew_down(self, a, chain):
        fill = self.ew_fill(self.chain(chain, SE), self.chain(chain, SW))
        return jnp.where(self.bottom, fill, roll(a, -1, 0))

    def chain_up(self, a, fill):
        swapped = jnp.where(self.even, roll(fill, -DEEP, 1), roll(fill, DEEP, 1))
        return jnp.where(self.chain_top, swapped, roll(a, 1, 0))

    def chain_west(self, a, fill, beyond=None):
        swapped = jnp.where(self.even, roll(fill, DEEP, 1), roll(fill, -DEEP, 1))
        if beyond is not None:
            swapped = jnp.where(self.seventh, beyond, swapped)
        return jnp.where(self.chain_left, swapped, roll(a, 1, 1))

    def neighbours(self, minus0, plus0, minus1, plus1, beyond=None, main_only=False):
        n, s, ew, m, c = "n", "s", "ew", "m", "c"
        out = {
            m: (
                self.main_up(plus0[m], minus0[n]),
                self.main_down(minus0[m], minus0[s]),
                self.main_west(plus1[m], minus1[ew]),
                self.main_east(minus1[m], minus1[ew]),
            )
        }
        if main_only:
            return out
        top, bottom = minus0[m][:1], plus0[m][self.last :]
        for part, row, west, east in ((n, top, NW, NE), (s, bottom, SW, SE)):
            out[part] = (
                self.band_toward(plus0[part], row),
                roll(minus0[part], -1, 0),
                self.band_west(plus1[part], self.chain(minus1[c], west)),
                self.band_east(minus1[part], self.chain(minus1[c], east)),
            )
        out[ew] = (
            self.ew_up(plus0[ew], minus0[c]),
            self.ew_down(minus0[ew], minus0[c]),
            self.ew_toward(plus1[ew], plus1[m], minus1[m]),
            roll(minus1[ew], -1, 1),
        )
        out[c] = (
            self.chain_up(plus0[c], minus0[c]),
            roll(minus0[c], -1, 0),
            self.chain_west(plus1[c], minus1[c], beyond),
            roll(minus1[c], -1, 1),
        )
        return out


PARTS = ("m", "n", "s", "ew", "c")


def evolve(levels, gathered_count, panels, slots, *refs):
    pair, flip, diffusion, vertical, prior = refs[:5]
    refs = refs[5:]
    messages, refs = refs[:gathered_count], refs[gathered_count:]
    directions, refs = refs[:levels], refs[levels:]
    winds, refs = refs[:levels], refs[levels:]
    residuals, refs = refs[:levels], refs[levels:]
    image_out, sums_out = refs[:2]
    (
        table,
        x_main,
        w_main,
        images,
        x_band,
        w_band,
        x_ew,
        w_ew,
        x_chain,
        w_chain,
        x_far,
        g_main,
        g_band,
        g_ew,
        g_chain,
        obs,
        square,
    ) = refs[2:]
    width = directions[0].shape[0]
    last = width - 1
    tiles, subs = lax.axis_size("tile"), lax.axis_size("sub")
    tile, sub = lax.axis_index("tile"), lax.axis_index("sub")
    me = tile * subs + sub
    rows = table.shape[1]
    if gathered_count == 1:
        table[...] = messages[0][...]
    else:
        for index in range(gathered_count):
            xt, xs = index // subs, index % subs
            table[(tile ^ xt) * subs + (sub ^ xs)] = messages[index][...]
    for k in range(levels):
        level = rotated(levels, k)
        x_main[level] = directions[k][...]
        w_main[level] = winds[k][...]

    lane8 = iota((DEEP, LANES), 1)
    straight, reverse = lane8 % DEEP, last - lane8 % DEEP
    slot_of = lane8 // DEEP

    def band(panel, side, level, field):
        start = pl.multiple_of(level * BAND + (side * FIELDS + field) * DEEP, 8)
        return table[panel, pl.ds(start, DEEP), :]

    def lookup(panel, side):
        at = SIDES * panel + side
        other = pair[at]
        return lax.shift_right_logical(other, 2), other & 3, flip[at]

    def cross_row(sheet):
        panel, row_side, col_side = sheet
        panel, side, flipped = lookup(panel, row_side)
        end = (col_side & 1) ^ flipped
        return panel, side, end + jnp.where(side < 2, 2, 0)

    def cross_col(sheet):
        panel, row_side, col_side = sheet
        panel, side, flipped = lookup(panel, col_side)
        end = (row_side & 1) ^ flipped
        return panel, end + jnp.where(side < 2, 2, 0), side

    partners = [lookup(me, side) for side in range(SIDES)]
    for level in range(levels):
        turned = [[None] * FIELDS for _ in range(SIDES)]
        for side, (panel, other, flipped) in enumerate(partners):
            order = jnp.where(flipped == 1, last - lane8, lane8)
            sign = jnp.where(flipped == 1, -1.0, 1.0).astype(F32)
            for field in range(FIELDS):
                values = jnp.take_along_axis(band(panel, other, level, field), order, axis=1)
                turned[side][field] = values * sign if field == 2 else values
        for index in range(2):
            x_band[level, index] = turned[index][0]
            w_band[level, index, 0] = turned[index][1]
            w_band[level, index, 1] = turned[index][2]
        square[...] = jnp.zeros((width, LANES), F32)
        for field, target in ((0, None), (2, 0), (1, 1)):
            square[:DEEP, :] = turned[3][field]
            square[LANES // 2 : LANES // 2 + DEEP, :] = turned[2][field]
            if target is None:
                x_ew[level] = square[...].T
            else:
                w_ew[level, target] = square[...].T

    keys, kinds = [], []
    for corner, (row_side, col_side) in enumerate(CORNERS):
        start = (me, jnp.int32(row_side), jnp.int32(col_side))
        sheets = {0: start}
        ahead, behind = start, start
        for k in range(DEEP):
            ahead = cross_row(ahead) if k % 2 == 0 else cross_col(ahead)
            behind = cross_col(behind) if k % 2 == 0 else cross_row(behind)
            sheets[k + 1], sheets[-k - 1] = ahead, behind
        filled = [[jnp.zeros((DEEP, LANES), F32)] * FIELDS for _ in range(levels)]
        key = jnp.full((1, LANES), -1, jnp.int32)
        kind = jnp.full((1, LANES), -1, jnp.int32)
        for k, (panel, side, other) in sheets.items():
            end = other & 1
            order = jnp.where(end == 1, reverse, straight)
            sign = jnp.where(end == 1, -1.0, 1.0).astype(F32)
            if k == DEEP:
                for level in range(levels):
                    x_far[level, corner * DEEP : (corner + 1) * DEEP, :] = jnp.take_along_axis(
                        band(panel, side, level, 0), order, axis=1
                    )
                continue
            here = slot_of == k % SHEETS
            for level in range(levels):
                for field in range(FIELDS):
                    values = jnp.take_along_axis(band(panel, side, level, field), order, axis=1)
                    values = values * sign if field == 2 else values
                    filled[level][field] = jnp.where(here, values, filled[level][field])
            if abs(k) <= STEPS:
                key = jnp.where(here[:1], panel * width + order[:1], key)
                kind = jnp.where(here[:1], side, kind)
        keys.append(key)
        kinds.append(kind)
        place = slice(corner * DEEP, (corner + 1) * DEEP)
        for level in range(levels):
            x_chain[level, place, :] = filled[level][0]
            w_chain[level, 0, place, :] = filled[level][1]
            w_chain[level, 1, place, :] = filled[level][2]

    pairs = level_pairs(levels)
    depth_rows = record_rows(levels)
    base = levels * BAND
    fold = LANES // slots
    lane_rec = iota((depth_rows, LANES), 1)
    chunk_tiles = obs.shape[2] // LANES
    for group in range(panels // fold):
        packed = table[group * fold, base : base + depth_rows, :]
        for part in range(1, fold):
            shifted = roll(table[group * fold + part, base : base + depth_rows, :], part * slots, 1)
            packed = jnp.where(lane_rec // slots == part, shifted, packed)
        column = (group % chunk_tiles) * LANES
        obs[group // chunk_tiles, :, column : column + LANES] = packed
    chunks = obs.shape[0]
    span = obs.shape[2]
    key_columns = jnp.concatenate(keys, axis=0)
    kind_columns = jnp.concatenate(kinds, axis=0)
    key_tall = jnp.concatenate(
        [key_columns, kind_columns, jnp.zeros((LANES - 8, LANES), jnp.int32)], axis=0
    ).astype(F32).T
    comps = STEPS * len(pairs)

    def hits(mask):
        return jnp.where(mask, 1.0, 0.0).astype(BF16)

    def accumulate(chunk, _):
        data = obs[chunk]
        panel = data[0:1].astype(jnp.int32)
        oi = data[1:2].astype(jnp.int32)
        oj = data[2:3].astype(jnp.int32)
        when = data[3:4].astype(jnp.int32)
        tall = iota((width, span), 0)
        short = iota((DEEP, span), 0)
        at_row = jnp.where(tall == oi, 1.0, 0.0)
        at_row_here = jnp.where(panel == me, at_row, 0.0)
        at_col = jnp.where(tall == oj, 1.0, 0.0)
        at_row_b, at_col_b = at_row.astype(BF16), at_col.astype(BF16)
        distance = (oi, last - oi, oj, last - oj)
        band_hit, band_place = [], []
        for q, r, f in partners:
            depth = jnp.where(r == 0, distance[0], jnp.where(r == 1, distance[1], jnp.where(r == 2, distance[2], distance[3])))
            along = jnp.where(r < 2, oj, oi)
            along = jnp.where(f == 1, last - along, along)
            band_hit.append(jnp.where(panel == q, jnp.where(short == depth, 1.0, 0.0), 0.0))
            band_place.append(hits(tall == along))
        spot = (panel * width + oj, panel * width + oi)
        chain_hit = [jnp.where(short == distance[side], 1.0, 0.0) for side in range(SIDES)]
        chain_place = []
        for corner in range(4):
            key = key_tall[:, corner : corner + 1].astype(jnp.int32)
            kind = key_tall[:, 4 + corner : 5 + corner].astype(jnp.int32)
            chain_place.append(
                [hits((key == spot[side // 2]) & (kind == side)) for side in range(SIDES)]
            )
        gs = []
        for t in range(STEPS):
            for index in range(len(pairs)):
                g = jnp.where(when == t + 1, data[4 + index : 5 + index], 0.0)
                high = g.astype(BF16).astype(F32)
                gs.append((high, g - high))

        def product(left, right):
            return lax.dot_general(left, right, NT, preferred_element_type=F32)

        def tall_rows(hit):
            return jnp.concatenate([hit * part for g in gs for part in g], axis=0).astype(BF16)

        def put(ref, at, value):
            if chunks == 1:
                ref[at] = value
            else:
                ref[at] = ref[at] + value

        for comp in range(comps):
            high, low = gs[comp]
            value = product((at_row_here * high).astype(BF16), at_col_b)
            value = value + product((at_row_here * low).astype(BF16), at_col_b)
            put(g_main, comp, value)
        for side in range(SIDES):
            value = product(tall_rows(band_hit[side]), band_place[side])
            for comp in range(comps):
                at = 2 * comp * DEEP
                put(g_band, (side, comp), value[at : at + DEEP] + value[at + DEEP : at + 2 * DEEP])
        lefts = [tall_rows(chain_hit[side]) for side in range(SIDES)]
        for corner in range(4):
            value = product(lefts[0], chain_place[corner][0])
            for side in range(1, SIDES):
                value = value + product(lefts[side], chain_place[corner][side])
            for comp in range(comps):
                at = 2 * comp * DEEP
                put(
                    g_chain,
                    (comp, slice(corner * DEEP, (corner + 1) * DEEP)),
                    value[at : at + DEEP] + value[at + DEEP : at + 2 * DEEP],
                )
        return 0

    if chunks == 1:
        accumulate(0, 0)
    else:
        g_main[...] = jnp.zeros(g_main.shape, F32)
        g_band[...] = jnp.zeros(g_band.shape, F32)
        g_chain[...] = jnp.zeros(g_chain.shape, F32)
        lax.fori_loop(0, chunks, accumulate, 0)
    for comp in range(comps):
        square[...] = jnp.zeros((width, LANES), F32)
        square[:DEEP, :] = g_band[3, comp]
        square[LANES // 2 : LANES // 2 + DEEP, :] = g_band[2, comp]
        g_ew[comp] = square[...].T

    geometry = Geometry(width)
    mix = [diffusion[level] for level in range(levels)]
    blend = [vertical[level] for level in range(levels)]
    center = [1.0 - 4.0 * mix[level] - 2.0 * blend[level] for level in range(levels)]

    def wind(level, axis, part):
        if part == "m":
            return w_main[level, axis]
        if part == "n":
            return w_band[level, 0, axis]
        if part == "s":
            return w_band[level, 1, axis]
        return (w_ew if part == "ew" else w_chain)[level, axis]

    def forward(states, beyond):
        out = []
        for level in range(levels):
            x = states[level]
            near = geometry.neighbours(x, x, x, x, None if beyond is None else beyond[level])
            result = {}
            for part in PARTS:
                up, down, west, east = near[part]
                p, q = wind(level, 0, part), wind(level, 1, part)
                value = center[level] * x[part] + mix[level] * ((up + down) + (west + east))
                value = value + p * (up - down) + q * (west - east)
                others = [states[k][part] for k in (level - 1, level + 1) if 0 <= k < levels]
                if others:
                    value = value + blend[level] * sum(others[1:], others[0])
                result[part] = value
            out.append(result)
        return out

    def adjoint(states, main_only):
        out = []
        parts = ("m",) if main_only else PARTS
        for level in range(levels):
            w = states[level]
            minus0, plus0, minus1, plus1 = {}, {}, {}, {}
            for part in PARTS:
                scaled = mix[level] * w[part]
                p, q = wind(level, 0, part) * w[part], wind(level, 1, part) * w[part]
                minus0[part], plus0[part] = scaled + p, scaled - p
                minus1[part], plus1[part] = scaled + q, scaled - q
            near = geometry.neighbours(minus0, plus0, minus1, plus1, None, main_only)
            result = {}
            for part in parts:
                up, down, west, east = near[part]
                value = center[level] * w[part] + ((up + down) + (west + east))
                for k in (level - 1, level + 1):
                    if 0 <= k < levels:
                        value = value + blend[k] * states[k][part]
                result[part] = value
            out.append(result)
        return out

    def gain(t, index, part):
        comp = t * len(pairs) + index
        if part == "m":
            return g_main[comp]
        if part == "n":
            return g_band[0, comp]
        if part == "s":
            return g_band[1, comp]
        return (g_ew if part == "ew" else g_chain)[comp]

    def force(t, states):
        out = []
        for level in range(levels):
            result = {}
            for part in PARTS:
                value = None
                for other in range(levels):
                    index = pairs.index((min(level, other), max(level, other)))
                    term = gain(t, index, part) * states[other][part]
                    value = term if value is None else value + term
                result[part] = value
            out.append(result)
        return out

    states = [
        {"m": x_main[k], "n": x_band[k, 0], "s": x_band[k, 1], "ew": x_ew[k], "c": x_chain[k]} for k in range(levels)
    ]
    forcing = []
    for step in range(STEPS):
        states = forward(states, [x_far[k] for k in range(levels)] if step == 0 else None)
        forcing.append(force(step, states))
    current = forcing[STEPS - 1]
    for step in range(STEPS - 1, 0, -1):
        current = adjoint(current, False)
        current = [{part: current[k][part] + forcing[step - 1][k][part] for part in PARTS} for k in range(levels)]
    current = adjoint(current, True)

    zero = jnp.zeros((1, LANES), F32)
    totals = [zero] * 4
    for k in range(levels):
        images[k] = prior[k] * x_main[k] + current[k]["m"]
    for k in range(levels):
        level = rotated(levels, k)
        image = images[level]
        residual, direction = residuals[k][...], directions[k][...]
        if k == 0:
            image_out[...] = image
        for index, term in enumerate((residual * residual, direction * image, residual * image, image * image)):
            totals[index] = totals[index] + jnp.sum(term, axis=0, keepdims=True)
    sums_out[...] = jnp.concatenate(totals + [zero] * 4, axis=0)


def update(*refs):
    parts = refs[:-7]
    increment, residual, direction, image, increment_new, residual_new, direction_new = refs[-7:]
    total = parts[0][...]
    for part in parts[1:]:
        total = total + part[...]
    total = jnp.sum(total, axis=1, keepdims=True)
    norm_old, curvature, cross, square = (total[index : index + 1] for index in range(4))
    alpha = norm_old / curvature
    norm_new = norm_old - 2.0 * alpha * cross + alpha * alpha * square
    ratio = norm_new / norm_old
    d = direction[...]
    increment_new[...] = increment[...] + alpha * d
    r = residual[...] - alpha * image[...]
    residual_new[...] = r
    direction_new[...] = r + ratio * d


def exchanged(value, axis, mask):
    count = lax.axis_size(axis)
    return lax.ppermute(value, axis, [(i, i ^ mask) for i in range(count)])


def level_parts(value):
    count = lax.axis_size("lev")
    return [value] + [
        lax.ppermute(value, "lev", [(i, (i + k) % count) for i in range(count)]) for k in range(1, count)
    ]


def body(
    increment,
    residual,
    direction,
    wind_u,
    wind_v,
    diffusion,
    vertical,
    background_inv,
    side_pair,
    side_flip,
    obs_column,
    obs_time,
    obs_count,
    jacobian,
    error_inv,
):
    width = increment.shape[2]
    slots, _, channels = jacobian.shape
    tiles, subs, levels = lax.axis_size("tile"), lax.axis_size("sub"), lax.axis_size("lev")
    panels = tiles * subs
    shape = (width, width)
    flat = lambda a: a.reshape(shape)
    own = jacobian.reshape(slots, channels)
    bands, winds, wide = pl.pallas_call(
        prepare,
        out_shape=(
            jax.ShapeDtypeStruct((BAND, LANES), F32),
            jax.ShapeDtypeStruct((2,) + shape, F32),
            jax.ShapeDtypeStruct((slots, channels), F32),
        ),
        in_specs=[WHOLE] * 4,
        out_specs=(WHOLE,) * 3,
        name="prepare",
    )(flat(direction), flat(wind_u), flat(wind_v), own)
    all_bands = level_parts(bands)
    all_wide = level_parts(wide)
    all_winds = level_parts(winds)
    all_directions = level_parts(flat(direction))
    all_residuals = level_parts(flat(residual))

    area = width * width
    alive = jnp.arange(slots, dtype=jnp.int32) < obs_count[0]
    places = [jnp.where(alive, obs_column // area, -1), (obs_column % area) // width, obs_column % width, obs_time]
    place_rows = jnp.full((8, LANES), -1.0, F32)
    row_at = iota((8, LANES), 0)
    for index, values in enumerate(places):
        padded = jnp.pad(values, (0, LANES - slots), constant_values=-1).astype(F32)
        place_rows = jnp.where(row_at == index, padded[None, :], place_rows)

    rows = levels * BAND + record_rows(levels)
    message = pl.pallas_call(
        lambda *refs: compose(levels, *refs),
        out_shape=jax.ShapeDtypeStruct((rows, LANES), F32),
        in_specs=[WHOLE] * (2 * levels + 2),
        out_specs=WHOLE,
        scratch_shapes=[pltpu.VMEM((levels, slots, channels), F32)],
        name="compose",
    )(*all_bands, *all_wide, error_inv.reshape(1, channels), place_rows)

    if tiles <= 4:
        mine = [message] + [exchanged(message, "tile", mask) for mask in range(1, tiles)]
        messages = []
        for value in mine:
            messages += [value] + [exchanged(value, "sub", mask) for mask in range(1, subs)]
    else:
        messages = [lax.all_gather(message, ("tile", "sub"), axis=0)]

    span = min(CHUNK, panels * slots)
    pairs = len(level_pairs(levels))
    comps = STEPS * pairs
    chain = (SIDES * DEEP, LANES)
    vmem = lambda *dims: pltpu.VMEM(dims, F32)
    image, sums = pl.pallas_call(
        lambda *refs: evolve(levels, len(messages), panels, slots, *refs),
        out_shape=(jax.ShapeDtypeStruct(shape, F32), jax.ShapeDtypeStruct((8, LANES), F32)),
        in_specs=[SCALAR] * 5 + [WHOLE] * (len(messages) + 3 * levels),
        out_specs=(WHOLE, WHOLE),
        scratch_shapes=[
            vmem(panels, rows, LANES),
            vmem(levels, *shape),
            vmem(levels, 2, *shape),
            vmem(levels, *shape),
            vmem(levels, 2, DEEP, LANES),
            vmem(levels, 2, 2, DEEP, LANES),
            vmem(levels, width, LANES),
            vmem(levels, 2, width, LANES),
            vmem(levels, *chain),
            vmem(levels, 2, *chain),
            vmem(levels, *chain),
            vmem(comps, *shape),
            vmem(SIDES, comps, DEEP, LANES),
            vmem(comps, width, LANES),
            vmem(comps, *chain),
            vmem(panels * slots // span, record_rows(levels), span),
            vmem(width, LANES),
        ],
        name="evolve",
    )(
        side_pair.reshape(-1),
        side_flip.reshape(-1),
        diffusion,
        vertical,
        background_inv,
        *messages,
        *all_directions,
        *all_winds,
        *all_residuals,
    )

    for mask in range(1, subs):
        sums = sums + exchanged(sums, "sub", mask)
    if tiles <= 4:
        parts = [sums] + [exchanged(sums, "tile", mask) for mask in range(1, tiles)]
    else:
        mask = 1
        while mask < tiles:
            sums = sums + exchanged(sums, "tile", mask)
            mask *= 2
        parts = [sums]
    outputs = pl.pallas_call(
        update,
        out_shape=(jax.ShapeDtypeStruct(shape, F32),) * 3,
        in_specs=[WHOLE] * (len(parts) + 4),
        out_specs=(WHOLE,) * 3,
        name="update",
    )(*parts, flat(increment), flat(residual), flat(direction), image)
    return tuple(out.reshape(increment.shape) for out in outputs)


def solution(mesh):
    field = P(("member", "lev"), ("tile", "sub"), None)
    placed = (
        (field,) * 5
        + (P(),) * 5
        + (P(("tile", "sub")),) * 3
        + (P(("tile", "sub"), "lev", None), P())
    )
    return jax.shard_map(body, mesh=mesh, in_specs=placed, out_specs=(field,) * 3, check_vma=False)
```

time: 301 us -> 49.7 us (0.17)
  blocking collectives: 133 us -> 0 us
  starting transfers between devices: 64.3 us -> 16.3 us
  other arithmetic: 27.2 us -> 1.4 us
  between operations: 20.7 us -> 1.48 us
  waiting for transfers between devices: 30 us -> 11.4 us
  local copies, waits for them, and re-layouts: 24.1 us -> 5.9 us
  Pallas kernels: 0 us -> 13 us
    all_gather x8 -> x0, blocking collectives: 103 us -> none  [neighbours(): everyone = lax.all_gather(strips, ('tile', 'sub'), axis=0, tiled=True)]
    ppermute x16, starting transfers between devices: 47.1 us -> 16.3 us  [the longest x11 10.1 us: exchanged(): return lax.ppermute(value, axis, [(i, i ^ mask) for i in range(count)])]
    psum x1 -> x0, blocking collectives: 30.5 us -> none  [body(): lax.psum((jnp.sum(residual * residual), jnp.sum(direction * image), jnp.s...]
    psum x1 -> x0, waiting for transfers between devices: 19.5 us -> none  [body(): departure = lax.psum(partial_value, 'lev')]
    all_to_all x4 -> x0, starting transfers between devices: 17.3 us -> none  [the longest x1 6.03 us: body(): lax.all_to_all(want_cell, ('tile', 'sub'), split_axis=0, concat_axis=0, t...]
    pallas_call x0 -> x4, Pallas kernels: none -> 13 us  [the longest x1 7.17 us: body(): pl.pallas_call(lambda *refs: evolve(levels, len(messages), panels, slots,...]
    ppermute x16, waiting for transfers between devices: 0.04 us -> 11.4 us  [the longest x11 5.97 us: exchanged(): return lax.ppermute(value, axis, [(i, i ^ mask) for i in range(count)])]
    all_to_all x4 -> x0, waiting for transfers between devices: 10.4 us -> none  [the longest x1 5.5 us: body(): lax.all_to_all(outgoing, ('tile', 'sub'), split_axis=0, concat_axis=0, ti...]
  transfers between devices with their start and end apart: 21 -> 16, of which waited for: 4 -> 7; matrix products, arithmetic and copies ran while one was open for 5% -> 5% of each run, Pallas kernels for 0% -> 0%
where the time goes in v1:
time: 49.7 us; the launch traced here: 49.4 us
  starting transfers between devices  16.3 us (33%)
  Pallas kernels  13 us (26%)
  waiting for transfers between devices  11.4 us (23%)
  local copies, waits for them, and re-layouts  5.9 us (12%)
  between operations  1.48 us (3%)
  other arithmetic  1.4 us (3%)
    ppermute x11, starting transfers between devices, exchanged(): return lax.ppermute(value, axis, [(i, i ^ mask) for i in range(count)])  10.1 us
    pallas_call x1, Pallas kernels, body(): pl.pallas_call(lambda *refs: evolve(levels, len(messages), panels, slots,...  7.17 us
    ppermute x5, starting transfers between devices, level_parts(): lax.ppermute(value, 'lev', [(i, (i + k) % count) for i in range(count)])  6.17 us
    ppermute x11, waiting for transfers between devices, exchanged(): return lax.ppermute(value, axis, [(i, i ^ mask) for i in range(count)])  5.97 us
    ppermute x5, waiting for transfers between devices, level_parts(): lax.ppermute(value, 'lev', [(i, (i + k) % count) for i in range(count)])  5.41 us
    unnamed x50, local copies, waits for them, and re-layouts  4.08 us
    pallas_call x1, Pallas kernels, body(): pl.pallas_call(lambda *refs: compose(levels, *refs), out_shape=jax.ShapeD...  2.3 us
    pallas_call x1, Pallas kernels, body(): pl.pallas_call(update, out_shape=(jax.ShapeDtypeStruct(shape, F32),) * 3,...  1.75 us
  transfers between devices with their start and end apart: 16, of which 7 were waited for; matrix products, arithmetic and copies ran while one was open for 5% of the time, Pallas kernels for 0%

profile of v1, /device:TPU:0, one launch (start us, length us, event | category | flops | bytes accessed | tf_op | source)
XLA Modules:
  0.0 49.4 jit_solution(8869658814952247749)
XLA Ops:
  0.6 1.7 %prepare.1 = (f32[96,128]{1,0:T(8,128)}, f32[2,128,128]{2,1,0:T(8,128)}, f32[64,616]{1,0:T(8,128)}) custom-call(f32[128,128]{1,0:T(8,128)} %bitcast.11, bf16[128,128]{1,0:T(8,128)(2,1)} %bitcast.20, bf16[128,128]{1,0:T(8,128)(2,1)} %bitcast.21, bf16[64,616]{1,0:T(8,128)(2,1)} %bitcast.18), custom_call_target="tpu_custom_call" | custom-call | tf_op jit(solution)/shard_map/prepare/pallas_call | solution.py:602
  2.4 3.0 %collective-permute-start = (f32[96,128]{1,0:T(8,128)}, f32[96,128]{1,0:T(8,128)S(1)}, u32[]{:S(2)}, u32[]{:S(2)}) collective-permute-start(f32[96,128]{1,0:T(8,128)} %get-tuple-element.11.refs_0_), channel_id=1, source_target_pairs={{0,2},{2,0},{1,3},{3,1},{4,6},{6,4},{5,7},{7,5},{8,10},{10,8},{9,1... | collective-permute-start | bytes 147464 | tf_op jit(solution)/shard_map/ppermute | solution.py:574
  5.3 0.0 collective-permute-start.1
  6.0 0.0 copy-start.22
  6.0 0.6 %copy-done.22 = s32[64]{0:T(128)S(1)} copy-done((s32[64]{0:T(128)S(1)}, s32[64]{0:T(128)}, u32[]{:S(2)}) %copy-start.22) | copy-done | bytes 280
  6.7 0.0 copy-start.23
  6.7 0.6 %copy-done.23 = s32[64]{0:T(128)S(1)} copy-done((s32[64]{0:T(128)S(1)}, s32[64]{0:T(128)}, u32[]{:S(2)}) %copy-start.23) | copy-done | bytes 280
  7.4 0.0 copy-start.19
  7.4 0.7 %select_select_fusion.refs_5_ = f32[8,128]{1,0:T(8,128)} fusion(f32[128]{0:T(128)S(1)} %get-tuple-element.22, f32[128]{0:T(128)S(1)} %get-tuple-element.23, f32[128]{0:T(128)S(1)} %get-tuple-element.26, f32[128]{0:T(128)S(1)} %get-tuple-element.27, pred[8]{0:T(512)(128)(4,1)S(1)} %get-tuple-element.24, pred[8]{0:T(512)(128)(4,1)S(1)} %get-tuple-element.25, ...), kind=kLoop, calls=%fused_computation | loop fusion | flops 4096 | bytes 6176 | tf_op jit(solution)/shard_map/jit(_where)/select_n | solution.py:626
  8.0 0.0 copy-done.19
  8.1 0.6 %reshape.55.refs_4_ = f32[1,616]{1,0:T(1,128)} reshape(f32[616]{0:T(1024)S(1)} %copy-done.19) | data formatting | bytes 4928 | tf_op jit(solution)/shard_map/reshape | solution.py:636
  8.7 0.0 collective-permute-done.refs_1_
  8.7 0.0 copy-start.14
  8.7 2.5 %collective-permute-done.1.refs_3_ = f32[64,616]{1,0:T(8,128)S(1)} collective-permute-done((f32[64,616]{1,0:T(8,128)}, f32[64,616]{1,0:T(8,128)S(1)}, u32[]{:S(2)}, u32[]{:S(2)}) %collective-permute-start.1) | collective-permute-done | bytes 157728 | tf_op jit(solution)/shard_map/ppermute | solution.py:574
  11.2 0.7 %copy-done.2 = f32[64,616]{1,0:T(8,128)} copy-done((f32[64,616]{1,0:T(8,128)}, f32[64,616]{1,0:T(8,128)S(1)}, u32[]{:S(2)}) %copy-start.2) | copy-done | bytes 157720
  11.9 2.3 %compose.1.refs_5_ = f32[200,128]{1,0:T(8,128)} custom-call(f32[96,128]{1,0:T(8,128)} %get-tuple-element.11.refs_0_, f32[96,128]{1,0:T(8,128)} %copy-done.14, f32[64,616]{1,0:T(8,128)} %get-tuple-element.12.refs_2_, f32[64,616]{1,0:T(8,128)} %copy-done.2, f32[1,616]{1,0:T(1,128)} %reshape.55.refs_4_, f32[8,128]{1,0:T(8,128)} %select_select_fusion.refs_5_), custom_call_target="tpu_custom_call" | custom-call | tf_op jit(solution)/shard_map/compose/pallas_call | solution.py:629
  14.2 4.1 %collective-permute-start.7 = (f32[200,128]{1,0:T(8,128)}, f32[200,128]{1,0:T(8,128)S(1)}, u32[]{:S(2)}, u32[]{:S(2)}) collective-permute-start(f32[200,128]{1,0:T(8,128)} %compose.1.refs_5_), channel_id=1, source_target_pairs={{0,12},{4,8},{8,4},{12,0},{1,13},{5,9},{9,5},{13,1},{2,14},{6,10},... | collective-permute-start | bytes 307208 | tf_op jit(solution)/shard_map/ppermute | solution.py:568
  18.2 0.0 collective-permute-start.5
  18.2 0.6 %collective-permute-start.3 = (f32[200,128]{1,0:T(8,128)}, f32[200,128]{1,0:T(8,128)S(1)}, u32[]{:S(2)}, u32[]{:S(2)}) collective-permute-start(f32[200,128]{1,0:T(8,128)} %compose.1.refs_5_), channel_id=1, source_target_pairs={{0,4},{4,0},{8,12},{12,8},{1,5},{5,1},{9,13},{13,9},{2,6},{6,2},{1... | collective-permute-start | bytes 307208 | tf_op jit(solution)/shard_map/ppermute | solution.py:568
  18.8 1.1 %collective-permute-start.11 = (f32[128,128]{1,0:T(8,128)S(1)}, f32[128,128]{1,0:T(8,128)S(1)}, u32[]{:S(2)}, u32[]{:S(2)}) collective-permute-start(f32[128,128]{1,0:T(8,128)S(1)} %bitcast.17), channel_id=1, source_target_pairs={{0,2},{2,0},{1,3},{3,1},{4,6},{6,4},{5,7},{7,5},{8,10},{10,8},{9,1... | collective-permute-start | bytes 196616 | tf_op jit(solution)/shard_map/ppermute | solution.py:574
  19.9 0.9 %collective-permute-start.9 = (f32[128,128]{1,0:T(8,128)S(1)}, f32[128,128]{1,0:T(8,128)S(1)}, u32[]{:S(2)}, u32[]{:S(2)}) collective-permute-start(f32[128,128]{1,0:T(8,128)S(1)} %bitcast.14), channel_id=1, source_target_pairs={{0,2},{2,0},{1,3},{3,1},{4,6},{6,4},{5,7},{7,5},{8,10},{10,8},{9,1... | collective-permute-start | bytes 196616 | tf_op jit(solution)/shard_map/ppermute | solution.py:574
  20.8 2.2 %collective-permute-done.11.refs_18_ = f32[128,128]{1,0:T(8,128)S(1)} collective-permute-done((f32[128,128]{1,0:T(8,128)S(1)}, f32[128,128]{1,0:T(8,128)S(1)}, u32[]{:S(2)}, u32[]{:S(2)}) %collective-permute-start.11) | collective-permute-done | bytes 65568 | tf_op jit(solution)/shard_map/ppermute | solution.py:574
  23.1 1.2 %collective-permute-start.10 = (f32[2,128,128]{2,1,0:T(8,128)S(1)}, f32[2,128,128]{2,1,0:T(8,128)S(1)}, u32[]{:S(2)}, u32[]{:S(2)}) collective-permute-start(f32[2,128,128]{2,1,0:T(8,128)S(1)} %copy-done.3), channel_id=1, source_target_pairs={{0,2},{2,0},{1,3},{3,1},{4,6},{6,4},{5,7},{7,5},{8,10},{10,8},{9,1... | collective-permute-start | bytes 393224 | tf_op jit(solution)/shard_map/ppermute | solution.py:574
  24.2 0.6 %collective-permute-done.9.refs_14_ = f32[128,128]{1,0:T(8,128)S(1)} collective-permute-done((f32[128,128]{1,0:T(8,128)S(1)}, f32[128,128]{1,0:T(8,128)S(1)}, u32[]{:S(2)}, u32[]{:S(2)}) %collective-permute-start.9) | collective-permute-done | bytes 65568 | tf_op jit(solution)/shard_map/ppermute | solution.py:574
  24.9 0.5 %collective-permute-start.8 = (f32[200,128]{1,0:T(8,128)S(1)}, f32[200,128]{1,0:T(8,128)S(1)}, u32[]{:S(2)}, u32[]{:S(2)}) collective-permute-start(f32[200,128]{1,0:T(8,128)S(1)} %collective-permute-done.7.refs_11_), channel_id=1, source_target_pairs={{0,1},{1,0},{2,3},{3,2},{4,5},{5,4},{6,7},{7,6},{8,9},{9,8},{10,11... | collective-permute-start | bytes 307208 | tf_op jit(solution)/shard_map/ppermute | solution.py:568
  25.4 1.0 %collective-permute-done.5.refs_9_ = f32[200,128]{1,0:T(8,128)S(1)} collective-permute-done((f32[200,128]{1,0:T(8,128)}, f32[200,128]{1,0:T(8,128)S(1)}, u32[]{:S(2)}, u32[]{:S(2)}) %collective-permute-start.5) | collective-permute-done | bytes 102432 | tf_op jit(solution)/shard_map/ppermute | solution.py:568
  26.4 0.5 %collective-permute-start.4 = (f32[200,128]{1,0:T(8,128)S(1)}, f32[200,128]{1,0:T(8,128)S(1)}, u32[]{:S(2)}, u32[]{:S(2)}) collective-permute-start(f32[200,128]{1,0:T(8,128)S(1)} %collective-permute-done.3.refs_7_), channel_id=1, source_target_pairs={{0,1},{1,0},{2,3},{3,2},{4,5},{5,4},{6,7},{7,6},{8,9},{9,8},{10,11... | collective-permute-start | bytes 307208 | tf_op jit(solution)/shard_map/ppermute | solution.py:568
  26.9 0.1 copy.20
  27.0 0.7 %reshape.49.refs_0_ = s32[32]{0:T(128)} reshape(s32[8,4]{1,0:T(8,128)S(1)} %copy.20) | data formatting | bytes 256 | tf_op jit(solution)/shard_map/reshape | solution.py:677
  27.6 0.0 copy-done.21
  27.6 0.1 copy.21
  27.7 0.6 %reshape.50.refs_1_ = s32[32]{0:T(128)} reshape(s32[8,4]{1,0:T(8,128)S(1)} %copy.21) | data formatting | bytes 256 | tf_op jit(solution)/shard_map/reshape | solution.py:678
  28.4 0.5 %copy-done.4 = f32[2,128,128]{2,1,0:T(8,128)} copy-done((f32[2,128,128]{2,1,0:T(8,128)}, f32[2,128,128]{2,1,0:T(8,128)S(1)}, u32[]{:S(2)}) %copy-start.4) | copy-done | bytes 131096
  28.9 0.0 copy-done.8
  29.0 0.0 copy-done.9
  29.0 0.0 copy-done.10
  29.1 0.6 %copy-done.11 = f32[200,128]{1,0:T(8,128)} copy-done((f32[200,128]{1,0:T(8,128)}, f32[200,128]{1,0:T(8,128)S(1)}, u32[]{:S(2)}) %copy-start.11) | copy-done | bytes 102424
  29.7 7.2 %evolve.1 = (f32[128,128]{1,0:T(8,128)}, f32[8,128]{1,0:T(8,128)}) custom-call(s32[32]{0:T(128)} %reshape.49.refs_0_, s32[32]{0:T(128)} %reshape.50.refs_1_, f32[2]{0:T(128)} %refs_2_.1, f32[2]{0:T(128)} %refs_3_.1, f32[2]{0:T(128)} %refs_4_.1, f32[200,128]{1,0:T(8,128)} %compose.1.refs_5_, f32[200,128]{1,0:T(8,128)} %copy-done.8, f32[200,128]{1,0:T(8,128)} %copy-done.7, ...), custom_call_target="tpu_custom_call" | custom-call | tf_op jit(solution)/shard_map/evolve/pallas_call | solution.py:651
  36.9 0.1 collective-permute-start.12
  37.0 1.3 %collective-permute-done.12 = f32[8,128]{1,0:T(8,128)S(1)} collective-permute-done((f32[8,128]{1,0:T(8,128)}, f32[8,128]{1,0:T(8,128)S(1)}, u32[]{:S(2)}, u32[]{:S(2)}) %collective-permute-start.12) | collective-permute-done | bytes 4128 | tf_op jit(solution)/shard_map/ppermute | solution.py:568
  38.3 0.7 %add.25.refs_0_ = f32[8,128]{1,0:T(8,128)S(1)} add(f32[8,128]{1,0:T(8,128)} %get-tuple-element.14, f32[8,128]{1,0:T(8,128)S(1)} %collective-permute-done.12) | non-fusion elementwise | flops 1024 | bytes 12288 | tf_op jit(solution)/shard_map/add | solution.py:689
  38.9 3.6 %collective-permute-start.15 = (f32[8,128]{1,0:T(8,128)S(1)}, f32[8,128]{1,0:T(8,128)S(1)}, u32[]{:S(2)}, u32[]{:S(2)}) collective-permute-start(f32[8,128]{1,0:T(8,128)S(1)} %add.25.refs_0_), channel_id=1, source_target_pairs={{0,12},{4,8},{8,4},{12,0},{1,13},{5,9},{9,5},{13,1},{2,14},{6,10},... | collective-permute-start | bytes 12296 | tf_op jit(solution)/shard_map/ppermute | solution.py:568
  42.5 0.8 %collective-permute-start.13 = (f32[8,128]{1,0:T(8,128)S(1)}, f32[8,128]{1,0:T(8,128)S(1)}, u32[]{:S(2)}, u32[]{:S(2)}) collective-permute-start(f32[8,128]{1,0:T(8,128)S(1)} %add.25.refs_0_), channel_id=1, source_target_pairs={{0,4},{4,0},{8,12},{12,8},{1,5},{5,1},{9,13},{13,9},{2,6},{6,2},{1... | collective-permute-start | bytes 12296 | tf_op jit(solution)/shard_map/ppermute | solution.py:568
  43.3 1.0 %collective-permute-done.15.refs_3_ = f32[8,128]{1,0:T(8,128)S(1)} collective-permute-done((f32[8,128]{1,0:T(8,128)S(1)}, f32[8,128]{1,0:T(8,128)S(1)}, u32[]{:S(2)}, u32[]{:S(2)}) %collective-permute-start.15) | collective-permute-done | bytes 4128 | tf_op jit(solution)/shard_map/ppermute | solution.py:568
  44.4 2.7 %collective-permute-done.14.refs_2_ = f32[8,128]{1,0:T(8,128)S(1)} collective-permute-done((f32[8,128]{1,0:T(8,128)S(1)}, f32[8,128]{1,0:T(8,128)S(1)}, u32[]{:S(2)}, u32[]{:S(2)}) %collective-permute-start.14) | collective-permute-done | bytes 4128 | tf_op jit(solution)/shard_map/ppermute | solution.py:568
  47.0 0.6 %copy-done.17 = f32[8,128]{1,0:T(8,128)} copy-done((f32[8,128]{1,0:T(8,128)}, f32[8,128]{1,0:T(8,128)S(1)}, u32[]{:S(2)}) %copy-start.17) | copy-done | bytes 4120
  47.6 0.0 copy-done.18
  47.6 1.8 %update.1 = (f32[128,128]{1,0:T(8,128)}, f32[128,128]{1,0:T(8,128)}, f32[128,128]{1,0:T(8,128)}) custom-call(f32[8,128]{1,0:T(8,128)} %copy-done.15, f32[8,128]{1,0:T(8,128)} %copy-done.18, f32[8,128]{1,0:T(8,128)} %copy-done.17, f32[8,128]{1,0:T(8,128)} %copy-done.16, f32[128,128]{1,0:T(8,128)} %bitcast.19, f32[128,128]{1,0:T(8,128)} %bitcast.16, ...), custom_call_target="tpu_custom_call" | custom-call | tf_op jit(solution)/shard_map/update/pallas_call | solution.py:698
  (48 shorter events, 0.1 us)
Async XLA Ops:
  2.4 6.3 %collective-permute-start = (f32[96,128]{1,0:T(8,128)}, f32[96,128]{1,0:T(8,128)S(1)}, u32[]{:S(2)}, u32[]{:S(2)}) collective-permute-start(f32[96,128]{1,0:T(8,128)} %get-tuple-element.11.refs_0_), channel_id=1, source_target_pairs={{0,2},{2,0},{1,3},{3,1},{4,6},{6,4},{5,7},{7,5},{8,10},{10,8},{9,1... | collective-permute-start | bytes 147464 | tf_op jit(solution)/shard_map/ppermute | solution.py:574
  5.3 5.9 %collective-permute-start.1 = (f32[64,616]{1,0:T(8,128)}, f32[64,616]{1,0:T(8,128)S(1)}, u32[]{:S(2)}, u32[]{:S(2)}) collective-permute-start(f32[64,616]{1,0:T(8,128)} %get-tuple-element.12.refs_2_), channel_id=1, source_target_pairs={{0,2},{2,0},{1,3},{3,1},{4,6},{6,4},{5,7},{7,5},{8,10},{10,8},{9,1... | collective-permute-start | bytes 473096 | tf_op jit(solution)/shard_map/ppermute | solution.py:574
  6.0 0.7 %copy-start.22 = (s32[64]{0:T(128)S(1)}, s32[64]{0:T(128)}, u32[]{:S(2)}) copy-start(s32[64]{0:T(128)} %param.25) | copy-start | bytes 772
  6.7 0.7 %copy-start.23 = (s32[64]{0:T(128)S(1)}, s32[64]{0:T(128)}, u32[]{:S(2)}) copy-start(s32[64]{0:T(128)} %param.26) | copy-start | bytes 772
  7.4 0.7 %copy-start.19 = (f32[616]{0:T(1024)S(1)}, f32[616]{0:T(1024)}, u32[]{:S(2)}) copy-start(f32[616]{0:T(1024)} %param.29) | copy-start | bytes 7396
  8.6 10.1 %copy-start.1 = (f32[1,128,128]{2,1,0:T(8,128)S(1)}, f32[1,128,128]{2,1,0:T(8,128)}, u32[]{:S(2)}) copy-start(f32[1,128,128]{2,1,0:T(8,128)} %param.16) | copy-start | bytes 196612
  8.7 11.2 %copy-start = (f32[1,128,128]{2,1,0:T(8,128)S(1)}, f32[1,128,128]{2,1,0:T(8,128)}, u32[]{:S(2)}) copy-start(f32[1,128,128]{2,1,0:T(8,128)} %param.17) | copy-start | bytes 196612
  8.7 14.4 %copy-start.3 = (f32[2,128,128]{2,1,0:T(8,128)S(1)}, f32[2,128,128]{2,1,0:T(8,128)}, u32[]{:S(2)}) copy-start(f32[2,128,128]{2,1,0:T(8,128)} %get-tuple-element.13.refs_15_) | copy-start | bytes 393220
  8.7 2.5 %copy-start.14 = (f32[96,128]{1,0:T(8,128)}, f32[96,128]{1,0:T(8,128)S(1)}, u32[]{:S(2)}) copy-start(f32[96,128]{1,0:T(8,128)S(1)} %collective-permute-done.refs_1_) | copy-start | bytes 147460
  11.2 0.7 %copy-start.2 = (f32[64,616]{1,0:T(8,128)}, f32[64,616]{1,0:T(8,128)S(1)}, u32[]{:S(2)}) copy-start(f32[64,616]{1,0:T(8,128)S(1)} %collective-permute-done.1.refs_3_) | copy-start | bytes 473092
  14.2 12.7 %copy-start.20 = (s32[8,4]{0,1:T(4,128)S(1)}, s32[8,4]{0,1:T(4,128)}, u32[]{:S(2)}) copy-start(s32[8,4]{0,1:T(4,128)} %param.23) | copy-start | bytes 388
  14.2 10.7 %collective-permute-start.7 = (f32[200,128]{1,0:T(8,128)}, f32[200,128]{1,0:T(8,128)S(1)}, u32[]{:S(2)}, u32[]{:S(2)}) collective-permute-start(f32[200,128]{1,0:T(8,128)} %compose.1.refs_5_), channel_id=1, source_target_pairs={{0,12},{4,8},{8,4},{12,0},{1,13},{5,9},{9,5},{13,1},{2,14},{6,10},... | collective-permute-start | bytes 307208 | tf_op jit(solution)/shard_map/ppermute | solution.py:568
  18.2 8.1 %collective-permute-start.5 = (f32[200,128]{1,0:T(8,128)}, f32[200,128]{1,0:T(8,128)S(1)}, u32[]{:S(2)}, u32[]{:S(2)}) collective-permute-start(f32[200,128]{1,0:T(8,128)} %compose.1.refs_5_), channel_id=1, source_target_pairs={{0,8},{4,12},{8,0},{12,4},{1,9},{5,13},{9,1},{13,5},{2,10},{6,14},... | collective-permute-start | bytes 307208 | tf_op jit(solution)/shard_map/ppermute | solution.py:568
  18.2 8.1 %collective-permute-start.3 = (f32[200,128]{1,0:T(8,128)}, f32[200,128]{1,0:T(8,128)S(1)}, u32[]{:S(2)}, u32[]{:S(2)}) collective-permute-start(f32[200,128]{1,0:T(8,128)} %compose.1.refs_5_), channel_id=1, source_target_pairs={{0,4},{4,0},{8,12},{12,8},{1,5},{5,1},{9,13},{13,9},{2,6},{6,2},{1... | collective-permute-start | bytes 307208 | tf_op jit(solution)/shard_map/ppermute | solution.py:568
  18.8 4.3 %collective-permute-start.11 = (f32[128,128]{1,0:T(8,128)S(1)}, f32[128,128]{1,0:T(8,128)S(1)}, u32[]{:S(2)}, u32[]{:S(2)}) collective-permute-start(f32[128,128]{1,0:T(8,128)S(1)} %bitcast.17), channel_id=1, source_target_pairs={{0,2},{2,0},{1,3},{3,1},{4,6},{6,4},{5,7},{7,5},{8,10},{10,8},{9,1... | collective-permute-start | bytes 196616 | tf_op jit(solution)/shard_map/ppermute | solution.py:574
  19.9 5.0 %collective-permute-start.9 = (f32[128,128]{1,0:T(8,128)S(1)}, f32[128,128]{1,0:T(8,128)S(1)}, u32[]{:S(2)}, u32[]{:S(2)}) collective-permute-start(f32[128,128]{1,0:T(8,128)S(1)} %bitcast.14), channel_id=1, source_target_pairs={{0,2},{2,0},{1,3},{3,1},{4,6},{6,4},{5,7},{7,5},{8,10},{10,8},{9,1... | collective-permute-start | bytes 196616 | tf_op jit(solution)/shard_map/ppermute | solution.py:574
  23.1 5.3 %copy-start.12 = (f32[128,128]{1,0:T(8,128)}, f32[128,128]{1,0:T(8,128)S(1)}, u32[]{:S(2)}) copy-start(f32[128,128]{1,0:T(8,128)S(1)} %collective-permute-done.11.refs_18_) | copy-start | bytes 196612
  23.1 5.2 %collective-permute-start.10 = (f32[2,128,128]{2,1,0:T(8,128)S(1)}, f32[2,128,128]{2,1,0:T(8,128)S(1)}, u32[]{:S(2)}, u32[]{:S(2)}) collective-permute-start(f32[2,128,128]{2,1,0:T(8,128)S(1)} %copy-done.3), channel_id=1, source_target_pairs={{0,2},{2,0},{1,3},{3,1},{4,6},{6,4},{5,7},{7,5},{8,10},{10,8},{9,1... | collective-permute-start | bytes 393224 | tf_op jit(solution)/shard_map/ppermute | solution.py:574
  24.9 3.5 %copy-start.13 = (f32[128,128]{1,0:T(8,128)}, f32[128,128]{1,0:T(8,128)S(1)}, u32[]{:S(2)}) copy-start(f32[128,128]{1,0:T(8,128)S(1)} %collective-permute-done.9.refs_14_) | copy-start | bytes 196612
  24.9 3.4 %collective-permute-start.2 = (f32[200,128]{1,0:T(8,128)}, f32[200,128]{1,0:T(8,128)S(1)}, u32[]{:S(2)}, u32[]{:S(2)}) collective-permute-start(f32[200,128]{1,0:T(8,128)} %compose.1.refs_5_), channel_id=1, source_target_pairs={{0,1},{1,0},{2,3},{3,2},{4,5},{5,4},{6,7},{7,6},{8,9},{9,8},{10,11... | collective-permute-start | bytes 307208 | tf_op jit(solution)/shard_map/ppermute | solution.py:568
  24.9 3.5 %copy-start.5 = (f32[200,128]{1,0:T(8,128)}, f32[200,128]{1,0:T(8,128)S(1)}, u32[]{:S(2)}) copy-start(f32[200,128]{1,0:T(8,128)S(1)} %collective-permute-done.7.refs_11_) | copy-start | bytes 307204
  24.9 3.4 %collective-permute-start.8 = (f32[200,128]{1,0:T(8,128)S(1)}, f32[200,128]{1,0:T(8,128)S(1)}, u32[]{:S(2)}, u32[]{:S(2)}) collective-permute-start(f32[200,128]{1,0:T(8,128)S(1)} %collective-permute-done.7.refs_11_), channel_id=1, source_target_pairs={{0,1},{1,0},{2,3},{3,2},{4,5},{5,4},{6,7},{7,6},{8,9},{9,8},{10,11... | collective-permute-start | bytes 307208 | tf_op jit(solution)/shard_map/ppermute | solution.py:568
  26.4 2.0 %copy-start.6 = (f32[200,128]{1,0:T(8,128)}, f32[200,128]{1,0:T(8,128)S(1)}, u32[]{:S(2)}) copy-start(f32[200,128]{1,0:T(8,128)S(1)} %collective-permute-done.5.refs_9_) | copy-start | bytes 307204
  26.4 2.0 %collective-permute-start.6 = (f32[200,128]{1,0:T(8,128)S(1)}, f32[200,128]{1,0:T(8,128)S(1)}, u32[]{:S(2)}, u32[]{:S(2)}) collective-permute-start(f32[200,128]{1,0:T(8,128)S(1)} %collective-permute-done.5.refs_9_), channel_id=1, source_target_pairs={{0,1},{1,0},{2,3},{3,2},{4,5},{5,4},{6,7},{7,6},{8,9},{9,8},{10,11... | collective-permute-start | bytes 307208 | tf_op jit(solution)/shard_map/ppermute | solution.py:568
  26.4 2.0 %copy-start.7 = (f32[200,128]{1,0:T(8,128)}, f32[200,128]{1,0:T(8,128)S(1)}, u32[]{:S(2)}) copy-start(f32[200,128]{1,0:T(8,128)S(1)} %collective-permute-done.3.refs_7_) | copy-start | bytes 307204
  26.4 2.0 %collective-permute-start.4 = (f32[200,128]{1,0:T(8,128)S(1)}, f32[200,128]{1,0:T(8,128)S(1)}, u32[]{:S(2)}, u32[]{:S(2)}) collective-permute-start(f32[200,128]{1,0:T(8,128)S(1)} %collective-permute-done.3.refs_7_), channel_id=1, source_target_pairs={{0,1},{1,0},{2,3},{3,2},{4,5},{5,4},{6,7},{7,6},{8,9},{9,8},{10,11... | collective-permute-start | bytes 307208 | tf_op jit(solution)/shard_map/ppermute | solution.py:568
  27.0 0.7 %copy-start.21 = (s32[8,4]{0,1:T(4,128)S(1)}, s32[8,4]{0,1:T(4,128)}, u32[]{:S(2)}) copy-start(s32[8,4]{0,1:T(4,128)} %param.24) | copy-start | bytes 388
  28.3 0.7 %copy-start.4 = (f32[2,128,128]{2,1,0:T(8,128)}, f32[2,128,128]{2,1,0:T(8,128)S(1)}, u32[]{:S(2)}) copy-start(f32[2,128,128]{2,1,0:T(8,128)S(1)} %collective-permute-done.10.refs_16_) | copy-start | bytes 393220
  28.3 0.7 %copy-start.8 = (f32[200,128]{1,0:T(8,128)}, f32[200,128]{1,0:T(8,128)S(1)}, u32[]{:S(2)}) copy-start(f32[200,128]{1,0:T(8,128)S(1)} %collective-permute-done.2.refs_6_) | copy-start | bytes 307204
  28.3 0.7 %copy-start.9 = (f32[200,128]{1,0:T(8,128)}, f32[200,128]{1,0:T(8,128)S(1)}, u32[]{:S(2)}) copy-start(f32[200,128]{1,0:T(8,128)S(1)} %collective-permute-done.8.refs_12_) | copy-start | bytes 307204
  28.3 0.7 %copy-start.10 = (f32[200,128]{1,0:T(8,128)}, f32[200,128]{1,0:T(8,128)S(1)}, u32[]{:S(2)}) copy-start(f32[200,128]{1,0:T(8,128)S(1)} %collective-permute-done.6.refs_10_) | copy-start | bytes 307204
  29.1 0.6 %copy-start.11 = (f32[200,128]{1,0:T(8,128)}, f32[200,128]{1,0:T(8,128)S(1)}, u32[]{:S(2)}) copy-start(f32[200,128]{1,0:T(8,128)S(1)} %collective-permute-done.4.refs_8_) | copy-start | bytes 307204
  36.9 1.4 %collective-permute-start.12 = (f32[8,128]{1,0:T(8,128)}, f32[8,128]{1,0:T(8,128)S(1)}, u32[]{:S(2)}, u32[]{:S(2)}) collective-permute-start(f32[8,128]{1,0:T(8,128)} %get-tuple-element.14), channel_id=1, source_target_pairs={{0,1},{1,0},{2,3},{3,2},{4,5},{5,4},{6,7},{7,6},{8,9},{9,8},{10,11... | collective-permute-start | bytes 12296 | tf_op jit(solution)/shard_map/ppermute | solution.py:568
  38.9 8.1 %copy-start.15 = (f32[8,128]{1,0:T(8,128)}, f32[8,128]{1,0:T(8,128)S(1)}, u32[]{:S(2)}) copy-start(f32[8,128]{1,0:T(8,128)S(1)} %add.25.refs_0_) | copy-start | bytes 12292
  38.9 5.4 %collective-permute-start.15 = (f32[8,128]{1,0:T(8,128)S(1)}, f32[8,128]{1,0:T(8,128)S(1)}, u32[]{:S(2)}, u32[]{:S(2)}) collective-permute-start(f32[8,128]{1,0:T(8,128)S(1)} %add.25.refs_0_), channel_id=1, source_target_pairs={{0,12},{4,8},{8,4},{12,0},{1,13},{5,9},{9,5},{13,1},{2,14},{6,10},... | collective-permute-start | bytes 12296 | tf_op jit(solution)/shard_map/ppermute | solution.py:568
  42.5 4.5 %collective-permute-start.14 = (f32[8,128]{1,0:T(8,128)S(1)}, f32[8,128]{1,0:T(8,128)S(1)}, u32[]{:S(2)}, u32[]{:S(2)}) collective-permute-start(f32[8,128]{1,0:T(8,128)S(1)} %add.25.refs_0_), channel_id=1, source_target_pairs={{0,8},{4,12},{8,0},{12,4},{1,9},{5,13},{9,1},{13,5},{2,10},{6,14},... | collective-permute-start | bytes 12296 | tf_op jit(solution)/shard_map/ppermute | solution.py:568
  42.5 4.5 %collective-permute-start.13 = (f32[8,128]{1,0:T(8,128)S(1)}, f32[8,128]{1,0:T(8,128)S(1)}, u32[]{:S(2)}, u32[]{:S(2)}) collective-permute-start(f32[8,128]{1,0:T(8,128)S(1)} %add.25.refs_0_), channel_id=1, source_target_pairs={{0,4},{4,0},{8,12},{12,8},{1,5},{5,1},{9,13},{13,9},{2,6},{6,2},{1... | collective-permute-start | bytes 12296 | tf_op jit(solution)/shard_map/ppermute | solution.py:568
  44.4 2.7 %copy-start.16 = (f32[8,128]{1,0:T(8,128)}, f32[8,128]{1,0:T(8,128)S(1)}, u32[]{:S(2)}) copy-start(f32[8,128]{1,0:T(8,128)S(1)} %collective-permute-done.15.refs_3_) | copy-start | bytes 12292
  47.0 0.6 %copy-start.17 = (f32[8,128]{1,0:T(8,128)}, f32[8,128]{1,0:T(8,128)S(1)}, u32[]{:S(2)}) copy-start(f32[8,128]{1,0:T(8,128)S(1)} %collective-permute-done.14.refs_2_) | copy-start | bytes 12292
  47.0 0.6 %copy-start.18 = (f32[8,128]{1,0:T(8,128)}, f32[8,128]{1,0:T(8,128)S(1)}, u32[]{:S(2)}) copy-start(f32[8,128]{1,0:T(8,128)S(1)} %collective-permute-done.13.refs_1_) | copy-start | bytes 12292

commit v2 on v1

--- a/solution.py
+++ b/solution.py
@@ -1,3 +1,5 @@
+import functools
+
 import jax
 import jax.numpy as jnp
 from jax import lax
@@ -5,12 +7,14 @@
 from jax.experimental.pallas import tpu as pltpu
 from jax.sharding import PartitionSpec as P
 
+
 STEPS = 4
 DEEP = 2 * STEPS
 SIDES = 4
 FIELDS = 3
 BAND = SIDES * FIELDS * DEEP
 LANES = 128
+CHAIN_AT = BAND
 SHEETS = LANES // DEEP
 CHUNK = 512
 F32 = jnp.float32
@@ -22,6 +26,14 @@
 NW, NE, SW, SE = range(4)
 
 
+def near(value):
+    return pltpu.with_memory_space_constraint(value, pltpu.VMEM)
+
+
+def limit(mebibytes):
+    return pltpu.CompilerParams(vmem_limit_bytes=mebibytes << 20)
+
+
 def iota(shape, axis):
     return lax.broadcasted_iota(jnp.int32, shape, axis)
 
@@ -38,14 +50,33 @@
     return lax.rem(lax.axis_index("lev") + (levels - k), levels)
 
 
-def prepare(direction, wind_u, wind_v, jacobian, bands, winds, wide):
+def prepare(bits, count, diffusion, vertical, prior, direction, wind_u, wind_v, residual, jacobian, columns, times, errors, bands, fields, wide, places, weights, scalars):
     x = direction[...]
     u = 0.5 * wind_u[...].astype(F32)
     v = 0.5 * wind_v[...].astype(F32)
     width = x.shape[0]
-    winds[0] = u
-    winds[1] = v
     wide[...] = jacobian[...].astype(F32)
+    fields[0] = x
+    fields[1] = u
+    fields[2] = v
+    fields[3] = residual[...]
+    slots = columns.shape[1]
+    column = columns[...]
+    mask = (1 << bits) - 1
+    alive = iota((1, slots), 1) < count[0]
+    panel = jnp.where(alive, lax.shift_right_logical(column, 2 * bits), -1)
+    rows = [panel, lax.shift_right_logical(column, bits) & mask, column & mask, times[...]]
+    rows = jnp.concatenate(rows + rows, axis=0).astype(F32)
+    if slots < LANES:
+        rows = jnp.concatenate([rows, jnp.full((rows.shape[0], LANES - slots), -1.0, F32)], axis=1)
+    places[...] = rows
+    weights[...] = errors[...].reshape(1, -1)
+    levels = diffusion.shape[0]
+    scalars[...] = jnp.zeros(scalars.shape, F32)
+    for index, values in enumerate((diffusion, vertical, prior)):
+        for level in range(levels):
+            at = index * levels + level
+            scalars[at : at + 1, :] = jnp.full((1, LANES), values[level], F32)
     first = lambda a: a[:DEEP]
     last = lambda a: jnp.concatenate([a[width - 1 - d : width - d] for d in range(DEEP)], axis=0)
     xt, ut, vt = x.T, u.T, v.T
@@ -62,31 +93,25 @@
 
 
 def compose(levels, *refs):
-    bands = refs[:levels]
-    jacobians = refs[levels : 2 * levels]
-    error_inv, places, message, ordered = refs[2 * levels :]
+    jacobians = refs[:levels]
+    weights, places, record, ordered = refs[levels:]
     for k in range(levels):
-        level = rotated(levels, k)
-        message[pl.ds(pl.multiple_of(level * BAND, 8), BAND), :] = bands[k][...]
-        ordered[level] = jacobians[k][...].astype(F32)
+        ordered[rotated(levels, k)] = jacobians[k][...]
     slots = ordered.shape[1]
-    base = levels * BAND
-    place = places[...]
     ones = jnp.ones((8, ordered.shape[2]), F32)
-    weights = error_inv[...]
-    pairs = level_pairs(levels)
-    rows = [place[:4, :]]
-    for low, high in pairs:
-        product = ordered[low] * weights * ordered[high]
+    scale = weights[...]
+    rows = []
+    for low, high in level_pairs(levels):
+        product = ordered[low] * scale * ordered[high]
         total = lax.dot_general(ones, product, NT, precision=lax.Precision.HIGHEST, preferred_element_type=F32)
-        row = total[:1]
-        if slots < LANES:
-            row = jnp.concatenate([row, jnp.zeros((1, LANES - slots), F32)], axis=1)
-        rows.append(row)
-    spare = record_rows(levels) - 4 - len(pairs)
+        rows.append(total[:1])
+    spare = record_rows(levels) - 4 - len(rows)
     if spare:
-        rows.append(jnp.zeros((spare, LANES), F32))
-    message[base : base + record_rows(levels), :] = jnp.concatenate(rows, axis=0)
+        rows.append(jnp.zeros((spare, slots), F32))
+    whole = jnp.concatenate(rows, axis=0)
+    if slots < LANES:
+        whole = jnp.concatenate([whole, jnp.zeros((whole.shape[0], LANES - slots), F32)], axis=1)
+    record[...] = jnp.concatenate([places[:4, :], whole], axis=0)
 
 
 def roll(a, shift, axis):
@@ -198,62 +223,34 @@
 PARTS = ("m", "n", "s", "ew", "c")
 
 
-def evolve(levels, gathered_count, panels, slots, *refs):
-    pair, flip, diffusion, vertical, prior = refs[:5]
-    refs = refs[5:]
-    messages, refs = refs[:gathered_count], refs[gathered_count:]
-    directions, refs = refs[:levels], refs[levels:]
-    winds, refs = refs[:levels], refs[levels:]
-    residuals, refs = refs[:levels], refs[levels:]
-    image_out, sums_out = refs[:2]
-    (
-        table,
-        x_main,
-        w_main,
-        images,
-        x_band,
-        w_band,
-        x_ew,
-        w_ew,
-        x_chain,
-        w_chain,
-        x_far,
-        g_main,
-        g_band,
-        g_ew,
-        g_chain,
-        obs,
-        square,
-    ) = refs[2:]
-    width = directions[0].shape[0]
+def assemble(count, *refs):
+    pair, flip = refs[:2]
+    messages = refs[2 : 2 + count]
+    parts, labels, table = refs[2 + count :]
+    width = LANES
     last = width - 1
-    tiles, subs = lax.axis_size("tile"), lax.axis_size("sub")
+    subs = lax.axis_size("sub")
     tile, sub = lax.axis_index("tile"), lax.axis_index("sub")
     me = tile * subs + sub
-    rows = table.shape[1]
-    if gathered_count == 1:
-        table[...] = messages[0][...]
+    if count == 1:
+        source = messages[0]
     else:
-        for index in range(gathered_count):
+        source = table
+        for index in range(count):
             xt, xs = index // subs, index % subs
             table[(tile ^ xt) * subs + (sub ^ xs)] = messages[index][...]
-    for k in range(levels):
-        level = rotated(levels, k)
-        x_main[level] = directions[k][...]
-        w_main[level] = winds[k][...]
 
     lane8 = iota((DEEP, LANES), 1)
     straight, reverse = lane8 % DEEP, last - lane8 % DEEP
     slot_of = lane8 // DEEP
 
-    def band(panel, side, level, field):
-        start = pl.multiple_of(level * BAND + (side * FIELDS + field) * DEEP, 8)
-        return table[panel, pl.ds(start, DEEP), :]
+    def band(panel, side, field):
+        start = pl.multiple_of((side * FIELDS + field) * DEEP, 8)
+        return source[panel, pl.ds(start, DEEP), :]
 
     def lookup(panel, side):
-        at = SIDES * panel + side
-        other = pair[at]
-        return lax.shift_right_logical(other, 2), other & 3, flip[at]
+        other = pair[side, panel]
+        return lax.shift_right_logical(other, 2), other & 3, flip[side, panel]
 
     def cross_row(sheet):
         panel, row_side, col_side = sheet
@@ -267,27 +264,14 @@
         end = (row_side & 1) ^ flipped
         return panel, end + jnp.where(side < 2, 2, 0), side
 
-    partners = [lookup(me, side) for side in range(SIDES)]
-    for level in range(levels):
-        turned = [[None] * FIELDS for _ in range(SIDES)]
-        for side, (panel, other, flipped) in enumerate(partners):
-            order = jnp.where(flipped == 1, last - lane8, lane8)
-            sign = jnp.where(flipped == 1, -1.0, 1.0).astype(F32)
-            for field in range(FIELDS):
-                values = jnp.take_along_axis(band(panel, other, level, field), order, axis=1)
-                turned[side][field] = values * sign if field == 2 else values
-        for index in range(2):
-            x_band[level, index] = turned[index][0]
-            w_band[level, index, 0] = turned[index][1]
-            w_band[level, index, 1] = turned[index][2]
-        square[...] = jnp.zeros((width, LANES), F32)
-        for field, target in ((0, None), (2, 0), (1, 1)):
-            square[:DEEP, :] = turned[3][field]
-            square[LANES // 2 : LANES // 2 + DEEP, :] = turned[2][field]
-            if target is None:
-                x_ew[level] = square[...].T
-            else:
-                w_ew[level, target] = square[...].T
+    for side in range(SIDES):
+        panel, other, flipped = lookup(me, side)
+        order = jnp.where(flipped == 1, last - lane8, lane8)
+        sign = jnp.where(flipped == 1, -1.0, 1.0).astype(F32)
+        for field in range(FIELDS):
+            values = jnp.take_along_axis(band(panel, other, field), order, axis=1)
+            at = (side * FIELDS + field) * DEEP
+            parts[at : at + DEEP, :] = values * sign if field == 2 else values
 
     keys, kinds = [], []
     for corner, (row_side, col_side) in enumerate(CORNERS):
@@ -298,7 +282,7 @@
             ahead = cross_row(ahead) if k % 2 == 0 else cross_col(ahead)
             behind = cross_col(behind) if k % 2 == 0 else cross_row(behind)
             sheets[k + 1], sheets[-k - 1] = ahead, behind
-        filled = [[jnp.zeros((DEEP, LANES), F32)] * FIELDS for _ in range(levels)]
+        filled = [jnp.zeros((DEEP, LANES), F32)] * FIELDS
         key = jnp.full((1, LANES), -1, jnp.int32)
         kind = jnp.full((1, LANES), -1, jnp.int32)
         for k, (panel, side, other) in sheets.items():
@@ -306,49 +290,58 @@
             order = jnp.where(end == 1, reverse, straight)
             sign = jnp.where(end == 1, -1.0, 1.0).astype(F32)
             if k == DEEP:
-                for level in range(levels):
-                    x_far[level, corner * DEEP : (corner + 1) * DEEP, :] = jnp.take_along_axis(
-                        band(panel, side, level, 0), order, axis=1
-                    )
+                at = CHAIN_AT + (FIELDS * SIDES + corner) * DEEP
+                parts[at : at + DEEP, :] = jnp.take_along_axis(band(panel, side, 0), order, axis=1)
                 continue
             here = slot_of == k % SHEETS
-            for level in range(levels):
-                for field in range(FIELDS):
-                    values = jnp.take_along_axis(band(panel, side, level, field), order, axis=1)
-                    values = values * sign if field == 2 else values
-                    filled[level][field] = jnp.where(here, values, filled[level][field])
+            for field in range(FIELDS):
+                values = jnp.take_along_axis(band(panel, side, field), order, axis=1)
+                values = values * sign if field == 2 else values
+                filled[field] = jnp.where(here, values, filled[field])
             if abs(k) <= STEPS:
                 key = jnp.where(here[:1], panel * width + order[:1], key)
                 kind = jnp.where(here[:1], side, kind)
         keys.append(key)
         kinds.append(kind)
-        place = slice(corner * DEEP, (corner + 1) * DEEP)
-        for level in range(levels):
-            x_chain[level, place, :] = filled[level][0]
-            w_chain[level, 0, place, :] = filled[level][1]
-            w_chain[level, 1, place, :] = filled[level][2]
-
+        for field in range(FIELDS):
+            at = CHAIN_AT + (field * SIDES + corner) * DEEP
+            parts[at : at + DEEP, :] = filled[field]
+    labels[...] = jnp.concatenate(keys + kinds, axis=0).astype(F32)
+
+
+def gains(levels, slots, count, *refs):
+    pair, flip, labels = refs[:3]
+    records = refs[3 : 3 + count]
+    g_main, g_band, g_ew, g_chain, obs, square = refs[3 + count :]
+    width = LANES
+    last = width - 1
+    subs = lax.axis_size("sub")
+    me = lax.axis_index("tile") * subs + lax.axis_index("sub")
     pairs = level_pairs(levels)
     depth_rows = record_rows(levels)
-    base = levels * BAND
     fold = LANES // slots
     lane_rec = iota((depth_rows, LANES), 1)
-    chunk_tiles = obs.shape[2] // LANES
-    for group in range(panels // fold):
-        packed = table[group * fold, base : base + depth_rows, :]
+    chunks, _, span = obs.shape
+    chunk_tiles = span // LANES
+    pieces = []
+    for ref in records:
+        if len(ref.shape) == 3:
+            pieces += [ref[index] for index in range(ref.shape[0])]
+        else:
+            pieces += [ref[at : at + depth_rows, :] for at in range(0, ref.shape[0], depth_rows)]
+    for group in range(len(pieces) // fold):
+        packed = pieces[group * fold]
         for part in range(1, fold):
-            shifted = roll(table[group * fold + part, base : base + depth_rows, :], part * slots, 1)
+            shifted = roll(pieces[group * fold + part], part * slots, 1)
             packed = jnp.where(lane_rec // slots == part, shifted, packed)
         column = (group % chunk_tiles) * LANES
         obs[group // chunk_tiles, :, column : column + LANES] = packed
-    chunks = obs.shape[0]
-    span = obs.shape[2]
-    key_columns = jnp.concatenate(keys, axis=0)
-    kind_columns = jnp.concatenate(kinds, axis=0)
-    key_tall = jnp.concatenate(
-        [key_columns, kind_columns, jnp.zeros((LANES - 8, LANES), jnp.int32)], axis=0
-    ).astype(F32).T
+    label_tall = jnp.concatenate([labels[...], jnp.zeros((LANES - 8, LANES), F32)], axis=0).T
     comps = STEPS * len(pairs)
+    partners = []
+    for side in range(SIDES):
+        other = pair[side, me]
+        partners.append((lax.shift_right_logical(other, 2), other & 3, flip[side, me]))
 
     def hits(mask):
         return jnp.where(mask, 1.0, 0.0).astype(BF16)
@@ -377,8 +370,8 @@
         chain_hit = [jnp.where(short == distance[side], 1.0, 0.0) for side in range(SIDES)]
         chain_place = []
         for corner in range(4):
-            key = key_tall[:, corner : corner + 1].astype(jnp.int32)
-            kind = key_tall[:, 4 + corner : 5 + corner].astype(jnp.int32)
+            key = label_tall[:, corner : corner + 1].astype(jnp.int32)
+            kind = label_tall[:, 4 + corner : 5 + corner].astype(jnp.int32)
             chain_place.append(
                 [hits((key == spot[side // 2]) & (kind == side)) for side in range(SIDES)]
             )
@@ -410,7 +403,11 @@
             value = product(tall_rows(band_hit[side]), band_place[side])
             for comp in range(comps):
                 at = 2 * comp * DEEP
-                put(g_band, (side, comp), value[at : at + DEEP] + value[at + DEEP : at + 2 * DEEP])
+                total = value[at : at + DEEP] + value[at + DEEP : at + 2 * DEEP]
+                if side < 2:
+                    put(g_band, (side, comp), total)
+                else:
+                    put(square, (side - 2, comp), total)
         lefts = [tall_rows(chain_hit[side]) for side in range(SIDES)]
         for corner in range(4):
             value = product(lefts[0], chain_place[corner][0])
@@ -431,12 +428,47 @@
         g_main[...] = jnp.zeros(g_main.shape, F32)
         g_band[...] = jnp.zeros(g_band.shape, F32)
         g_chain[...] = jnp.zeros(g_chain.shape, F32)
+        square[...] = jnp.zeros(square.shape, F32)
         lax.fori_loop(0, chunks, accumulate, 0)
     for comp in range(comps):
-        square[...] = jnp.zeros((width, LANES), F32)
-        square[:DEEP, :] = g_band[3, comp]
-        square[LANES // 2 : LANES // 2 + DEEP, :] = g_band[2, comp]
-        g_ew[comp] = square[...].T
+        g_ew[comp] = side_by_side(square[1, comp], square[0, comp])
+
+
+def side_by_side(east, west):
+    gap = jnp.zeros((LANES // 2 - DEEP, LANES), F32)
+    return jnp.concatenate([east, gap, west, gap], axis=0).T
+
+
+def evolve(levels, *refs):
+    scalars, refs = refs[0], refs[1:]
+    diffusion, vertical, prior = (
+        [scalars[index * levels + level : index * levels + level + 1, :] for level in range(levels)] for index in range(3)
+    )
+    parts, refs = refs[:levels], refs[levels:]
+    fields, refs = refs[:levels], refs[levels:]
+    g_main, g_band, g_ew, g_chain = refs[:4]
+    image_out, sums_out, x_main, w_main, images, x_band, w_band, x_ew, w_ew, x_chain, w_chain, x_far = refs[4:]
+    width = LANES
+    pairs = level_pairs(levels)
+    for k in range(levels):
+        level = rotated(levels, k)
+        x_main[level] = fields[k][0]
+        w_main[level, 0] = fields[k][1]
+        w_main[level, 1] = fields[k][2]
+        part = parts[k]
+        piece = lambda side, field: part[(side * FIELDS + field) * DEEP : (side * FIELDS + field + 1) * DEEP, :]
+        for index in range(2):
+            x_band[level, index] = piece(index, 0)
+            w_band[level, index, 0] = piece(index, 1)
+            w_band[level, index, 1] = piece(index, 2)
+        x_ew[level] = side_by_side(piece(3, 0), piece(2, 0))
+        w_ew[level, 0] = side_by_side(piece(3, 2), piece(2, 2))
+        w_ew[level, 1] = side_by_side(piece(3, 1), piece(2, 1))
+        chain = lambda field: part[CHAIN_AT + field * SIDES * DEEP : CHAIN_AT + (field + 1) * SIDES * DEEP, :]
+        x_chain[level] = chain(0)
+        w_chain[level, 0] = chain(1)
+        w_chain[level, 1] = chain(2)
+        x_far[level] = chain(3)
 
     geometry = Geometry(width)
     mix = [diffusion[level] for level in range(levels)]
@@ -537,7 +569,7 @@
     for k in range(levels):
         level = rotated(levels, k)
         image = images[level]
-        residual, direction = residuals[k][...], directions[k][...]
+        residual, direction = fields[k][3], fields[k][0]
         if k == 0:
             image_out[...] = image
         for index, term in enumerate((residual * residual, direction * image, residual * image, image * image)):
@@ -568,11 +600,24 @@
     return lax.ppermute(value, axis, [(i, i ^ mask) for i in range(count)])
 
 
+def gathered(value, joined):
+    tiles, subs = lax.axis_size("tile"), lax.axis_size("sub")
+    if tiles > 4:
+        return [lax.all_gather(value, ("tile", "sub"), axis=0)]
+    if joined:
+        out = [value] + [exchanged(value, "tile", mask) for mask in range(1, tiles)]
+        whole = jnp.concatenate(out, axis=0)
+        return [whole] + [exchanged(whole, "sub", mask) for mask in range(1, subs)]
+    out = [value] + [exchanged(value, "sub", mask) for mask in range(1, subs)]
+    for mask in range(1, tiles):
+        other = exchanged(value, "tile", mask)
+        out += [other] + [exchanged(other, "sub", by) for by in range(1, subs)]
+    return out
+
+
 def level_parts(value):
     count = lax.axis_size("lev")
-    return [value] + [
-        lax.ppermute(value, "lev", [(i, (i + k) % count) for i in range(count)]) for k in range(1, count)
-    ]
+    return [value] + [lax.ppermute(value, "lev", [(i, (i + k) % count) for i in range(count)]) for k in range(1, count)]
 
 
 def body(
@@ -599,91 +644,97 @@
     shape = (width, width)
     flat = lambda a: a.reshape(shape)
     own = jacobian.reshape(slots, channels)
-    bands, winds, wide = pl.pallas_call(
-        prepare,
+    depth_rows = record_rows(levels)
+    row = lambda a: a.reshape(1, -1)
+    scalar_rows = -(-3 * levels // 8) * 8
+    bands, fields, wide, places, weights, scalars = pl.pallas_call(
+        functools.partial(prepare, width.bit_length() - 1),
         out_shape=(
-            jax.ShapeDtypeStruct((BAND, LANES), F32),
-            jax.ShapeDtypeStruct((2,) + shape, F32),
-            jax.ShapeDtypeStruct((slots, channels), F32),
+            pltpu.VMEM((BAND, LANES), F32),
+            pltpu.VMEM((4,) + shape, F32),
+            pltpu.VMEM((slots, channels), F32),
+            pltpu.VMEM((8, LANES), F32),
+            pltpu.VMEM((1, channels), F32),
+            pltpu.VMEM((scalar_rows, LANES), F32),
         ),
-        in_specs=[WHOLE] * 4,
-        out_specs=(WHOLE,) * 3,
+        in_specs=[SCALAR] * 4 + [WHOLE] * 8,
+        out_specs=(WHOLE,) * 6,
+        compiler_params=limit(60),
         name="prepare",
-    )(flat(direction), flat(wind_u), flat(wind_v), own)
-    all_bands = level_parts(bands)
+    )(
+        obs_count,
+        diffusion,
+        vertical,
+        background_inv,
+        flat(direction),
+        flat(wind_u),
+        flat(wind_v),
+        flat(residual),
+        own,
+        row(obs_column),
+        row(obs_time),
+        error_inv,
+    )
     all_wide = level_parts(wide)
-    all_winds = level_parts(winds)
-    all_directions = level_parts(flat(direction))
-    all_residuals = level_parts(flat(residual))
-
-    area = width * width
-    alive = jnp.arange(slots, dtype=jnp.int32) < obs_count[0]
-    places = [jnp.where(alive, obs_column // area, -1), (obs_column % area) // width, obs_column % width, obs_time]
-    place_rows = jnp.full((8, LANES), -1.0, F32)
-    row_at = iota((8, LANES), 0)
-    for index, values in enumerate(places):
-        padded = jnp.pad(values, (0, LANES - slots), constant_values=-1).astype(F32)
-        place_rows = jnp.where(row_at == index, padded[None, :], place_rows)
-
-    rows = levels * BAND + record_rows(levels)
-    message = pl.pallas_call(
-        lambda *refs: compose(levels, *refs),
-        out_shape=jax.ShapeDtypeStruct((rows, LANES), F32),
-        in_specs=[WHOLE] * (2 * levels + 2),
+    all_fields = level_parts(fields)
+
+    record = pl.pallas_call(
+        functools.partial(compose, levels),
+        out_shape=pltpu.VMEM((depth_rows, LANES), F32),
+        in_specs=[WHOLE] * (levels + 2),
         out_specs=WHOLE,
         scratch_shapes=[pltpu.VMEM((levels, slots, channels), F32)],
+        compiler_params=limit(8),
         name="compose",
-    )(*all_bands, *all_wide, error_inv.reshape(1, channels), place_rows)
-
-    if tiles <= 4:
-        mine = [message] + [exchanged(message, "tile", mask) for mask in range(1, tiles)]
-        messages = []
-        for value in mine:
-            messages += [value] + [exchanged(value, "sub", mask) for mask in range(1, subs)]
-    else:
-        messages = [lax.all_gather(message, ("tile", "sub"), axis=0)]
+    )(*[near(a) for a in (*all_wide, weights, places)])
+    messages, records = gathered(bands, False), gathered(record, True)
+
+    pair, flip = side_pair.T, side_flip.T
+    vmem = lambda *dims: pltpu.VMEM(dims, F32)
+    parts, labels = pl.pallas_call(
+        functools.partial(assemble, len(messages)),
+        out_shape=(vmem(CHAIN_AT + 4 * SIDES * DEEP, LANES), vmem(8, LANES)),
+        in_specs=[SCALAR] * 2 + [WHOLE] * len(messages),
+        out_specs=(WHOLE, WHOLE),
+        scratch_shapes=[vmem(panels, BAND, LANES)],
+        compiler_params=limit(8),
+        name="assemble",
+    )(pair, flip, *[near(a) for a in messages])
+    all_parts = level_parts(parts)
 
     span = min(CHUNK, panels * slots)
-    pairs = len(level_pairs(levels))
-    comps = STEPS * pairs
+    comps = STEPS * len(level_pairs(levels))
     chain = (SIDES * DEEP, LANES)
-    vmem = lambda *dims: pltpu.VMEM(dims, F32)
+    products = pl.pallas_call(
+        functools.partial(gains, levels, slots, len(records)),
+        out_shape=(vmem(comps, *shape), vmem(2, comps, DEEP, LANES), vmem(comps, *shape), vmem(comps, *chain)),
+        in_specs=[SCALAR] * 2 + [WHOLE] * (1 + len(records)),
+        out_specs=(WHOLE,) * 4,
+        scratch_shapes=[vmem(panels * slots // span, depth_rows, span), vmem(2, comps, DEEP, LANES)],
+        compiler_params=limit(16),
+        name="gains",
+    )(pair, flip, *[near(a) for a in (labels, *records)])
+
     image, sums = pl.pallas_call(
-        lambda *refs: evolve(levels, len(messages), panels, slots, *refs),
-        out_shape=(jax.ShapeDtypeStruct(shape, F32), jax.ShapeDtypeStruct((8, LANES), F32)),
-        in_specs=[SCALAR] * 5 + [WHOLE] * (len(messages) + 3 * levels),
+        functools.partial(evolve, levels),
+        out_shape=(vmem(*shape), vmem(8, LANES)),
+        in_specs=[WHOLE] * (2 * levels + 5),
         out_specs=(WHOLE, WHOLE),
         scratch_shapes=[
-            vmem(panels, rows, LANES),
             vmem(levels, *shape),
             vmem(levels, 2, *shape),
             vmem(levels, *shape),
             vmem(levels, 2, DEEP, LANES),
             vmem(levels, 2, 2, DEEP, LANES),
-            vmem(levels, width, LANES),
-            vmem(levels, 2, width, LANES),
+            vmem(levels, *shape),
+            vmem(levels, 2, *shape),
             vmem(levels, *chain),
             vmem(levels, 2, *chain),
             vmem(levels, *chain),
-            vmem(comps, *shape),
-            vmem(SIDES, comps, DEEP, LANES),
-            vmem(comps, width, LANES),
-            vmem(comps, *chain),
-            vmem(panels * slots // span, record_rows(levels), span),
-            vmem(width, LANES),
         ],
+        compiler_params=limit(12),
         name="evolve",
-    )(
-        side_pair.reshape(-1),
-        side_flip.reshape(-1),
-        diffusion,
-        vertical,
-        background_inv,
-        *messages,
-        *all_directions,
-        *all_winds,
-        *all_residuals,
-    )
+    )(*[near(a) for a in (scalars, *all_parts, *all_fields, *products)])
 
     for mask in range(1, subs):
         sums = sums + exchanged(sums, "sub", mask)
@@ -700,8 +751,9 @@
         out_shape=(jax.ShapeDtypeStruct(shape, F32),) * 3,
         in_specs=[WHOLE] * (len(parts) + 4),
         out_specs=(WHOLE,) * 3,
+        compiler_params=limit(4),
         name="update",
-    )(*parts, flat(increment), flat(residual), flat(direction), image)
+    )(*[near(a) for a in (*parts, flat(increment), flat(residual), flat(direction), image)])
     return tuple(out.reshape(increment.shape) for out in outputs)
 
 

time: 49.7 us -> 38.3 us (0.77)
  local copies, waits for them, and re-layouts: 5.9 us -> 0.03 us
  Pallas kernels: 13 us -> 9.27 us
  waiting for transfers between devices: 11.4 us -> 8.37 us
  starting transfers between devices: 16.3 us -> 19 us
  other arithmetic: 1.4 us -> 0.01 us
    ppermute x5 -> x3, waiting for transfers between devices: 5.41 us -> 0.01 us  [level_parts(): lax.ppermute(value, 'lev', [(i, (i + k) % count) for i in range(count)])]
    ppermute x11 -> x15, starting transfers between devices: 10.1 us -> 14.3 us  [exchanged(): return lax.ppermute(value, axis, [(i, i ^ mask) for i in range(count)])]
    unnamed x50 -> x10, local copies, waits for them, and re-layouts: 4.08 us -> 0.03 us
    pallas_call x3 -> x5, Pallas kernels: 11.2 us -> 8.47 us  [the longest x1 2.79 us: body(): pl.pallas_call(functools.partial(gains, levels, slots, len(records)), out...]
    ppermute x11 -> x15, waiting for transfers between devices: 5.97 us -> 8.36 us  [exchanged(): return lax.ppermute(value, axis, [(i, i ^ mask) for i in range(count)])]
    reshape x3 -> x0, local copies, waits for them, and re-layouts: 1.82 us -> none  [the longest x1 0.66 us: body(): side_pair.reshape(-1)]
    ppermute x5 -> x3, starting transfers between devices: 6.17 us -> 4.67 us  [level_parts(): lax.ppermute(value, 'lev', [(i, (i + k) % count) for i in range(count)])]
    pallas_call x1, Pallas kernels: 1.75 us -> 0.81 us  [body(): pl.pallas_call(update, out_shape=(jax.ShapeDtypeStruct(shape, F32),) * 3,...]
  transfers between devices with their start and end apart: 16 -> 18, of which waited for: 7 -> 6; matrix products, arithmetic and copies ran while one was open for 5% -> 0% of each run, Pallas kernels for 0% -> 12%
where the time goes in v2:
time: 38.3 us; the launch traced here: 38.1 us
  starting transfers between devices  19 us (50%)
  Pallas kernels  9.27 us (24%)
  waiting for transfers between devices  8.37 us (22%)
  between operations  1.4 us (4%)
    ppermute x15, starting transfers between devices, exchanged(): return lax.ppermute(value, axis, [(i, i ^ mask) for i in range(count)])  14.3 us
    ppermute x15, waiting for transfers between devices, exchanged(): return lax.ppermute(value, axis, [(i, i ^ mask) for i in range(count)])  8.36 us
    ppermute x3, starting transfers between devices, level_parts(): lax.ppermute(value, 'lev', [(i, (i + k) % count) for i in range(count)])  4.67 us
    pallas_call x1, Pallas kernels, body(): pl.pallas_call(functools.partial(gains, levels, slots, len(records)), out...  2.79 us
    pallas_call x1, Pallas kernels, body(): pl.pallas_call(functools.partial(evolve, levels), out_shape=(vmem(*shape)...  2.73 us
    pallas_call x1, Pallas kernels, body(): pl.pallas_call(functools.partial(assemble, len(messages)), out_shape=(vme...  1.19 us
    pallas_call x1, Pallas kernels, body(): pl.pallas_call(functools.partial(prepare, width.bit_length() - 1), out_sh...  1.17 us
    pallas_call x1, Pallas kernels, body(): pl.pallas_call(update, out_shape=(jax.ShapeDtypeStruct(shape, F32),) * 3,...  0.81 us
  transfers between devices with their start and end apart: 18, of which 6 were waited for; matrix products, arithmetic and copies ran while one was open for 0% of the time, Pallas kernels for 12%

profile of v2, /device:TPU:0, one launch (start us, length us, event | category | flops | bytes accessed | tf_op | source)
XLA Modules:
  0.0 38.1 jit_solution(12339473783959268194)
XLA Ops:
  1.3 1.2 %prepare.1 = (f32[96,128]{1,0:T(8,128)S(1)}, f32[4,128,128]{2,1,0:T(8,128)S(1)}, f32[64,616]{1,0:T(8,128)S(1)}, f32[8,128]{1,0:T(8,128)S(1)}, f32[1,616]{1,0:T(1,128)S(1)}, /*index=5*/f32[8,128]{1,0:T(8,128)S(1)}) custom-call(s32[1]{0:T(128)S(6)} %copy.18.count, f32[2]{0:T(128)} %diffusion.1, f32[2]{0:T(128)} %vertical.1, f32[2]{0:T(128)} %prior.1, ...), custom_call_target="tpu_custom_call" | custom-call | tf_op jit(solution)/shard_map/prepare/pallas_call | solution.py:650
  2.5 3.0 %collective-permute-start.9 = (f32[64,616]{1,0:T(8,128)S(1)}, f32[64,616]{1,0:T(8,128)S(1)}, u32[]{:S(2)}, u32[]{:S(2)}) collective-permute-start(f32[64,616]{1,0:T(8,128)S(1)} %get-tuple-element.25.refs_0_), channel_id=1, source_target_pairs={{0,2},{2,0},{1,3},{3,1},{4,6},{6,4},{5,7},{7,5},{8,10},{10,8},{9,1... | collective-permute-start | bytes 473096 | tf_op jit(solution)/shard_map/ppermute | solution.py:620
  5.5 0.1 collective-permute-start.8
  5.6 4.1 %collective-permute-start.5 = (f32[96,128]{1,0:T(8,128)S(1)}, f32[96,128]{1,0:T(8,128)S(1)}, u32[]{:S(2)}, u32[]{:S(2)}) collective-permute-start(f32[96,128]{1,0:T(8,128)S(1)} %get-tuple-element.21.refs_2_), channel_id=1, source_target_pairs={{0,12},{4,8},{8,4},{12,0},{1,13},{5,9},{9,5},{13,1},{2,14},{6,10},... | collective-permute-start | bytes 147464 | tf_op jit(solution)/shard_map/ppermute | solution.py:600
  9.6 0.0 collective-permute-start.3
  9.6 0.6 %collective-permute-start.1 = (f32[96,128]{1,0:T(8,128)S(1)}, f32[96,128]{1,0:T(8,128)S(1)}, u32[]{:S(2)}, u32[]{:S(2)}) collective-permute-start(f32[96,128]{1,0:T(8,128)S(1)} %get-tuple-element.21.refs_2_), channel_id=1, source_target_pairs={{0,4},{4,0},{8,12},{12,8},{1,5},{5,1},{9,13},{13,9},{2,6},{6,2},{1... | collective-permute-start | bytes 147464 | tf_op jit(solution)/shard_map/ppermute | solution.py:600
  10.2 2.1 %collective-permute-done.5.refs_8_ = f32[96,128]{1,0:T(8,128)S(1)} collective-permute-done((f32[96,128]{1,0:T(8,128)S(1)}, f32[96,128]{1,0:T(8,128)S(1)}, u32[]{:S(2)}, u32[]{:S(2)}) %collective-permute-start.5) | collective-permute-done | bytes 49184 | tf_op jit(solution)/shard_map/ppermute | solution.py:600
  12.3 0.0 collective-permute-start
  12.3 2.3 %collective-permute-done.3.refs_6_ = f32[96,128]{1,0:T(8,128)S(1)} collective-permute-done((f32[96,128]{1,0:T(8,128)S(1)}, f32[96,128]{1,0:T(8,128)S(1)}, u32[]{:S(2)}, u32[]{:S(2)}) %collective-permute-start.3) | collective-permute-done | bytes 49184 | tf_op jit(solution)/shard_map/ppermute | solution.py:600
  14.6 0.0 collective-permute-start.6
  14.6 0.0 collective-permute-done.1.refs_4_
  14.6 0.5 %collective-permute-start.4 = (f32[96,128]{1,0:T(8,128)S(1)}, f32[96,128]{1,0:T(8,128)S(1)}, u32[]{:S(2)}, u32[]{:S(2)}) collective-permute-start(f32[96,128]{1,0:T(8,128)S(1)} %collective-permute-done.3.refs_6_), channel_id=1, source_target_pairs={{0,1},{1,0},{2,3},{3,2},{4,5},{5,4},{6,7},{7,6},{8,9},{9,8},{10,11... | collective-permute-start | bytes 147464 | tf_op jit(solution)/shard_map/ppermute | solution.py:600
  15.1 0.0 collective-permute-done.9.refs_1_
  15.1 0.1 collective-permute-start.2
  15.2 0.6 %compose.1 = f32[8,128]{1,0:T(8,128)S(1)} custom-call(f32[64,616]{1,0:T(8,128)S(1)} %get-tuple-element.25.refs_0_, f32[64,616]{1,0:T(8,128)S(1)} %collective-permute-done.9.refs_1_, f32[1,616]{1,0:T(1,128)S(1)} %get-tuple-element.26.refs_2_, f32[8,128]{1,0:T(8,128)S(1)} %get-tuple-element.27.refs_3_), custom_call_target="tpu_custom_call" | custom-call | tf_op jit(solution)/shard_map/compose/pallas_call | solution.py:681
  15.8 0.0 collective-permute-done.refs_3_
  15.8 1.7 %collective-permute-start.12 = (f32[8,128]{1,0:T(8,128)S(1)}, f32[8,128]{1,0:T(8,128)S(1)}, u32[]{:S(2)}, u32[]{:S(2)}) collective-permute-start(f32[8,128]{1,0:T(8,128)S(1)} %compose.1), channel_id=1, source_target_pairs={{0,12},{4,8},{8,4},{12,0},{1,13},{5,9},{9,5},{13,1},{2,14},{6,10},... | collective-permute-start | bytes 12296 | tf_op jit(solution)/shard_map/ppermute | solution.py:600
  17.5 0.0 collective-permute-done.6.refs_9_
  17.5 0.4 %collective-permute-start.11 = (f32[8,128]{1,0:T(8,128)S(1)}, f32[8,128]{1,0:T(8,128)S(1)}, u32[]{:S(2)}, u32[]{:S(2)}) collective-permute-start(f32[8,128]{1,0:T(8,128)S(1)} %compose.1), channel_id=1, source_target_pairs={{0,8},{4,12},{8,0},{12,4},{1,9},{5,13},{9,1},{13,5},{2,10},{6,14},... | collective-permute-start | bytes 12296 | tf_op jit(solution)/shard_map/ppermute | solution.py:600
  17.9 0.0 collective-permute-done.4.refs_7_
  17.9 2.4 %collective-permute-start.10 = (f32[8,128]{1,0:T(8,128)S(1)}, f32[8,128]{1,0:T(8,128)S(1)}, u32[]{:S(2)}, u32[]{:S(2)}) collective-permute-start(f32[8,128]{1,0:T(8,128)S(1)} %compose.1), channel_id=1, source_target_pairs={{0,4},{4,0},{8,12},{12,8},{1,5},{5,1},{9,13},{13,9},{2,6},{6,2},{1... | collective-permute-start | bytes 12296 | tf_op jit(solution)/shard_map/ppermute | solution.py:600
  20.3 0.0 collective-permute-done.2.refs_5_
  20.3 0.0 copy-done.4
  20.3 0.0 copy-done.3
  20.3 1.2 %assemble.1 = (f32[224,128]{1,0:T(8,128)S(1)}, f32[8,128]{1,0:T(8,128)S(1)}) custom-call(s32[4,8]{1,0:T(4,128)S(1)} %bitcast.18, s32[4,8]{1,0:T(4,128)S(1)} %bitcast.20, f32[96,128]{1,0:T(8,128)S(1)} %get-tuple-element.21.refs_2_, f32[96,128]{1,0:T(8,128)S(1)} %collective-permute-done.refs_3_, f32[96,128]{1,0:T(8,128)S(1)} %collective-permute-done.1.refs_4_, ...), custom_call_target="tpu_custom_call" | custom-call | tf_op jit(solution)/shard_map/assemble/pallas_call | solution.py:694
  21.5 1.6 %collective-permute-start.7 = (f32[224,128]{1,0:T(8,128)S(1)}, f32[224,128]{1,0:T(8,128)S(1)}, u32[]{:S(2)}, u32[]{:S(2)}) collective-permute-start(f32[224,128]{1,0:T(8,128)S(1)} %get-tuple-element.22.refs_1_), channel_id=1, source_target_pairs={{0,2},{2,0},{1,3},{3,1},{4,6},{6,4},{5,7},{7,5},{8,10},{10,8},{9,1... | collective-permute-start | bytes 344072 | tf_op jit(solution)/shard_map/ppermute | solution.py:620
  23.1 0.0 collective-permute-done.12
  23.1 0.0 collective-permute-done.11
  23.1 0.0 collective-permute-done.10
  23.1 0.1 collective-permute-start.13
  23.2 1.2 %collective-permute-done.13.refs_4_ = f32[32,128]{1,0:T(8,128)S(1)} collective-permute-done((f32[32,128]{1,0:T(8,128)S(1)}, f32[32,128]{1,0:T(8,128)S(1)}, u32[]{:S(2)}, u32[]{:S(2)}) %collective-permute-start.13) | collective-permute-done | bytes 16416 | tf_op jit(solution)/shard_map/ppermute | solution.py:600
  24.3 2.8 %gains.1 = (f32[12,128,128]{2,1,0:T(8,128)S(1)}, f32[2,12,8,128]{3,2,1,0:T(8,128)S(1)}, f32[12,128,128]{2,1,0:T(8,128)S(1)}, f32[12,32,128]{2,1,0:T(8,128)S(1)}) custom-call(s32[4,8]{1,0:T(4,128)S(1)} %bitcast.19, s32[4,8]{1,0:T(4,128)S(1)} %bitcast.21, f32[8,128]{1,0:T(8,128)S(1)} %get-tuple-element.24.refs_2_, f32[32,128]{1,0:T(8,128)S(1)} %pad_maximum_fusion.refs_3_, ...), custom_call_target="tpu_custom_call" | custom-call | tf_op jit(solution)/shard_map/gains/pallas_call | solution.py:708
  27.1 0.0 collective-permute-done.7.refs_2_
  27.1 0.0 collective-permute-done.8.refs_4_
  27.1 0.0 copy-start
  27.2 0.0 copy-start.1
  27.2 0.0 copy-start.2
  27.2 2.7 %evolve.1 = (f32[128,128]{1,0:T(8,128)S(1)}, f32[8,128]{1,0:T(8,128)S(1)}) custom-call(f32[8,128]{1,0:T(8,128)S(1)} %get-tuple-element.20.refs_0_, f32[224,128]{1,0:T(8,128)S(1)} %get-tuple-element.22.refs_1_, f32[224,128]{1,0:T(8,128)S(1)} %collective-permute-done.7.refs_2_, f32[4,128,128]{2,1,0:T(8,128)S(1)} %get-tuple-element.23.refs_3_, ...), custom_call_target="tpu_custom_call" | custom-call | tf_op jit(solution)/shard_map/evolve/pallas_call | solution.py:718
  29.9 0.2 collective-permute-start.14
  30.1 1.0 %collective-permute-done.14 = f32[8,128]{1,0:T(8,128)S(1)} collective-permute-done((f32[8,128]{1,0:T(8,128)S(1)}, f32[8,128]{1,0:T(8,128)S(1)}, u32[]{:S(2)}, u32[]{:S(2)}) %collective-permute-start.14) | collective-permute-done | bytes 4128 | tf_op jit(solution)/shard_map/ppermute | solution.py:600
  31.2 1.6 %collective-permute-start.17 = (f32[8,128]{1,0:T(8,128)S(1)}, f32[8,128]{1,0:T(8,128)S(1)}, u32[]{:S(2)}, u32[]{:S(2)}) collective-permute-start(f32[8,128]{1,0:T(8,128)S(1)} %add.3.refs_0_), channel_id=1, source_target_pairs={{0,12},{4,8},{8,4},{12,0},{1,13},{5,9},{9,5},{13,1},{2,14},{6,10},... | collective-permute-start | bytes 12296 | tf_op jit(solution)/shard_map/ppermute | solution.py:600
  32.8 0.6 %collective-permute-start.16 = (f32[8,128]{1,0:T(8,128)S(1)}, f32[8,128]{1,0:T(8,128)S(1)}, u32[]{:S(2)}, u32[]{:S(2)}) collective-permute-start(f32[8,128]{1,0:T(8,128)S(1)} %add.3.refs_0_), channel_id=1, source_target_pairs={{0,8},{4,12},{8,0},{12,4},{1,9},{5,13},{9,1},{13,5},{2,10},{6,14},... | collective-permute-start | bytes 12296 | tf_op jit(solution)/shard_map/ppermute | solution.py:600
  33.4 2.2 %collective-permute-start.15 = (f32[8,128]{1,0:T(8,128)S(1)}, f32[8,128]{1,0:T(8,128)S(1)}, u32[]{:S(2)}, u32[]{:S(2)}) collective-permute-start(f32[8,128]{1,0:T(8,128)S(1)} %add.3.refs_0_), channel_id=1, source_target_pairs={{0,4},{4,0},{8,12},{12,8},{1,5},{5,1},{9,13},{13,9},{2,6},{6,2},{1... | collective-permute-start | bytes 12296 | tf_op jit(solution)/shard_map/ppermute | solution.py:600
  35.5 1.0 %collective-permute-done.17.refs_3_ = f32[8,128]{1,0:T(8,128)S(1)} collective-permute-done((f32[8,128]{1,0:T(8,128)S(1)}, f32[8,128]{1,0:T(8,128)S(1)}, u32[]{:S(2)}, u32[]{:S(2)}) %collective-permute-start.17) | collective-permute-done | bytes 4128 | tf_op jit(solution)/shard_map/ppermute | solution.py:600
  36.6 0.7 %collective-permute-done.16.refs_2_ = f32[8,128]{1,0:T(8,128)S(1)} collective-permute-done((f32[8,128]{1,0:T(8,128)S(1)}, f32[8,128]{1,0:T(8,128)S(1)}, u32[]{:S(2)}, u32[]{:S(2)}) %collective-permute-start.16) | collective-permute-done | bytes 4128 | tf_op jit(solution)/shard_map/ppermute | solution.py:600
  37.3 0.0 collective-permute-done.15.refs_1_
  37.3 0.0 copy-done
  37.3 0.8 %update.1 = (f32[128,128]{1,0:T(8,128)}, f32[128,128]{1,0:T(8,128)}, f32[128,128]{1,0:T(8,128)}) custom-call(f32[8,128]{1,0:T(8,128)S(1)} %add.3.refs_0_, f32[8,128]{1,0:T(8,128)S(1)} %collective-permute-done.15.refs_1_, f32[8,128]{1,0:T(8,128)S(1)} %collective-permute-done.16.refs_2_, f32[8,128]{1,0:T(8,128)S(1)} %collective-permute-done.17.refs_3_, ...), custom_call_target="tpu_custom_call" | custom-call | tf_op jit(solution)/shard_map/update/pallas_call | solution.py:749
  (6 shorter events, 0.0 us)
Async XLA Ops:
  2.5 12.7 %collective-permute-start.9 = (f32[64,616]{1,0:T(8,128)S(1)}, f32[64,616]{1,0:T(8,128)S(1)}, u32[]{:S(2)}, u32[]{:S(2)}) collective-permute-start(f32[64,616]{1,0:T(8,128)S(1)} %get-tuple-element.25.refs_0_), channel_id=1, source_target_pairs={{0,2},{2,0},{1,3},{3,1},{4,6},{6,4},{5,7},{7,5},{8,10},{10,8},{9,1... | collective-permute-start | bytes 473096 | tf_op jit(solution)/shard_map/ppermute | solution.py:620
  5.5 21.6 %collective-permute-start.8 = (f32[4,128,128]{2,1,0:T(8,128)S(1)}, f32[4,128,128]{2,1,0:T(8,128)S(1)}, u32[]{:S(2)}, u32[]{:S(2)}) collective-permute-start(f32[4,128,128]{2,1,0:T(8,128)S(1)} %get-tuple-element.23.refs_3_), channel_id=1, source_target_pairs={{0,2},{2,0},{1,3},{3,1},{4,6},{6,4},{5,7},{7,5},{8,10},{10,8},{9,1... | collective-permute-start | bytes 786440 | tf_op jit(solution)/shard_map/ppermute | solution.py:620
  5.6 6.7 %collective-permute-start.5 = (f32[96,128]{1,0:T(8,128)S(1)}, f32[96,128]{1,0:T(8,128)S(1)}, u32[]{:S(2)}, u32[]{:S(2)}) collective-permute-start(f32[96,128]{1,0:T(8,128)S(1)} %get-tuple-element.21.refs_2_), channel_id=1, source_target_pairs={{0,12},{4,8},{8,4},{12,0},{1,13},{5,9},{9,5},{13,1},{2,14},{6,10},... | collective-permute-start | bytes 147464 | tf_op jit(solution)/shard_map/ppermute | solution.py:600
  9.6 5.0 %collective-permute-start.3 = (f32[96,128]{1,0:T(8,128)S(1)}, f32[96,128]{1,0:T(8,128)S(1)}, u32[]{:S(2)}, u32[]{:S(2)}) collective-permute-start(f32[96,128]{1,0:T(8,128)S(1)} %get-tuple-element.21.refs_2_), channel_id=1, source_target_pairs={{0,8},{4,12},{8,0},{12,4},{1,9},{5,13},{9,1},{13,5},{2,10},{6,14},... | collective-permute-start | bytes 147464 | tf_op jit(solution)/shard_map/ppermute | solution.py:600
  9.6 5.0 %collective-permute-start.1 = (f32[96,128]{1,0:T(8,128)S(1)}, f32[96,128]{1,0:T(8,128)S(1)}, u32[]{:S(2)}, u32[]{:S(2)}) collective-permute-start(f32[96,128]{1,0:T(8,128)S(1)} %get-tuple-element.21.refs_2_), channel_id=1, source_target_pairs={{0,4},{4,0},{8,12},{12,8},{1,5},{5,1},{9,13},{13,9},{2,6},{6,2},{1... | collective-permute-start | bytes 147464 | tf_op jit(solution)/shard_map/ppermute | solution.py:600
  12.3 3.6 %collective-permute-start = (f32[96,128]{1,0:T(8,128)S(1)}, f32[96,128]{1,0:T(8,128)S(1)}, u32[]{:S(2)}, u32[]{:S(2)}) collective-permute-start(f32[96,128]{1,0:T(8,128)S(1)} %get-tuple-element.21.refs_2_), channel_id=1, source_target_pairs={{0,1},{1,0},{2,3},{3,2},{4,5},{5,4},{6,7},{7,6},{8,9},{9,8},{10,11... | collective-permute-start | bytes 147464 | tf_op jit(solution)/shard_map/ppermute | solution.py:600
  14.6 2.9 %collective-permute-start.6 = (f32[96,128]{1,0:T(8,128)S(1)}, f32[96,128]{1,0:T(8,128)S(1)}, u32[]{:S(2)}, u32[]{:S(2)}) collective-permute-start(f32[96,128]{1,0:T(8,128)S(1)} %collective-permute-done.5.refs_8_), channel_id=1, source_target_pairs={{0,1},{1,0},{2,3},{3,2},{4,5},{5,4},{6,7},{7,6},{8,9},{9,8},{10,11... | collective-permute-start | bytes 147464 | tf_op jit(solution)/shard_map/ppermute | solution.py:600
  14.6 3.3 %collective-permute-start.4 = (f32[96,128]{1,0:T(8,128)S(1)}, f32[96,128]{1,0:T(8,128)S(1)}, u32[]{:S(2)}, u32[]{:S(2)}) collective-permute-start(f32[96,128]{1,0:T(8,128)S(1)} %collective-permute-done.3.refs_6_), channel_id=1, source_target_pairs={{0,1},{1,0},{2,3},{3,2},{4,5},{5,4},{6,7},{7,6},{8,9},{9,8},{10,11... | collective-permute-start | bytes 147464 | tf_op jit(solution)/shard_map/ppermute | solution.py:600
  15.1 5.2 %collective-permute-start.2 = (f32[96,128]{1,0:T(8,128)S(1)}, f32[96,128]{1,0:T(8,128)S(1)}, u32[]{:S(2)}, u32[]{:S(2)}) collective-permute-start(f32[96,128]{1,0:T(8,128)S(1)} %collective-permute-done.1.refs_4_), channel_id=1, source_target_pairs={{0,1},{1,0},{2,3},{3,2},{4,5},{5,4},{6,7},{7,6},{8,9},{9,8},{10,11... | collective-permute-start | bytes 147464 | tf_op jit(solution)/shard_map/ppermute | solution.py:600
  15.2 5.1 %copy-start.4 = (s32[8,4]{0,1:T(4,128)S(1)}, s32[8,4]{0,1:T(4,128)}, u32[]{:S(2)}) copy-start(s32[8,4]{0,1:T(4,128)} %param.24) | copy-start | bytes 388
  15.8 4.5 %copy-start.3 = (s32[8,4]{0,1:T(4,128)S(1)}, s32[8,4]{0,1:T(4,128)}, u32[]{:S(2)}) copy-start(s32[8,4]{0,1:T(4,128)} %param.23) | copy-start | bytes 388
  15.8 7.2 %collective-permute-start.12 = (f32[8,128]{1,0:T(8,128)S(1)}, f32[8,128]{1,0:T(8,128)S(1)}, u32[]{:S(2)}, u32[]{:S(2)}) collective-permute-start(f32[8,128]{1,0:T(8,128)S(1)} %compose.1), channel_id=1, source_target_pairs={{0,12},{4,8},{8,4},{12,0},{1,13},{5,9},{9,5},{13,1},{2,14},{6,10},... | collective-permute-start | bytes 12296 | tf_op jit(solution)/shard_map/ppermute | solution.py:600
  17.5 5.5 %collective-permute-start.11 = (f32[8,128]{1,0:T(8,128)S(1)}, f32[8,128]{1,0:T(8,128)S(1)}, u32[]{:S(2)}, u32[]{:S(2)}) collective-permute-start(f32[8,128]{1,0:T(8,128)S(1)} %compose.1), channel_id=1, source_target_pairs={{0,8},{4,12},{8,0},{12,4},{1,9},{5,13},{9,1},{13,5},{2,10},{6,14},... | collective-permute-start | bytes 12296 | tf_op jit(solution)/shard_map/ppermute | solution.py:600
  17.9 5.1 %collective-permute-start.10 = (f32[8,128]{1,0:T(8,128)S(1)}, f32[8,128]{1,0:T(8,128)S(1)}, u32[]{:S(2)}, u32[]{:S(2)}) collective-permute-start(f32[8,128]{1,0:T(8,128)S(1)} %compose.1), channel_id=1, source_target_pairs={{0,4},{4,0},{8,12},{12,8},{1,5},{5,1},{9,13},{13,9},{2,6},{6,2},{1... | collective-permute-start | bytes 12296 | tf_op jit(solution)/shard_map/ppermute | solution.py:600
  21.5 5.6 %collective-permute-start.7 = (f32[224,128]{1,0:T(8,128)S(1)}, f32[224,128]{1,0:T(8,128)S(1)}, u32[]{:S(2)}, u32[]{:S(2)}) collective-permute-start(f32[224,128]{1,0:T(8,128)S(1)} %get-tuple-element.22.refs_1_), channel_id=1, source_target_pairs={{0,2},{2,0},{1,3},{3,1},{4,6},{6,4},{5,7},{7,5},{8,10},{10,8},{9,1... | collective-permute-start | bytes 344072 | tf_op jit(solution)/shard_map/ppermute | solution.py:620
  23.1 1.2 %collective-permute-start.13 = (f32[32,128]{1,0:T(8,128)S(1)}, f32[32,128]{1,0:T(8,128)S(1)}, u32[]{:S(2)}, u32[]{:S(2)}) collective-permute-start(f32[32,128]{1,0:T(8,128)S(1)} %pad_maximum_fusion.refs_3_), channel_id=1, source_target_pairs={{0,1},{1,0},{2,3},{3,2},{4,5},{5,4},{6,7},{7,6},{8,9},{9,8},{10,11... | collective-permute-start | bytes 49160 | tf_op jit(solution)/shard_map/ppermute | solution.py:600
  27.1 10.1 %copy-start = (f32[1,128,128]{2,1,0:T(8,128)S(1)}, f32[1,128,128]{2,1,0:T(8,128)}, u32[]{:S(2)}) copy-start(f32[1,128,128]{2,1,0:T(8,128)} %param.17) | copy-start | bytes 196612
  27.2 10.1 %copy-start.1 = (f32[1,128,128]{2,1,0:T(8,128)S(1)}, f32[1,128,128]{2,1,0:T(8,128)}, u32[]{:S(2)}) copy-start(f32[1,128,128]{2,1,0:T(8,128)} %param.16) | copy-start | bytes 196612
  27.2 10.1 %copy-start.2 = (f32[1,128,128]{2,1,0:T(8,128)S(1)}, f32[1,128,128]{2,1,0:T(8,128)}, u32[]{:S(2)}) copy-start(f32[1,128,128]{2,1,0:T(8,128)} %param.15) | copy-start | bytes 196612
  29.9 1.2 %collective-permute-start.14 = (f32[8,128]{1,0:T(8,128)S(1)}, f32[8,128]{1,0:T(8,128)S(1)}, u32[]{:S(2)}, u32[]{:S(2)}) collective-permute-start(f32[8,128]{1,0:T(8,128)S(1)} %get-tuple-element.32), channel_id=1, source_target_pairs={{0,1},{1,0},{2,3},{3,2},{4,5},{5,4},{6,7},{7,6},{8,9},{9,8},{10,11... | collective-permute-start | bytes 12296 | tf_op jit(solution)/shard_map/ppermute | solution.py:600
  31.2 5.4 %collective-permute-start.17 = (f32[8,128]{1,0:T(8,128)S(1)}, f32[8,128]{1,0:T(8,128)S(1)}, u32[]{:S(2)}, u32[]{:S(2)}) collective-permute-start(f32[8,128]{1,0:T(8,128)S(1)} %add.3.refs_0_), channel_id=1, source_target_pairs={{0,12},{4,8},{8,4},{12,0},{1,13},{5,9},{9,5},{13,1},{2,14},{6,10},... | collective-permute-start | bytes 12296 | tf_op jit(solution)/shard_map/ppermute | solution.py:600
  32.8 4.5 %collective-permute-start.16 = (f32[8,128]{1,0:T(8,128)S(1)}, f32[8,128]{1,0:T(8,128)S(1)}, u32[]{:S(2)}, u32[]{:S(2)}) collective-permute-start(f32[8,128]{1,0:T(8,128)S(1)} %add.3.refs_0_), channel_id=1, source_target_pairs={{0,8},{4,12},{8,0},{12,4},{1,9},{5,13},{9,1},{13,5},{2,10},{6,14},... | collective-permute-start | bytes 12296 | tf_op jit(solution)/shard_map/ppermute | solution.py:600
  33.4 3.9 %collective-permute-start.15 = (f32[8,128]{1,0:T(8,128)S(1)}, f32[8,128]{1,0:T(8,128)S(1)}, u32[]{:S(2)}, u32[]{:S(2)}) collective-permute-start(f32[8,128]{1,0:T(8,128)S(1)} %add.3.refs_0_), channel_id=1, source_target_pairs={{0,4},{4,0},{8,12},{12,8},{1,5},{5,1},{9,13},{13,9},{2,6},{6,2},{1... | collective-permute-start | bytes 12296 | tf_op jit(solution)/shard_map/ppermute | solution.py:600

commit v3 on v2

--- a/solution.py
+++ b/solution.py
@@ -120,60 +120,30 @@
 
 class Geometry:
     def __init__(self, width):
-        last = width - 1
-        self.last = last
-        row, lane = iota((width, LANES), 0), iota((width, LANES), 1)
-        self.top, self.bottom = row == 0, row == last
+        self.last = last = width - 1
+        row, lane = iota((DEEP, LANES), 0), iota((DEEP, LANES), 1)
+        self.band_first = row == 0
         self.left, self.right = lane == 0, lane == last
-        self.half = lane == LANES // 2
-        brow, blane = iota((DEEP, LANES), 0), iota((DEEP, LANES), 1)
-        self.band_first = brow == 0
-        self.band_left, self.band_right = blane == 0, blane == last
+        self.near = lane < LANES // 2
+        self.mirror = jnp.where(lane >= LANES - DEEP, 2 * LANES - 2 * DEEP + last - LANES - lane, lane)
         crow, clane = iota((SIDES * DEEP, LANES), 0), iota((SIDES * DEEP, LANES), 1)
         self.chain_top = crow % DEEP == 0
         self.chain_left = clane % DEEP == 0
         self.even = (clane // DEEP) % 2 == 0
         self.seventh = clane // DEEP == DEEP - 1
-        self.near = iota((1, LANES), 1) < LANES // 2
 
     def chain(self, a, corner):
         return a[corner * DEEP : (corner + 1) * DEEP]
 
-    def main_up(self, a, north):
-        return jnp.where(self.top, north[:1], roll(a, 1, 0))
-
-    def main_down(self, a, south):
-        return jnp.where(self.bottom, south[:1], roll(a, -1, 0))
-
-    def main_west(self, a, ew):
-        return jnp.where(self.left, roll(ew, LANES // 2, 1), roll(a, 1, 1))
-
-    def main_east(self, a, ew):
-        return jnp.where(self.right, roll(ew, -1, 1), roll(a, -1, 1))
-
-    def band_toward(self, a, main_row):
-        return jnp.where(self.band_first, main_row, roll(a, 1, 0))
-
     def band_west(self, a, chain_block):
-        return jnp.where(self.band_left, roll(chain_block, -2 * DEEP, 1), roll(a, 1, 1))
+        return jnp.where(self.left, roll(chain_block, -2 * DEEP, 1), roll(a, 1, 1))
 
     def band_east(self, a, chain_block):
-        return jnp.where(self.band_right, roll(chain_block, self.last - 2 * DEEP, 1), roll(a, -1, 1))
-
-    def ew_toward(self, a, main_east, main_west):
-        inner = jnp.where(self.half, roll(main_west, LANES // 2, 1), roll(a, 1, 1))
-        return jnp.where(self.left, roll(main_east, 1, 1), inner)
-
-    def ew_fill(self, east, west):
-        return jnp.where(self.near, roll(east, 2 * DEEP, 1)[:1], roll(west, 2 * DEEP + LANES // 2, 1)[:1])
-
-    def ew_up(self, a, chain):
-        fill = self.ew_fill(self.chain(chain, NE), self.chain(chain, NW))
-        return jnp.where(self.top, fill, roll(a, 1, 0))
-
-    def ew_down(self, a, chain):
-        fill = self.ew_fill(self.chain(chain, SE), self.chain(chain, SW))
-        return jnp.where(self.bottom, fill, roll(a, -1, 0))
+        return jnp.where(self.right, roll(chain_block, self.last - 2 * DEEP, 1), roll(a, -1, 1))
+
+    def column_fill(self, a, east, west):
+        mirrored = jnp.take_along_axis(self.chain(a, west), self.mirror, axis=1)
+        return jnp.where(self.near, roll(self.chain(a, east), 2 * DEEP, 1), mirrored)[:1]
 
     def chain_up(self, a, fill):
         swapped = jnp.where(self.even, roll(fill, -DEEP, 1), roll(fill, DEEP, 1))
@@ -185,42 +155,35 @@
             swapped = jnp.where(self.seventh, beyond, swapped)
         return jnp.where(self.chain_left, swapped, roll(a, 1, 1))
 
-    def neighbours(self, minus0, plus0, minus1, plus1, beyond=None, main_only=False):
-        n, s, ew, m, c = "n", "s", "ew", "m", "c"
-        out = {
-            m: (
-                self.main_up(plus0[m], minus0[n]),
-                self.main_down(minus0[m], minus0[s]),
-                self.main_west(plus1[m], minus1[ew]),
-                self.main_east(minus1[m], minus1[ew]),
+    def across(self, main, columns):
+        before_m, before_c = roll(main[0], 1, 1), roll(columns[0], 1, 1)
+        after_m, after_c = roll(main[1], -1, 1), roll(columns[1], -1, 1)
+        left, right = self.left, self.right
+        return (
+            (jnp.where(left, before_c, before_m), jnp.where(right, after_c, after_m)),
+            (jnp.where(left, before_m, before_c), jnp.where(right, after_m, after_c)),
+        )
+
+    def neighbours(self, minus0, plus0, minus1, plus1, top, bottom, beyond=None):
+        out = {}
+        for part, row, west, east in (("n", top, NW, NE), ("s", bottom, SW, SE)):
+            out[part] = (
+                jnp.where(self.band_first, row, roll(plus0[part], 1, 0)),
+                roll(minus0[part], -1, 0),
+                self.band_west(plus1[part], self.chain(minus1["c"], west)),
+                self.band_east(minus1[part], self.chain(minus1["c"], east)),
             )
-        }
-        if main_only:
-            return out
-        top, bottom = minus0[m][:1], plus0[m][self.last :]
-        for part, row, west, east in ((n, top, NW, NE), (s, bottom, SW, SE)):
-            out[part] = (
-                self.band_toward(plus0[part], row),
-                roll(minus0[part], -1, 0),
-                self.band_west(plus1[part], self.chain(minus1[c], west)),
-                self.band_east(minus1[part], self.chain(minus1[c], east)),
-            )
-        out[ew] = (
-            self.ew_up(plus0[ew], minus0[c]),
-            self.ew_down(minus0[ew], minus0[c]),
-            self.ew_toward(plus1[ew], plus1[m], minus1[m]),
-            roll(minus1[ew], -1, 1),
-        )
-        out[c] = (
-            self.chain_up(plus0[c], minus0[c]),
-            roll(minus0[c], -1, 0),
-            self.chain_west(plus1[c], minus1[c], beyond),
-            roll(minus1[c], -1, 1),
+        out["c"] = (
+            self.chain_up(plus0["c"], minus0["c"]),
+            roll(minus0["c"], -1, 0),
+            self.chain_west(plus1["c"], minus1["c"], beyond),
+            roll(minus1["c"], -1, 1),
         )
         return out
 
 
-PARTS = ("m", "n", "s", "ew", "c")
+PARTS = ("n", "s", "c")
+EDGE = 8
 
 
 def assemble(count, *refs):
@@ -243,6 +206,7 @@
     lane8 = iota((DEEP, LANES), 1)
     straight, reverse = lane8 % DEEP, last - lane8 % DEEP
     slot_of = lane8 // DEEP
+    far_cell = (lane8 == DEEP * DEEP) & (iota((DEEP, LANES), 0) == 1)
 
     def band(panel, side, field):
         start = pl.multiple_of((side * FIELDS + field) * DEEP, 8)
@@ -273,7 +237,8 @@
             at = (side * FIELDS + field) * DEEP
             parts[at : at + DEEP, :] = values * sign if field == 2 else values
 
-    keys, kinds = [], []
+    keys = []
+    panels = lax.axis_size("tile") * subs
     for corner, (row_side, col_side) in enumerate(CORNERS):
         start = (me, jnp.int32(row_side), jnp.int32(col_side))
         sheets = {0: start}
@@ -282,16 +247,16 @@
             ahead = cross_row(ahead) if k % 2 == 0 else cross_col(ahead)
             behind = cross_col(behind) if k % 2 == 0 else cross_row(behind)
             sheets[k + 1], sheets[-k - 1] = ahead, behind
+        sheets[DEEP] = sheets.pop(DEEP)
         filled = [jnp.zeros((DEEP, LANES), F32)] * FIELDS
         key = jnp.full((1, LANES), -1, jnp.int32)
-        kind = jnp.full((1, LANES), -1, jnp.int32)
         for k, (panel, side, other) in sheets.items():
             end = other & 1
             order = jnp.where(end == 1, reverse, straight)
             sign = jnp.where(end == 1, -1.0, 1.0).astype(F32)
             if k == DEEP:
-                at = CHAIN_AT + (FIELDS * SIDES + corner) * DEEP
-                parts[at : at + DEEP, :] = jnp.take_along_axis(band(panel, side, 0), order, axis=1)
+                values = roll(jnp.take_along_axis(band(panel, side, 0), order, axis=1), 1, 0)
+                filled[0] = jnp.where(far_cell, values, filled[0])
                 continue
             here = slot_of == k % SHEETS
             for field in range(FIELDS):
@@ -299,24 +264,28 @@
                 values = values * sign if field == 2 else values
                 filled[field] = jnp.where(here, values, filled[field])
             if abs(k) <= STEPS:
-                key = jnp.where(here[:1], panel * width + order[:1], key)
-                kind = jnp.where(here[:1], side, kind)
+                key = jnp.where(here[:1], (side * panels + panel) * width + order[:1], key)
         keys.append(key)
-        kinds.append(kind)
         for field in range(FIELDS):
             at = CHAIN_AT + (field * SIDES + corner) * DEEP
             parts[at : at + DEEP, :] = filled[field]
-    labels[...] = jnp.concatenate(keys + kinds, axis=0).astype(F32)
+    lane = lane8[:1]
+    sides = []
+    for side in range(SIDES):
+        panel, other, flipped = lookup(me, side)
+        sides.append(jnp.where(lane == 0, panel, jnp.where(lane == 1, other, flipped)))
+    labels[...] = jnp.concatenate(keys + sides, axis=0).astype(F32)
 
 
 def gains(levels, slots, count, *refs):
-    pair, flip, labels = refs[:3]
-    records = refs[3 : 3 + count]
-    g_main, g_band, g_ew, g_chain, obs, square = refs[3 + count :]
+    labels = refs[0]
+    records = refs[1 : 1 + count]
+    g_main, g_band, g_ew, g_chain, obs, square = refs[1 + count :]
     width = LANES
     last = width - 1
     subs = lax.axis_size("sub")
     me = lax.axis_index("tile") * subs + lax.axis_index("sub")
+    panels = lax.axis_size("tile") * subs
     pairs = level_pairs(levels)
     depth_rows = record_rows(levels)
     fold = LANES // slots
@@ -340,8 +309,8 @@
     comps = STEPS * len(pairs)
     partners = []
     for side in range(SIDES):
-        other = pair[side, me]
-        partners.append((lax.shift_right_logical(other, 2), other & 3, flip[side, me]))
+        row = labels[SIDES + side : SIDES + side + 1, :].astype(jnp.int32)
+        partners.append((row[:, 0:1], row[:, 1:2], row[:, 2:3]))
 
     def hits(mask):
         return jnp.where(mask, 1.0, 0.0).astype(BF16)
@@ -353,40 +322,20 @@
         oj = data[2:3].astype(jnp.int32)
         when = data[3:4].astype(jnp.int32)
         tall = iota((width, span), 0)
-        short = iota((DEEP, span), 0)
-        at_row = jnp.where(tall == oi, 1.0, 0.0)
-        at_row_here = jnp.where(panel == me, at_row, 0.0)
-        at_col = jnp.where(tall == oj, 1.0, 0.0)
-        at_row_b, at_col_b = at_row.astype(BF16), at_col.astype(BF16)
+        at_row = jnp.where((tall == oi) & (panel == me), 1.0, 0.0)
+        half = iota((DEEP, span), 0)
+        first_half = half < STEPS
+        shallow = half % STEPS
         distance = (oi, last - oi, oj, last - oj)
-        band_hit, band_place = [], []
-        for q, r, f in partners:
-            depth = jnp.where(r == 0, distance[0], jnp.where(r == 1, distance[1], jnp.where(r == 2, distance[2], distance[3])))
-            along = jnp.where(r < 2, oj, oi)
-            along = jnp.where(f == 1, last - along, along)
-            band_hit.append(jnp.where(panel == q, jnp.where(short == depth, 1.0, 0.0), 0.0))
-            band_place.append(hits(tall == along))
-        spot = (panel * width + oj, panel * width + oi)
-        chain_hit = [jnp.where(short == distance[side], 1.0, 0.0) for side in range(SIDES)]
-        chain_place = []
-        for corner in range(4):
-            key = label_tall[:, corner : corner + 1].astype(jnp.int32)
-            kind = label_tall[:, 4 + corner : 5 + corner].astype(jnp.int32)
-            chain_place.append(
-                [hits((key == spot[side // 2]) & (kind == side)) for side in range(SIDES)]
-            )
-        gs = []
-        for t in range(STEPS):
-            for index in range(len(pairs)):
-                g = jnp.where(when == t + 1, data[4 + index : 5 + index], 0.0)
-                high = g.astype(BF16).astype(F32)
-                gs.append((high, g - high))
+        pieces = []
+        for index in range(len(pairs)):
+            g = data[4 + index : 5 + index]
+            high = g.astype(BF16).astype(F32)
+            pieces.append((high, g - high))
+        stacks = [jnp.where(first_half, high, low) for high, low in pieces]
 
         def product(left, right):
             return lax.dot_general(left, right, NT, preferred_element_type=F32)
-
-        def tall_rows(hit):
-            return jnp.concatenate([hit * part for g in gs for part in g], axis=0).astype(BF16)
 
         def put(ref, at, value):
             if chunks == 1:
@@ -394,32 +343,58 @@
             else:
                 ref[at] = ref[at] + value
 
-        for comp in range(comps):
-            high, low = gs[comp]
-            value = product((at_row_here * high).astype(BF16), at_col_b)
-            value = value + product((at_row_here * low).astype(BF16), at_col_b)
-            put(g_main, comp, value)
-        for side in range(SIDES):
-            value = product(tall_rows(band_hit[side]), band_place[side])
+        at_times = jnp.concatenate([hits((tall == oj) & (when == t + 1)) for t in range(STEPS)], axis=0)
+        for index, (high, low) in enumerate(pieces):
+            value = product((at_row * high).astype(BF16), at_times) + product((at_row * low).astype(BF16), at_times)
+            for t in range(STEPS):
+                put(g_main, t * len(pairs) + index, value[:, t * LANES : (t + 1) * LANES])
+
+        def rows_of(depth):
+            hit = jnp.where(shallow == depth, 1.0, 0.0)
+            return jnp.concatenate(
+                [jnp.where(when == t + 1, hit, 0.0) * stack for t in range(STEPS) for stack in stacks], axis=0
+            ).astype(BF16)
+
+        def joined(value, comp):
+            part = value[comp * DEEP : (comp + 1) * DEEP]
+            return part + roll(part, STEPS, 0)
+
+        for side, (q, r, f) in enumerate(partners):
+            depth = jnp.where(
+                r == 0, distance[0], jnp.where(r == 1, distance[1], jnp.where(r == 2, distance[2], distance[3]))
+            )
+            along = jnp.where(r < 2, oj, oi)
+            along = jnp.where(f == 1, last - along, along)
+            value = product(rows_of(jnp.where(panel == q, depth, -1)), hits(tall == along))
             for comp in range(comps):
-                at = 2 * comp * DEEP
-                total = value[at : at + DEEP] + value[at + DEEP : at + 2 * DEEP]
                 if side < 2:
-                    put(g_band, (side, comp), total)
+                    put(g_band, (side, comp), joined(value, comp))
                 else:
-                    put(square, (side - 2, comp), total)
-        lefts = [tall_rows(chain_hit[side]) for side in range(SIDES)]
-        for corner in range(4):
-            value = product(lefts[0], chain_place[corner][0])
-            for side in range(1, SIDES):
-                value = value + product(lefts[side], chain_place[corner][side])
+                    put(square, (side - 2, comp), joined(value, comp))
+        lefts = jnp.concatenate([rows_of(distance[side]) for side in range(SIDES)], axis=1)
+        area = panels * width
+        spots = [
+            jnp.where(panel < 0, -2, panel * width + (oj if side < 2 else oi) + side * area) for side in range(SIDES)
+        ]
+        keys = [label_tall[:, corner : corner + 1].astype(jnp.int32) for corner in range(4)]
+        for duo in range(2):
+            places = jnp.concatenate(
+                [
+                    jnp.concatenate([hits(keys[corner] == spot) for spot in spots], axis=1)
+                    for corner in (2 * duo, 2 * duo + 1)
+                ],
+                axis=0,
+            )
+            value = product(lefts, places)
             for comp in range(comps):
-                at = 2 * comp * DEEP
-                put(
-                    g_chain,
-                    (comp, slice(corner * DEEP, (corner + 1) * DEEP)),
-                    value[at : at + DEEP] + value[at + DEEP : at + 2 * DEEP],
-                )
+                total = joined(value, comp)
+                for half_index in range(2):
+                    corner = 2 * duo + half_index
+                    put(
+                        g_chain,
+                        (comp, slice(corner * DEEP, (corner + 1) * DEEP)),
+                        total[:, half_index * LANES : (half_index + 1) * LANES],
+                    )
         return 0
 
     if chunks == 1:
@@ -430,82 +405,149 @@
         g_chain[...] = jnp.zeros(g_chain.shape, F32)
         square[...] = jnp.zeros(square.shape, F32)
         lax.fori_loop(0, chunks, accumulate, 0)
-    for comp in range(comps):
-        g_ew[comp] = side_by_side(square[1, comp], square[0, comp])
-
-
-def side_by_side(east, west):
-    gap = jnp.zeros((LANES // 2 - DEEP, LANES), F32)
-    return jnp.concatenate([east, gap, west, gap], axis=0).T
+    for start in range(0, comps, DEEP):
+        columns = as_columns([(square[1, comp], square[0, comp]) for comp in range(start, min(comps, start + DEEP))])
+        for index, value in enumerate(columns):
+            g_ew[start + index] = value
+
+
+def as_columns(duos):
+    groups = [jnp.zeros((DEEP, LANES), F32)] * SHEETS
+    for index, (east, west) in enumerate(duos):
+        groups[2 * index] = east
+        groups[(2 * index - 1) % SHEETS] = jnp.concatenate([west[d : d + 1] for d in reversed(range(DEEP))], axis=0)
+    columns = jnp.concatenate(groups, axis=0).T
+    return [columns if index == 0 else roll(columns, -2 * DEEP * index, 1) for index in range(len(duos))]
 
 
 def evolve(levels, *refs):
     scalars, refs = refs[0], refs[1:]
-    diffusion, vertical, prior = (
+    mix, blend, prior = (
         [scalars[index * levels + level : index * levels + level + 1, :] for level in range(levels)] for index in range(3)
     )
     parts, refs = refs[:levels], refs[levels:]
     fields, refs = refs[:levels], refs[levels:]
     g_main, g_band, g_ew, g_chain = refs[:4]
-    image_out, sums_out, x_main, w_main, images, x_band, w_band, x_ew, w_ew, x_chain, w_chain, x_far = refs[4:]
+    image_out, sums_out, x_main, x_ew, w_main, w_ew, f_main, f_ew, images, x_band, w_band, x_chain, w_chain, x_far = refs[4:]
     width = LANES
     pairs = level_pairs(levels)
+    inner = slice(EDGE, EDGE + width)
+    above, below = slice(EDGE - 1, EDGE), slice(EDGE + width, EDGE + width + 1)
+    geometry = Geometry(width)
     for k in range(levels):
         level = rotated(levels, k)
-        x_main[level] = fields[k][0]
-        w_main[level, 0] = fields[k][1]
-        w_main[level, 1] = fields[k][2]
+        x_main[0, level, inner] = fields[k][0]
+        w_main[level, 0, inner] = fields[k][1]
+        w_main[level, 1, inner] = fields[k][2]
         part = parts[k]
         piece = lambda side, field: part[(side * FIELDS + field) * DEEP : (side * FIELDS + field + 1) * DEEP, :]
         for index in range(2):
             x_band[level, index] = piece(index, 0)
             w_band[level, index, 0] = piece(index, 1)
             w_band[level, index, 1] = piece(index, 2)
-        x_ew[level] = side_by_side(piece(3, 0), piece(2, 0))
-        w_ew[level, 0] = side_by_side(piece(3, 2), piece(2, 2))
-        w_ew[level, 1] = side_by_side(piece(3, 1), piece(2, 1))
+        columns = as_columns(
+            [(piece(3, 0), piece(2, 0)), (piece(3, 2), piece(2, 2)), (piece(3, 1), -piece(2, 1))]
+        )
+        x_ew[0, level, inner], w_ew[level, 0, inner], w_ew[level, 1, inner] = columns
         chain = lambda field: part[CHAIN_AT + field * SIDES * DEEP : CHAIN_AT + (field + 1) * SIDES * DEEP, :]
         x_chain[level] = chain(0)
         w_chain[level, 0] = chain(1)
         w_chain[level, 1] = chain(2)
-        x_far[level] = chain(3)
-
-    geometry = Geometry(width)
-    mix = [diffusion[level] for level in range(levels)]
-    blend = [vertical[level] for level in range(levels)]
+        x_far[level] = roll(roll(chain(0), -1, 0), -DEEP, 1)
+        w_main[level, 0, above] = -piece(0, 1)[:1]
+        w_main[level, 0, below] = piece(1, 1)[:1]
+        w_ew[level, 0, above] = -geometry.column_fill(chain(1), NE, NW)
+        w_ew[level, 0, below] = geometry.column_fill(chain(1), SE, SW)
+
     center = [1.0 - 4.0 * mix[level] - 2.0 * blend[level] for level in range(levels)]
 
     def wind(level, axis, part):
-        if part == "m":
-            return w_main[level, axis]
-        if part == "n":
-            return w_band[level, 0, axis]
-        if part == "s":
-            return w_band[level, 1, axis]
-        return (w_ew if part == "ew" else w_chain)[level, axis]
-
-    def forward(states, beyond):
+        if part == "c":
+            return w_chain[level, axis]
+        return w_band[level, 0 if part == "n" else 1, axis]
+
+    def gain(t, low, high, part):
+        comp = t * len(pairs) + pairs.index((min(low, high), max(low, high)))
+        if part == "c":
+            return g_chain[comp]
+        return g_band[0 if part == "n" else 1, comp]
+
+    def beside(level):
+        return [k for k in (level - 1, level + 1) if 0 <= k < levels]
+
+    def added(terms):
+        total = terms[0]
+        for term in terms[1:]:
+            total = total + term
+        return total
+
+    def edges(now, states):
+        for level in range(levels):
+            state = states[level]
+            x_main[now, level, above] = state["n"][:1]
+            x_main[now, level, below] = state["s"][:1]
+            x_ew[now, level, above] = geometry.column_fill(state["c"], NE, NW)
+            x_ew[now, level, below] = geometry.column_fill(state["c"], SE, SW)
+
+    def forward(t, states):
+        now, then = t % 2, (t + 1) % 2
+        edges(now, states)
         out = []
         for level in range(levels):
             x = states[level]
-            near = geometry.neighbours(x, x, x, x, None if beyond is None else beyond[level])
+            top, bottom = x_main[now, level, EDGE : EDGE + 1], x_main[now, level, EDGE + width - 1 : EDGE + width]
+            near = geometry.neighbours(x, x, x, x, top, bottom, x_far[level] if t == 0 else None)
             result = {}
             for part in PARTS:
                 up, down, west, east = near[part]
-                p, q = wind(level, 0, part), wind(level, 1, part)
                 value = center[level] * x[part] + mix[level] * ((up + down) + (west + east))
-                value = value + p * (up - down) + q * (west - east)
-                others = [states[k][part] for k in (level - 1, level + 1) if 0 <= k < levels]
-                if others:
-                    value = value + blend[level] * sum(others[1:], others[0])
+                value = value + wind(level, 0, part) * (up - down) + wind(level, 1, part) * (west - east)
+                for k in beside(level):
+                    value = value + blend[level] * states[k][part]
                 result[part] = value
             out.append(result)
-        return out
-
-    def adjoint(states, main_only):
+        for start in range(EDGE, EDGE + width, 8):
+            at, before, after = slice(start, start + 8), slice(start - 1, start + 7), slice(start + 1, start + 9)
+            mains = [x_main[now, level, at] for level in range(levels)]
+            columns = [x_ew[now, level, at] for level in range(levels)]
+            fresh = ([], [])
+            for level in range(levels):
+                lanes = geometry.across((mains[level],) * 2, (columns[level],) * 2)
+                for which, (x, w, own) in enumerate(((x_main, w_main, mains), (x_ew, w_ew, columns))):
+                    up, down = x[now, level, before], x[now, level, after]
+                    west, east = lanes[which]
+                    value = center[level] * own[level] + mix[level] * ((up + down) + (west + east))
+                    value = value + w[level, 0, at] * (up - down) + w[level, 1, at] * (west - east)
+                    if beside(level):
+                        value = value + blend[level] * added([own[k] for k in beside(level)])
+                    fresh[which].append(value)
+            rows = slice(start - EDGE, start - EDGE + 8)
+            for which, (x, g, f) in enumerate(((x_main, g_main, f_main), (x_ew, g_ew, f_ew))):
+                for level in range(levels):
+                    if t < STEPS - 1:
+                        x[then, level, at] = fresh[which][level]
+                    terms = []
+                    for other in range(levels):
+                        comp = t * len(pairs) + pairs.index((min(level, other), max(level, other)))
+                        terms.append(g[comp, rows] * fresh[which][other])
+                    if t < STEPS - 1:
+                        f[t, level, rows] = added(terms)
+                    else:
+                        x[then, level, at] = added(terms)
+        forces = [
+            {
+                part: added([gain(t, level, other, part) * out[other][part] for other in range(levels)])
+                for part in PARTS
+            }
+            for level in range(levels)
+        ]
+        return out, forces
+
+    def adjoint(t, states, forces):
+        now, then = (t + 1) % 2, t % 2
+        edges(now, states)
         out = []
-        parts = ("m",) if main_only else PARTS
-        for level in range(levels):
+        for level in range(levels if forces is not None else 0):
             w = states[level]
             minus0, plus0, minus1, plus1 = {}, {}, {}, {}
             for part in PARTS:
@@ -513,62 +555,62 @@
                 p, q = wind(level, 0, part) * w[part], wind(level, 1, part) * w[part]
                 minus0[part], plus0[part] = scaled + p, scaled - p
                 minus1[part], plus1[part] = scaled + q, scaled - q
-            near = geometry.neighbours(minus0, plus0, minus1, plus1, None, main_only)
+            first, final = slice(EDGE, EDGE + 1), slice(EDGE + width - 1, EDGE + width)
+            top = (mix[level] + w_main[level, 0, first]) * x_main[now, level, first]
+            bottom = (mix[level] - w_main[level, 0, final]) * x_main[now, level, final]
+            near = geometry.neighbours(minus0, plus0, minus1, plus1, top, bottom)
             result = {}
-            for part in parts:
+            for part in PARTS:
                 up, down, west, east = near[part]
-                value = center[level] * w[part] + ((up + down) + (west + east))
-                for k in (level - 1, level + 1):
-                    if 0 <= k < levels:
-                        value = value + blend[k] * states[k][part]
+                value = center[level] * w[part] + ((up + down) + (west + east)) + forces[level][part]
+                for k in beside(level):
+                    value = value + blend[k] * states[k][part]
                 result[part] = value
             out.append(result)
+        for start in range(EDGE, EDGE + width, 8):
+            at, before, after = slice(start, start + 8), slice(start - 1, start + 7), slice(start + 1, start + 9)
+            rows = slice(start - EDGE, start - EDGE + 8)
+            mains = [x_main[now, level, at] for level in range(levels)]
+            columns = [x_ew[now, level, at] for level in range(levels)]
+            for level in range(levels):
+                given = []
+                for w, own in ((w_main, mains), (w_ew, columns)):
+                    scaled, turned = mix[level] * own[level], w[level, 1, at] * own[level]
+                    given.append((scaled - turned, scaled + turned))
+                lanes = geometry.across(*given)
+                for which, (x, w, own, f) in enumerate(
+                    ((x_main, w_main, mains, f_main), (x_ew, w_ew, columns, f_ew))
+                ):
+                    if which and forces is None:
+                        continue
+                    up = (mix[level] - w[level, 0, before]) * x[now, level, before]
+                    down = (mix[level] + w[level, 0, after]) * x[now, level, after]
+                    west, east = lanes[which]
+                    value = center[level] * own[level] + ((up + down) + (west + east))
+                    for k in beside(level):
+                        value = value + blend[k] * own[k]
+                    if forces is None:
+                        images[level, rows] = value + prior[level] * x_start[level][rows]
+                    else:
+                        x[then, level, at] = value + f[t - 1, level, rows]
         return out
 
-    def gain(t, index, part):
-        comp = t * len(pairs) + index
-        if part == "m":
-            return g_main[comp]
-        if part == "n":
-            return g_band[0, comp]
-        if part == "s":
-            return g_band[1, comp]
-        return (g_ew if part == "ew" else g_chain)[comp]
-
-    def force(t, states):
-        out = []
-        for level in range(levels):
-            result = {}
-            for part in PARTS:
-                value = None
-                for other in range(levels):
-                    index = pairs.index((min(level, other), max(level, other)))
-                    term = gain(t, index, part) * states[other][part]
-                    value = term if value is None else value + term
-                result[part] = value
-            out.append(result)
-        return out
-
-    states = [
-        {"m": x_main[k], "n": x_band[k, 0], "s": x_band[k, 1], "ew": x_ew[k], "c": x_chain[k]} for k in range(levels)
-    ]
+    x_start = [f_main.at[STEPS - 1, level] for level in range(levels)]
+    for level in range(levels):
+        x_start[level][...] = x_main[0, level, inner]
+    states = [{"n": x_band[k, 0], "s": x_band[k, 1], "c": x_chain[k]} for k in range(levels)]
     forcing = []
-    for step in range(STEPS):
-        states = forward(states, [x_far[k] for k in range(levels)] if step == 0 else None)
-        forcing.append(force(step, states))
+    for t in range(STEPS):
+        states, forces = forward(t, states)
+        forcing.append(forces)
     current = forcing[STEPS - 1]
-    for step in range(STEPS - 1, 0, -1):
-        current = adjoint(current, False)
-        current = [{part: current[k][part] + forcing[step - 1][k][part] for part in PARTS} for k in range(levels)]
-    current = adjoint(current, True)
+    for t in range(STEPS - 1, -1, -1):
+        current = adjoint(t, current, forcing[t - 1] if t else None)
 
     zero = jnp.zeros((1, LANES), F32)
     totals = [zero] * 4
     for k in range(levels):
-        images[k] = prior[k] * x_main[k] + current[k]["m"]
-    for k in range(levels):
-        level = rotated(levels, k)
-        image = images[level]
+        image = images[rotated(levels, k)]
         residual, direction = fields[k][3], fields[k][0]
         if k == 0:
             image_out[...] = image
@@ -693,7 +735,7 @@
     vmem = lambda *dims: pltpu.VMEM(dims, F32)
     parts, labels = pl.pallas_call(
         functools.partial(assemble, len(messages)),
-        out_shape=(vmem(CHAIN_AT + 4 * SIDES * DEEP, LANES), vmem(8, LANES)),
+        out_shape=(vmem(CHAIN_AT + FIELDS * SIDES * DEEP, LANES), vmem(8, LANES)),
         in_specs=[SCALAR] * 2 + [WHOLE] * len(messages),
         out_specs=(WHOLE, WHOLE),
         scratch_shapes=[vmem(panels, BAND, LANES)],
@@ -705,15 +747,16 @@
     span = min(CHUNK, panels * slots)
     comps = STEPS * len(level_pairs(levels))
     chain = (SIDES * DEEP, LANES)
+    padded = (width + 2 * EDGE, LANES)
     products = pl.pallas_call(
         functools.partial(gains, levels, slots, len(records)),
         out_shape=(vmem(comps, *shape), vmem(2, comps, DEEP, LANES), vmem(comps, *shape), vmem(comps, *chain)),
-        in_specs=[SCALAR] * 2 + [WHOLE] * (1 + len(records)),
+        in_specs=[WHOLE] * (1 + len(records)),
         out_specs=(WHOLE,) * 4,
         scratch_shapes=[vmem(panels * slots // span, depth_rows, span), vmem(2, comps, DEEP, LANES)],
         compiler_params=limit(16),
         name="gains",
-    )(pair, flip, *[near(a) for a in (labels, *records)])
+    )(*[near(a) for a in (labels, *records)])
 
     image, sums = pl.pallas_call(
         functools.partial(evolve, levels),
@@ -721,13 +764,15 @@
         in_specs=[WHOLE] * (2 * levels + 5),
         out_specs=(WHOLE, WHOLE),
         scratch_shapes=[
-            vmem(levels, *shape),
-            vmem(levels, 2, *shape),
+            vmem(2, levels, *padded),
+            vmem(2, levels, *padded),
+            vmem(levels, 2, *padded),
+            vmem(levels, 2, *padded),
+            vmem(STEPS, levels, *shape),
+            vmem(STEPS, levels, *shape),
             vmem(levels, *shape),
             vmem(levels, 2, DEEP, LANES),
             vmem(levels, 2, 2, DEEP, LANES),
-            vmem(levels, *shape),
-            vmem(levels, 2, *shape),
             vmem(levels, *chain),
             vmem(levels, 2, *chain),
             vmem(levels, *chain),

time: 38.3 us -> 37.2 us (0.971)
  Pallas kernels: 9.27 us -> 8.15 us
    pallas_call x1, Pallas kernels: 2.79 us -> 2.1 us  [body(): pl.pallas_call(functools.partial(gains, levels, slots, len(records)), out...]
    pallas_call x1, Pallas kernels: 2.73 us -> 2.29 us  [body(): pl.pallas_call(functools.partial(evolve, levels), out_shape=(vmem(*shape)...]
  transfers between devices with their start and end apart: 18 -> 18, of which waited for: 6 -> 6; matrix products, arithmetic and copies ran while one was open for 0% -> 0% of each run, Pallas kernels for 12% -> 11%
where the time goes in v3:
time: 37.2 us; the launch traced here: 37 us
  starting transfers between devices  19 us (51%)
  waiting for transfers between devices  8.39 us (23%)
  Pallas kernels  8.15 us (22%)
  between operations  1.41 us (4%)
    ppermute x15, starting transfers between devices, exchanged(): return lax.ppermute(value, axis, [(i, i ^ mask) for i in range(count)])  14.3 us
    ppermute x15, waiting for transfers between devices, exchanged(): return lax.ppermute(value, axis, [(i, i ^ mask) for i in range(count)])  8.38 us
    ppermute x3, starting transfers between devices, level_parts(): lax.ppermute(value, 'lev', [(i, (i + k) % count) for i in range(count)])  4.67 us
    pallas_call x1, Pallas kernels, body(): pl.pallas_call(functools.partial(evolve, levels), out_shape=(vmem(*shape)...  2.29 us
    pallas_call x1, Pallas kernels, body(): pl.pallas_call(functools.partial(gains, levels, slots, len(records)), out...  2.1 us
    pallas_call x1, Pallas kernels, body(): pl.pallas_call(functools.partial(assemble, len(messages)), out_shape=(vme...  1.2 us
    pallas_call x1, Pallas kernels, body(): pl.pallas_call(functools.partial(prepare, width.bit_length() - 1), out_sh...  1.17 us
    pallas_call x1, Pallas kernels, body(): pl.pallas_call(update, out_shape=(jax.ShapeDtypeStruct(shape, F32),) * 3,...  0.8 us
  transfers between devices with their start and end apart: 18, of which 6 were waited for; matrix products, arithmetic and copies ran while one was open for 0% of the time, Pallas kernels for 11%

profile of v3, /device:TPU:0, one launch (start us, length us, event | category | flops | bytes accessed | tf_op | source)
XLA Modules:
  0.0 37.0 jit_solution(10388123469620651422)
XLA Ops:
  1.3 1.2 %prepare.1 = (f32[96,128]{1,0:T(8,128)S(1)}, f32[4,128,128]{2,1,0:T(8,128)S(1)}, f32[64,616]{1,0:T(8,128)S(1)}, f32[8,128]{1,0:T(8,128)S(1)}, f32[1,616]{1,0:T(1,128)S(1)}, /*index=5*/f32[8,128]{1,0:T(8,128)S(1)}) custom-call(s32[1]{0:T(128)S(6)} %copy.18.count, f32[2]{0:T(128)} %diffusion.1, f32[2]{0:T(128)} %vertical.1, f32[2]{0:T(128)} %prior.1, ...), custom_call_target="tpu_custom_call" | custom-call | tf_op jit(solution)/shard_map/prepare/pallas_call | solution.py:692
  2.5 3.0 %collective-permute-start.9 = (f32[64,616]{1,0:T(8,128)S(1)}, f32[64,616]{1,0:T(8,128)S(1)}, u32[]{:S(2)}, u32[]{:S(2)}) collective-permute-start(f32[64,616]{1,0:T(8,128)S(1)} %get-tuple-element.25.refs_0_), channel_id=1, source_target_pairs={{0,2},{2,0},{1,3},{3,1},{4,6},{6,4},{5,7},{7,5},{8,10},{10,8},{9,1... | collective-permute-start | bytes 473096 | tf_op jit(solution)/shard_map/ppermute | solution.py:662
  5.5 0.1 collective-permute-start.8
  5.6 4.1 %collective-permute-start.5 = (f32[96,128]{1,0:T(8,128)S(1)}, f32[96,128]{1,0:T(8,128)S(1)}, u32[]{:S(2)}, u32[]{:S(2)}) collective-permute-start(f32[96,128]{1,0:T(8,128)S(1)} %get-tuple-element.21.refs_2_), channel_id=1, source_target_pairs={{0,12},{4,8},{8,4},{12,0},{1,13},{5,9},{9,5},{13,1},{2,14},{6,10},... | collective-permute-start | bytes 147464 | tf_op jit(solution)/shard_map/ppermute | solution.py:642
  9.6 0.0 collective-permute-start.3
  9.6 0.6 %collective-permute-start.1 = (f32[96,128]{1,0:T(8,128)S(1)}, f32[96,128]{1,0:T(8,128)S(1)}, u32[]{:S(2)}, u32[]{:S(2)}) collective-permute-start(f32[96,128]{1,0:T(8,128)S(1)} %get-tuple-element.21.refs_2_), channel_id=1, source_target_pairs={{0,4},{4,0},{8,12},{12,8},{1,5},{5,1},{9,13},{13,9},{2,6},{6,2},{1... | collective-permute-start | bytes 147464 | tf_op jit(solution)/shard_map/ppermute | solution.py:642
  10.2 2.1 %collective-permute-done.5.refs_8_ = f32[96,128]{1,0:T(8,128)S(1)} collective-permute-done((f32[96,128]{1,0:T(8,128)S(1)}, f32[96,128]{1,0:T(8,128)S(1)}, u32[]{:S(2)}, u32[]{:S(2)}) %collective-permute-start.5) | collective-permute-done | bytes 49184 | tf_op jit(solution)/shard_map/ppermute | solution.py:642
  12.3 0.0 collective-permute-start
  12.3 2.3 %collective-permute-done.3.refs_6_ = f32[96,128]{1,0:T(8,128)S(1)} collective-permute-done((f32[96,128]{1,0:T(8,128)S(1)}, f32[96,128]{1,0:T(8,128)S(1)}, u32[]{:S(2)}, u32[]{:S(2)}) %collective-permute-start.3) | collective-permute-done | bytes 49184 | tf_op jit(solution)/shard_map/ppermute | solution.py:642
  14.6 0.0 collective-permute-start.6
  14.6 0.0 collective-permute-done.1.refs_4_
  14.6 0.5 %collective-permute-start.4 = (f32[96,128]{1,0:T(8,128)S(1)}, f32[96,128]{1,0:T(8,128)S(1)}, u32[]{:S(2)}, u32[]{:S(2)}) collective-permute-start(f32[96,128]{1,0:T(8,128)S(1)} %collective-permute-done.3.refs_6_), channel_id=1, source_target_pairs={{0,1},{1,0},{2,3},{3,2},{4,5},{5,4},{6,7},{7,6},{8,9},{9,8},{10,11... | collective-permute-start | bytes 147464 | tf_op jit(solution)/shard_map/ppermute | solution.py:642
  15.1 0.0 collective-permute-done.9.refs_1_
  15.1 0.1 collective-permute-start.2
  15.2 0.6 %compose.1 = f32[8,128]{1,0:T(8,128)S(1)} custom-call(f32[64,616]{1,0:T(8,128)S(1)} %get-tuple-element.25.refs_0_, f32[64,616]{1,0:T(8,128)S(1)} %collective-permute-done.9.refs_1_, f32[1,616]{1,0:T(1,128)S(1)} %get-tuple-element.26.refs_2_, f32[8,128]{1,0:T(8,128)S(1)} %get-tuple-element.27.refs_3_), custom_call_target="tpu_custom_call" | custom-call | tf_op jit(solution)/shard_map/compose/pallas_call | solution.py:723
  15.8 0.0 collective-permute-done.refs_3_
  15.8 1.7 %collective-permute-start.12 = (f32[8,128]{1,0:T(8,128)S(1)}, f32[8,128]{1,0:T(8,128)S(1)}, u32[]{:S(2)}, u32[]{:S(2)}) collective-permute-start(f32[8,128]{1,0:T(8,128)S(1)} %compose.1), channel_id=1, source_target_pairs={{0,12},{4,8},{8,4},{12,0},{1,13},{5,9},{9,5},{13,1},{2,14},{6,10},... | collective-permute-start | bytes 12296 | tf_op jit(solution)/shard_map/ppermute | solution.py:642
  17.5 0.0 collective-permute-done.6.refs_9_
  17.5 0.4 %collective-permute-start.11 = (f32[8,128]{1,0:T(8,128)S(1)}, f32[8,128]{1,0:T(8,128)S(1)}, u32[]{:S(2)}, u32[]{:S(2)}) collective-permute-start(f32[8,128]{1,0:T(8,128)S(1)} %compose.1), channel_id=1, source_target_pairs={{0,8},{4,12},{8,0},{12,4},{1,9},{5,13},{9,1},{13,5},{2,10},{6,14},... | collective-permute-start | bytes 12296 | tf_op jit(solution)/shard_map/ppermute | solution.py:642
  17.9 0.0 collective-permute-done.4.refs_7_
  17.9 2.4 %collective-permute-start.10 = (f32[8,128]{1,0:T(8,128)S(1)}, f32[8,128]{1,0:T(8,128)S(1)}, u32[]{:S(2)}, u32[]{:S(2)}) collective-permute-start(f32[8,128]{1,0:T(8,128)S(1)} %compose.1), channel_id=1, source_target_pairs={{0,4},{4,0},{8,12},{12,8},{1,5},{5,1},{9,13},{13,9},{2,6},{6,2},{1... | collective-permute-start | bytes 12296 | tf_op jit(solution)/shard_map/ppermute | solution.py:642
  20.3 0.0 collective-permute-done.2.refs_5_
  20.3 0.0 copy-done.4
  20.3 0.0 copy-done.3
  20.3 1.2 %assemble.1 = (f32[192,128]{1,0:T(8,128)S(1)}, f32[8,128]{1,0:T(8,128)S(1)}) custom-call(s32[4,8]{1,0:T(4,128)S(1)} %bitcast.18, s32[4,8]{1,0:T(4,128)S(1)} %bitcast.19, f32[96,128]{1,0:T(8,128)S(1)} %get-tuple-element.21.refs_2_, f32[96,128]{1,0:T(8,128)S(1)} %collective-permute-done.refs_3_, f32[96,128]{1,0:T(8,128)S(1)} %collective-permute-done.1.refs_4_, ...), custom_call_target="tpu_custom_call" | custom-call | tf_op jit(solution)/shard_map/assemble/pallas_call | solution.py:736
  21.5 1.6 %collective-permute-start.7 = (f32[192,128]{1,0:T(8,128)S(1)}, f32[192,128]{1,0:T(8,128)S(1)}, u32[]{:S(2)}, u32[]{:S(2)}) collective-permute-start(f32[192,128]{1,0:T(8,128)S(1)} %get-tuple-element.22.refs_1_), channel_id=1, source_target_pairs={{0,2},{2,0},{1,3},{3,1},{4,6},{6,4},{5,7},{7,5},{8,10},{10,8},{9,1... | collective-permute-start | bytes 294920 | tf_op jit(solution)/shard_map/ppermute | solution.py:662
  23.1 0.0 collective-permute-done.12
  23.1 0.0 collective-permute-done.11
  23.1 0.0 collective-permute-done.10
  23.1 0.1 collective-permute-start.13
  23.2 1.2 %collective-permute-done.13.refs_2_ = f32[32,128]{1,0:T(8,128)S(1)} collective-permute-done((f32[32,128]{1,0:T(8,128)S(1)}, f32[32,128]{1,0:T(8,128)S(1)}, u32[]{:S(2)}, u32[]{:S(2)}) %collective-permute-start.13) | collective-permute-done | bytes 16416 | tf_op jit(solution)/shard_map/ppermute | solution.py:642
  24.3 2.1 %gains.1 = (f32[12,128,128]{2,1,0:T(8,128)S(1)}, f32[2,12,8,128]{3,2,1,0:T(8,128)S(1)}, f32[12,128,128]{2,1,0:T(8,128)S(1)}, f32[12,32,128]{2,1,0:T(8,128)S(1)}) custom-call(f32[8,128]{1,0:T(8,128)S(1)} %get-tuple-element.24.refs_0_, f32[32,128]{1,0:T(8,128)S(1)} %pad_maximum_fusion.refs_1_, f32[32,128]{1,0:T(8,128)S(1)} %collective-permute-done.13.refs_2_), custom_call_target="tpu_custom_call" | custom-call | tf_op jit(solution)/shard_map/gains/pallas_call | solution.py:751
  26.5 0.0 collective-permute-done.7.refs_2_
  26.5 0.0 collective-permute-done.8.refs_4_
  26.5 0.0 copy-start
  26.5 0.0 copy-start.1
  26.5 0.0 copy-start.2
  26.5 2.3 %evolve.1 = (f32[128,128]{1,0:T(8,128)S(1)}, f32[8,128]{1,0:T(8,128)S(1)}) custom-call(f32[8,128]{1,0:T(8,128)S(1)} %get-tuple-element.20.refs_0_, f32[192,128]{1,0:T(8,128)S(1)} %get-tuple-element.22.refs_1_, f32[192,128]{1,0:T(8,128)S(1)} %collective-permute-done.7.refs_2_, f32[4,128,128]{2,1,0:T(8,128)S(1)} %get-tuple-element.23.refs_3_, ...), custom_call_target="tpu_custom_call" | custom-call | tf_op jit(solution)/shard_map/evolve/pallas_call | solution.py:761
  28.8 0.2 collective-permute-start.14
  29.0 1.0 %collective-permute-done.14 = f32[8,128]{1,0:T(8,128)S(1)} collective-permute-done((f32[8,128]{1,0:T(8,128)S(1)}, f32[8,128]{1,0:T(8,128)S(1)}, u32[]{:S(2)}, u32[]{:S(2)}) %collective-permute-start.14) | collective-permute-done | bytes 4128 | tf_op jit(solution)/shard_map/ppermute | solution.py:642
  30.0 1.6 %collective-permute-start.17 = (f32[8,128]{1,0:T(8,128)S(1)}, f32[8,128]{1,0:T(8,128)S(1)}, u32[]{:S(2)}, u32[]{:S(2)}) collective-permute-start(f32[8,128]{1,0:T(8,128)S(1)} %add.3.refs_0_), channel_id=1, source_target_pairs={{0,12},{4,8},{8,4},{12,0},{1,13},{5,9},{9,5},{13,1},{2,14},{6,10},... | collective-permute-start | bytes 12296 | tf_op jit(solution)/shard_map/ppermute | solution.py:642
  31.7 0.6 %collective-permute-start.16 = (f32[8,128]{1,0:T(8,128)S(1)}, f32[8,128]{1,0:T(8,128)S(1)}, u32[]{:S(2)}, u32[]{:S(2)}) collective-permute-start(f32[8,128]{1,0:T(8,128)S(1)} %add.3.refs_0_), channel_id=1, source_target_pairs={{0,8},{4,12},{8,0},{12,4},{1,9},{5,13},{9,1},{13,5},{2,10},{6,14},... | collective-permute-start | bytes 12296 | tf_op jit(solution)/shard_map/ppermute | solution.py:642
  32.3 2.2 %collective-permute-start.15 = (f32[8,128]{1,0:T(8,128)S(1)}, f32[8,128]{1,0:T(8,128)S(1)}, u32[]{:S(2)}, u32[]{:S(2)}) collective-permute-start(f32[8,128]{1,0:T(8,128)S(1)} %add.3.refs_0_), channel_id=1, source_target_pairs={{0,4},{4,0},{8,12},{12,8},{1,5},{5,1},{9,13},{13,9},{2,6},{6,2},{1... | collective-permute-start | bytes 12296 | tf_op jit(solution)/shard_map/ppermute | solution.py:642
  34.4 1.0 %collective-permute-done.17.refs_3_ = f32[8,128]{1,0:T(8,128)S(1)} collective-permute-done((f32[8,128]{1,0:T(8,128)S(1)}, f32[8,128]{1,0:T(8,128)S(1)}, u32[]{:S(2)}, u32[]{:S(2)}) %collective-permute-start.17) | collective-permute-done | bytes 4128 | tf_op jit(solution)/shard_map/ppermute | solution.py:642
  35.4 0.7 %collective-permute-done.16.refs_2_ = f32[8,128]{1,0:T(8,128)S(1)} collective-permute-done((f32[8,128]{1,0:T(8,128)S(1)}, f32[8,128]{1,0:T(8,128)S(1)}, u32[]{:S(2)}, u32[]{:S(2)}) %collective-permute-start.16) | collective-permute-done | bytes 4128 | tf_op jit(solution)/shard_map/ppermute | solution.py:642
  36.2 0.0 collective-permute-done.15.refs_1_
  36.2 0.0 copy-done
  36.2 0.8 %update.1 = (f32[128,128]{1,0:T(8,128)}, f32[128,128]{1,0:T(8,128)}, f32[128,128]{1,0:T(8,128)}) custom-call(f32[8,128]{1,0:T(8,128)S(1)} %add.3.refs_0_, f32[8,128]{1,0:T(8,128)S(1)} %collective-permute-done.15.refs_1_, f32[8,128]{1,0:T(8,128)S(1)} %collective-permute-done.16.refs_2_, f32[8,128]{1,0:T(8,128)S(1)} %collective-permute-done.17.refs_3_, ...), custom_call_target="tpu_custom_call" | custom-call | tf_op jit(solution)/shard_map/update/pallas_call | solution.py:794
  (6 shorter events, 0.0 us)
Async XLA Ops:
  2.5 12.7 %collective-permute-start.9 = (f32[64,616]{1,0:T(8,128)S(1)}, f32[64,616]{1,0:T(8,128)S(1)}, u32[]{:S(2)}, u32[]{:S(2)}) collective-permute-start(f32[64,616]{1,0:T(8,128)S(1)} %get-tuple-element.25.refs_0_), channel_id=1, source_target_pairs={{0,2},{2,0},{1,3},{3,1},{4,6},{6,4},{5,7},{7,5},{8,10},{10,8},{9,1... | collective-permute-start | bytes 473096 | tf_op jit(solution)/shard_map/ppermute | solution.py:662
  5.5 21.0 %collective-permute-start.8 = (f32[4,128,128]{2,1,0:T(8,128)S(1)}, f32[4,128,128]{2,1,0:T(8,128)S(1)}, u32[]{:S(2)}, u32[]{:S(2)}) collective-permute-start(f32[4,128,128]{2,1,0:T(8,128)S(1)} %get-tuple-element.23.refs_3_), channel_id=1, source_target_pairs={{0,2},{2,0},{1,3},{3,1},{4,6},{6,4},{5,7},{7,5},{8,10},{10,8},{9,1... | collective-permute-start | bytes 786440 | tf_op jit(solution)/shard_map/ppermute | solution.py:662
  5.6 6.7 %collective-permute-start.5 = (f32[96,128]{1,0:T(8,128)S(1)}, f32[96,128]{1,0:T(8,128)S(1)}, u32[]{:S(2)}, u32[]{:S(2)}) collective-permute-start(f32[96,128]{1,0:T(8,128)S(1)} %get-tuple-element.21.refs_2_), channel_id=1, source_target_pairs={{0,12},{4,8},{8,4},{12,0},{1,13},{5,9},{9,5},{13,1},{2,14},{6,10},... | collective-permute-start | bytes 147464 | tf_op jit(solution)/shard_map/ppermute | solution.py:642
  9.6 5.0 %collective-permute-start.3 = (f32[96,128]{1,0:T(8,128)S(1)}, f32[96,128]{1,0:T(8,128)S(1)}, u32[]{:S(2)}, u32[]{:S(2)}) collective-permute-start(f32[96,128]{1,0:T(8,128)S(1)} %get-tuple-element.21.refs_2_), channel_id=1, source_target_pairs={{0,8},{4,12},{8,0},{12,4},{1,9},{5,13},{9,1},{13,5},{2,10},{6,14},... | collective-permute-start | bytes 147464 | tf_op jit(solution)/shard_map/ppermute | solution.py:642
  9.6 5.0 %collective-permute-start.1 = (f32[96,128]{1,0:T(8,128)S(1)}, f32[96,128]{1,0:T(8,128)S(1)}, u32[]{:S(2)}, u32[]{:S(2)}) collective-permute-start(f32[96,128]{1,0:T(8,128)S(1)} %get-tuple-element.21.refs_2_), channel_id=1, source_target_pairs={{0,4},{4,0},{8,12},{12,8},{1,5},{5,1},{9,13},{13,9},{2,6},{6,2},{1... | collective-permute-start | bytes 147464 | tf_op jit(solution)/shard_map/ppermute | solution.py:642
  12.3 3.6 %collective-permute-start = (f32[96,128]{1,0:T(8,128)S(1)}, f32[96,128]{1,0:T(8,128)S(1)}, u32[]{:S(2)}, u32[]{:S(2)}) collective-permute-start(f32[96,128]{1,0:T(8,128)S(1)} %get-tuple-element.21.refs_2_), channel_id=1, source_target_pairs={{0,1},{1,0},{2,3},{3,2},{4,5},{5,4},{6,7},{7,6},{8,9},{9,8},{10,11... | collective-permute-start | bytes 147464 | tf_op jit(solution)/shard_map/ppermute | solution.py:642
  14.6 2.9 %collective-permute-start.6 = (f32[96,128]{1,0:T(8,128)S(1)}, f32[96,128]{1,0:T(8,128)S(1)}, u32[]{:S(2)}, u32[]{:S(2)}) collective-permute-start(f32[96,128]{1,0:T(8,128)S(1)} %collective-permute-done.5.refs_8_), channel_id=1, source_target_pairs={{0,1},{1,0},{2,3},{3,2},{4,5},{5,4},{6,7},{7,6},{8,9},{9,8},{10,11... | collective-permute-start | bytes 147464 | tf_op jit(solution)/shard_map/ppermute | solution.py:642
  14.6 3.3 %collective-permute-start.4 = (f32[96,128]{1,0:T(8,128)S(1)}, f32[96,128]{1,0:T(8,128)S(1)}, u32[]{:S(2)}, u32[]{:S(2)}) collective-permute-start(f32[96,128]{1,0:T(8,128)S(1)} %collective-permute-done.3.refs_6_), channel_id=1, source_target_pairs={{0,1},{1,0},{2,3},{3,2},{4,5},{5,4},{6,7},{7,6},{8,9},{9,8},{10,11... | collective-permute-start | bytes 147464 | tf_op jit(solution)/shard_map/ppermute | solution.py:642
  15.1 5.2 %collective-permute-start.2 = (f32[96,128]{1,0:T(8,128)S(1)}, f32[96,128]{1,0:T(8,128)S(1)}, u32[]{:S(2)}, u32[]{:S(2)}) collective-permute-start(f32[96,128]{1,0:T(8,128)S(1)} %collective-permute-done.1.refs_4_), channel_id=1, source_target_pairs={{0,1},{1,0},{2,3},{3,2},{4,5},{5,4},{6,7},{7,6},{8,9},{9,8},{10,11... | collective-permute-start | bytes 147464 | tf_op jit(solution)/shard_map/ppermute | solution.py:642
  15.2 5.1 %copy-start.4 = (s32[8,4]{0,1:T(4,128)S(1)}, s32[8,4]{0,1:T(4,128)}, u32[]{:S(2)}) copy-start(s32[8,4]{0,1:T(4,128)} %param.24) | copy-start | bytes 388
  15.8 4.5 %copy-start.3 = (s32[8,4]{0,1:T(4,128)S(1)}, s32[8,4]{0,1:T(4,128)}, u32[]{:S(2)}) copy-start(s32[8,4]{0,1:T(4,128)} %param.23) | copy-start | bytes 388
  15.8 7.2 %collective-permute-start.12 = (f32[8,128]{1,0:T(8,128)S(1)}, f32[8,128]{1,0:T(8,128)S(1)}, u32[]{:S(2)}, u32[]{:S(2)}) collective-permute-start(f32[8,128]{1,0:T(8,128)S(1)} %compose.1), channel_id=1, source_target_pairs={{0,12},{4,8},{8,4},{12,0},{1,13},{5,9},{9,5},{13,1},{2,14},{6,10},... | collective-permute-start | bytes 12296 | tf_op jit(solution)/shard_map/ppermute | solution.py:642
  17.5 5.6 %collective-permute-start.11 = (f32[8,128]{1,0:T(8,128)S(1)}, f32[8,128]{1,0:T(8,128)S(1)}, u32[]{:S(2)}, u32[]{:S(2)}) collective-permute-start(f32[8,128]{1,0:T(8,128)S(1)} %compose.1), channel_id=1, source_target_pairs={{0,8},{4,12},{8,0},{12,4},{1,9},{5,13},{9,1},{13,5},{2,10},{6,14},... | collective-permute-start | bytes 12296 | tf_op jit(solution)/shard_map/ppermute | solution.py:642
  17.9 5.1 %collective-permute-start.10 = (f32[8,128]{1,0:T(8,128)S(1)}, f32[8,128]{1,0:T(8,128)S(1)}, u32[]{:S(2)}, u32[]{:S(2)}) collective-permute-start(f32[8,128]{1,0:T(8,128)S(1)} %compose.1), channel_id=1, source_target_pairs={{0,4},{4,0},{8,12},{12,8},{1,5},{5,1},{9,13},{13,9},{2,6},{6,2},{1... | collective-permute-start | bytes 12296 | tf_op jit(solution)/shard_map/ppermute | solution.py:642
  21.5 4.9 %collective-permute-start.7 = (f32[192,128]{1,0:T(8,128)S(1)}, f32[192,128]{1,0:T(8,128)S(1)}, u32[]{:S(2)}, u32[]{:S(2)}) collective-permute-start(f32[192,128]{1,0:T(8,128)S(1)} %get-tuple-element.22.refs_1_), channel_id=1, source_target_pairs={{0,2},{2,0},{1,3},{3,1},{4,6},{6,4},{5,7},{7,5},{8,10},{10,8},{9,1... | collective-permute-start | bytes 294920 | tf_op jit(solution)/shard_map/ppermute | solution.py:662
  23.1 1.2 %collective-permute-start.13 = (f32[32,128]{1,0:T(8,128)S(1)}, f32[32,128]{1,0:T(8,128)S(1)}, u32[]{:S(2)}, u32[]{:S(2)}) collective-permute-start(f32[32,128]{1,0:T(8,128)S(1)} %pad_maximum_fusion.refs_1_), channel_id=1, source_target_pairs={{0,1},{1,0},{2,3},{3,2},{4,5},{5,4},{6,7},{7,6},{8,9},{9,8},{10,11... | collective-permute-start | bytes 49160 | tf_op jit(solution)/shard_map/ppermute | solution.py:642
  26.5 9.7 %copy-start = (f32[1,128,128]{2,1,0:T(8,128)S(1)}, f32[1,128,128]{2,1,0:T(8,128)}, u32[]{:S(2)}) copy-start(f32[1,128,128]{2,1,0:T(8,128)} %param.17) | copy-start | bytes 196612
  26.5 9.7 %copy-start.1 = (f32[1,128,128]{2,1,0:T(8,128)S(1)}, f32[1,128,128]{2,1,0:T(8,128)}, u32[]{:S(2)}) copy-start(f32[1,128,128]{2,1,0:T(8,128)} %param.16) | copy-start | bytes 196612
  26.5 9.7 %copy-start.2 = (f32[1,128,128]{2,1,0:T(8,128)S(1)}, f32[1,128,128]{2,1,0:T(8,128)}, u32[]{:S(2)}) copy-start(f32[1,128,128]{2,1,0:T(8,128)} %param.15) | copy-start | bytes 196612
  28.8 1.2 %collective-permute-start.14 = (f32[8,128]{1,0:T(8,128)S(1)}, f32[8,128]{1,0:T(8,128)S(1)}, u32[]{:S(2)}, u32[]{:S(2)}) collective-permute-start(f32[8,128]{1,0:T(8,128)S(1)} %get-tuple-element.32), channel_id=1, source_target_pairs={{0,1},{1,0},{2,3},{3,2},{4,5},{5,4},{6,7},{7,6},{8,9},{9,8},{10,11... | collective-permute-start | bytes 12296 | tf_op jit(solution)/shard_map/ppermute | solution.py:642
  30.0 5.4 %collective-permute-start.17 = (f32[8,128]{1,0:T(8,128)S(1)}, f32[8,128]{1,0:T(8,128)S(1)}, u32[]{:S(2)}, u32[]{:S(2)}) collective-permute-start(f32[8,128]{1,0:T(8,128)S(1)} %add.3.refs_0_), channel_id=1, source_target_pairs={{0,12},{4,8},{8,4},{12,0},{1,13},{5,9},{9,5},{13,1},{2,14},{6,10},... | collective-permute-start | bytes 12296 | tf_op jit(solution)/shard_map/ppermute | solution.py:642
  31.7 4.5 %collective-permute-start.16 = (f32[8,128]{1,0:T(8,128)S(1)}, f32[8,128]{1,0:T(8,128)S(1)}, u32[]{:S(2)}, u32[]{:S(2)}) collective-permute-start(f32[8,128]{1,0:T(8,128)S(1)} %add.3.refs_0_), channel_id=1, source_target_pairs={{0,8},{4,12},{8,0},{12,4},{1,9},{5,13},{9,1},{13,5},{2,10},{6,14},... | collective-permute-start | bytes 12296 | tf_op jit(solution)/shard_map/ppermute | solution.py:642
  32.3 3.9 %collective-permute-start.15 = (f32[8,128]{1,0:T(8,128)S(1)}, f32[8,128]{1,0:T(8,128)S(1)}, u32[]{:S(2)}, u32[]{:S(2)}) collective-permute-start(f32[8,128]{1,0:T(8,128)S(1)} %add.3.refs_0_), channel_id=1, source_target_pairs={{0,4},{4,0},{8,12},{12,8},{1,5},{5,1},{9,13},{13,9},{2,6},{6,2},{1... | collective-permute-start | bytes 12296 | tf_op jit(solution)/shard_map/ppermute | solution.py:642

commit v4 on v3

--- a/solution.py
+++ b/solution.py
@@ -640,6 +640,11 @@
 def exchanged(value, axis, mask):
     count = lax.axis_size(axis)
     return lax.ppermute(value, axis, [(i, i ^ mask) for i in range(count)])
+
+
+def split_exchange(value):
+    pairs = [(2 * tile + sub, 2 * (tile ^ (2 + sub)) + sub) for tile in range(4) for sub in range(2)]
+    return lax.ppermute(value, ("tile", "sub"), pairs)
 
 
 def gathered(value, joined):
@@ -783,8 +788,9 @@
 
     for mask in range(1, subs):
         sums = sums + exchanged(sums, "sub", mask)
-    if tiles <= 4:
-        parts = [sums] + [exchanged(sums, "tile", mask) for mask in range(1, tiles)]
+    if (tiles, subs) == (4, 2):
+        far = split_exchange(sums)
+        parts = [sums, far, exchanged(sums, "tile", 1), exchanged(far, "sub", 1)]
     else:
         mask = 1
         while mask < tiles:

time: 37.2 us -> 36.7 us (0.987)
  starting transfers between devices: 19 us -> 16.8 us
  waiting for transfers between devices: 8.39 us -> 10.1 us
    ppermute x15 -> x14, starting transfers between devices: 14.3 us -> 11.1 us  [exchanged(): return lax.ppermute(value, axis, [(i, i ^ mask) for i in range(count)])]
    ppermute x0 -> x1, waiting for transfers between devices: none -> 2.32 us  [split_exchange(): return lax.ppermute(value, ('tile', 'sub'), pairs)]
    ppermute x0 -> x1, starting transfers between devices: none -> 1.06 us  [split_exchange(): return lax.ppermute(value, ('tile', 'sub'), pairs)]
    ppermute x15 -> x14, waiting for transfers between devices: 8.38 us -> 7.8 us  [exchanged(): return lax.ppermute(value, axis, [(i, i ^ mask) for i in range(count)])]
  transfers between devices with their start and end apart: 18 -> 18, of which waited for: 6 -> 7; matrix products, arithmetic and copies ran while one was open for 0% -> 0% of each run, Pallas kernels for 11% -> 11%
where the time goes in v4:
time: 36.7 us; the launch traced here: 36.5 us
  starting transfers between devices  16.8 us (46%)
  waiting for transfers between devices  10.1 us (28%)
  Pallas kernels  8.15 us (22%)
  between operations  1.4 us (4%)
    ppermute x14, starting transfers between devices, exchanged(): return lax.ppermute(value, axis, [(i, i ^ mask) for i in range(count)])  11.1 us
    ppermute x14, waiting for transfers between devices, exchanged(): return lax.ppermute(value, axis, [(i, i ^ mask) for i in range(count)])  7.8 us
    ppermute x3, starting transfers between devices, level_parts(): lax.ppermute(value, 'lev', [(i, (i + k) % count) for i in range(count)])  4.67 us
    ppermute x1, waiting for transfers between devices, split_exchange(): return lax.ppermute(value, ('tile', 'sub'), pairs)  2.32 us
    pallas_call x1, Pallas kernels, body(): pl.pallas_call(functools.partial(evolve, levels), out_shape=(vmem(*shape)...  2.29 us
    pallas_call x1, Pallas kernels, body(): pl.pallas_call(functools.partial(gains, levels, slots, len(records)), out...  2.1 us
    pallas_call x1, Pallas kernels, body(): pl.pallas_call(functools.partial(assemble, len(messages)), out_shape=(vme...  1.2 us
    pallas_call x1, Pallas kernels, body(): pl.pallas_call(functools.partial(prepare, width.bit_length() - 1), out_sh...  1.17 us
  transfers between devices with their start and end apart: 18, of which 7 were waited for; matrix products, arithmetic and copies ran while one was open for 0% of the time, Pallas kernels for 11%

profile of v4, /device:TPU:0, one launch (start us, length us, event | category | flops | bytes accessed | tf_op | source)
XLA Modules:
  0.0 36.5 jit_solution(10735144168346800534)
XLA Ops:
  1.3 1.2 %prepare.1 = (f32[96,128]{1,0:T(8,128)S(1)}, f32[4,128,128]{2,1,0:T(8,128)S(1)}, f32[64,616]{1,0:T(8,128)S(1)}, f32[8,128]{1,0:T(8,128)S(1)}, f32[1,616]{1,0:T(1,128)S(1)}, /*index=5*/f32[8,128]{1,0:T(8,128)S(1)}) custom-call(s32[1]{0:T(128)S(6)} %copy.18.count, f32[2]{0:T(128)} %diffusion.1, f32[2]{0:T(128)} %vertical.1, f32[2]{0:T(128)} %prior.1, ...), custom_call_target="tpu_custom_call" | custom-call | tf_op jit(solution)/shard_map/prepare/pallas_call | solution.py:697
  2.5 3.0 %collective-permute-start.9 = (f32[64,616]{1,0:T(8,128)S(1)}, f32[64,616]{1,0:T(8,128)S(1)}, u32[]{:S(2)}, u32[]{:S(2)}) collective-permute-start(f32[64,616]{1,0:T(8,128)S(1)} %get-tuple-element.25.refs_0_), channel_id=1, source_target_pairs={{0,2},{2,0},{1,3},{3,1},{4,6},{6,4},{5,7},{7,5},{8,10},{10,8},{9,1... | collective-permute-start | bytes 473096 | tf_op jit(solution)/shard_map/ppermute | solution.py:667
  5.5 0.1 collective-permute-start.8
  5.6 4.1 %collective-permute-start.5 = (f32[96,128]{1,0:T(8,128)S(1)}, f32[96,128]{1,0:T(8,128)S(1)}, u32[]{:S(2)}, u32[]{:S(2)}) collective-permute-start(f32[96,128]{1,0:T(8,128)S(1)} %get-tuple-element.21.refs_2_), channel_id=1, source_target_pairs={{0,12},{4,8},{8,4},{12,0},{1,13},{5,9},{9,5},{13,1},{2,14},{6,10},... | collective-permute-start | bytes 147464 | tf_op jit(solution)/shard_map/ppermute | solution.py:642
  9.6 0.0 collective-permute-start.3
  9.6 0.6 %collective-permute-start.1 = (f32[96,128]{1,0:T(8,128)S(1)}, f32[96,128]{1,0:T(8,128)S(1)}, u32[]{:S(2)}, u32[]{:S(2)}) collective-permute-start(f32[96,128]{1,0:T(8,128)S(1)} %get-tuple-element.21.refs_2_), channel_id=1, source_target_pairs={{0,4},{4,0},{8,12},{12,8},{1,5},{5,1},{9,13},{13,9},{2,6},{6,2},{1... | collective-permute-start | bytes 147464 | tf_op jit(solution)/shard_map/ppermute | solution.py:642
  10.2 2.1 %collective-permute-done.5.refs_8_ = f32[96,128]{1,0:T(8,128)S(1)} collective-permute-done((f32[96,128]{1,0:T(8,128)S(1)}, f32[96,128]{1,0:T(8,128)S(1)}, u32[]{:S(2)}, u32[]{:S(2)}) %collective-permute-start.5) | collective-permute-done | bytes 49184 | tf_op jit(solution)/shard_map/ppermute | solution.py:642
  12.3 0.0 collective-permute-start
  12.3 2.3 %collective-permute-done.3.refs_6_ = f32[96,128]{1,0:T(8,128)S(1)} collective-permute-done((f32[96,128]{1,0:T(8,128)S(1)}, f32[96,128]{1,0:T(8,128)S(1)}, u32[]{:S(2)}, u32[]{:S(2)}) %collective-permute-start.3) | collective-permute-done | bytes 49184 | tf_op jit(solution)/shard_map/ppermute | solution.py:642
  14.6 0.0 collective-permute-start.6
  14.6 0.0 collective-permute-done.1.refs_4_
  14.6 0.5 %collective-permute-start.4 = (f32[96,128]{1,0:T(8,128)S(1)}, f32[96,128]{1,0:T(8,128)S(1)}, u32[]{:S(2)}, u32[]{:S(2)}) collective-permute-start(f32[96,128]{1,0:T(8,128)S(1)} %collective-permute-done.3.refs_6_), channel_id=1, source_target_pairs={{0,1},{1,0},{2,3},{3,2},{4,5},{5,4},{6,7},{7,6},{8,9},{9,8},{10,11... | collective-permute-start | bytes 147464 | tf_op jit(solution)/shard_map/ppermute | solution.py:642
  15.1 0.0 collective-permute-done.9.refs_1_
  15.1 0.1 collective-permute-start.2
  15.2 0.6 %compose.1 = f32[8,128]{1,0:T(8,128)S(1)} custom-call(f32[64,616]{1,0:T(8,128)S(1)} %get-tuple-element.25.refs_0_, f32[64,616]{1,0:T(8,128)S(1)} %collective-permute-done.9.refs_1_, f32[1,616]{1,0:T(1,128)S(1)} %get-tuple-element.26.refs_2_, f32[8,128]{1,0:T(8,128)S(1)} %get-tuple-element.27.refs_3_), custom_call_target="tpu_custom_call" | custom-call | tf_op jit(solution)/shard_map/compose/pallas_call | solution.py:728
  15.8 0.0 collective-permute-done.refs_3_
  15.8 1.7 %collective-permute-start.12 = (f32[8,128]{1,0:T(8,128)S(1)}, f32[8,128]{1,0:T(8,128)S(1)}, u32[]{:S(2)}, u32[]{:S(2)}) collective-permute-start(f32[8,128]{1,0:T(8,128)S(1)} %compose.1), channel_id=1, source_target_pairs={{0,12},{4,8},{8,4},{12,0},{1,13},{5,9},{9,5},{13,1},{2,14},{6,10},... | collective-permute-start | bytes 12296 | tf_op jit(solution)/shard_map/ppermute | solution.py:642
  17.5 0.0 collective-permute-done.6.refs_9_
  17.5 0.4 %collective-permute-start.11 = (f32[8,128]{1,0:T(8,128)S(1)}, f32[8,128]{1,0:T(8,128)S(1)}, u32[]{:S(2)}, u32[]{:S(2)}) collective-permute-start(f32[8,128]{1,0:T(8,128)S(1)} %compose.1), channel_id=1, source_target_pairs={{0,8},{4,12},{8,0},{12,4},{1,9},{5,13},{9,1},{13,5},{2,10},{6,14},... | collective-permute-start | bytes 12296 | tf_op jit(solution)/shard_map/ppermute | solution.py:642
  17.9 0.0 collective-permute-done.4.refs_7_
  17.9 2.4 %collective-permute-start.10 = (f32[8,128]{1,0:T(8,128)S(1)}, f32[8,128]{1,0:T(8,128)S(1)}, u32[]{:S(2)}, u32[]{:S(2)}) collective-permute-start(f32[8,128]{1,0:T(8,128)S(1)} %compose.1), channel_id=1, source_target_pairs={{0,4},{4,0},{8,12},{12,8},{1,5},{5,1},{9,13},{13,9},{2,6},{6,2},{1... | collective-permute-start | bytes 12296 | tf_op jit(solution)/shard_map/ppermute | solution.py:642
  20.3 0.0 collective-permute-done.2.refs_5_
  20.3 0.0 copy-done.4
  20.3 0.0 copy-done.3
  20.3 1.2 %assemble.1 = (f32[192,128]{1,0:T(8,128)S(1)}, f32[8,128]{1,0:T(8,128)S(1)}) custom-call(s32[4,8]{1,0:T(4,128)S(1)} %bitcast.18, s32[4,8]{1,0:T(4,128)S(1)} %bitcast.19, f32[96,128]{1,0:T(8,128)S(1)} %get-tuple-element.21.refs_2_, f32[96,128]{1,0:T(8,128)S(1)} %collective-permute-done.refs_3_, f32[96,128]{1,0:T(8,128)S(1)} %collective-permute-done.1.refs_4_, ...), custom_call_target="tpu_custom_call" | custom-call | tf_op jit(solution)/shard_map/assemble/pallas_call | solution.py:741
  21.5 1.6 %collective-permute-start.7 = (f32[192,128]{1,0:T(8,128)S(1)}, f32[192,128]{1,0:T(8,128)S(1)}, u32[]{:S(2)}, u32[]{:S(2)}) collective-permute-start(f32[192,128]{1,0:T(8,128)S(1)} %get-tuple-element.22.refs_1_), channel_id=1, source_target_pairs={{0,2},{2,0},{1,3},{3,1},{4,6},{6,4},{5,7},{7,5},{8,10},{10,8},{9,1... | collective-permute-start | bytes 294920 | tf_op jit(solution)/shard_map/ppermute | solution.py:667
  23.1 0.0 collective-permute-done.12
  23.1 0.0 collective-permute-done.11
  23.1 0.0 collective-permute-done.10
  23.1 0.1 collective-permute-start.13
  23.2 1.2 %collective-permute-done.13.refs_2_ = f32[32,128]{1,0:T(8,128)S(1)} collective-permute-done((f32[32,128]{1,0:T(8,128)S(1)}, f32[32,128]{1,0:T(8,128)S(1)}, u32[]{:S(2)}, u32[]{:S(2)}) %collective-permute-start.13) | collective-permute-done | bytes 16416 | tf_op jit(solution)/shard_map/ppermute | solution.py:642
  24.3 2.1 %gains.1 = (f32[12,128,128]{2,1,0:T(8,128)S(1)}, f32[2,12,8,128]{3,2,1,0:T(8,128)S(1)}, f32[12,128,128]{2,1,0:T(8,128)S(1)}, f32[12,32,128]{2,1,0:T(8,128)S(1)}) custom-call(f32[8,128]{1,0:T(8,128)S(1)} %get-tuple-element.24.refs_0_, f32[32,128]{1,0:T(8,128)S(1)} %pad_maximum_fusion.refs_1_, f32[32,128]{1,0:T(8,128)S(1)} %collective-permute-done.13.refs_2_), custom_call_target="tpu_custom_call" | custom-call | tf_op jit(solution)/shard_map/gains/pallas_call | solution.py:756
  26.5 0.0 collective-permute-done.7.refs_2_
  26.5 0.0 collective-permute-done.8.refs_4_
  26.5 0.0 copy-start
  26.5 0.0 copy-start.1
  26.5 0.0 copy-start.2
  26.5 2.3 %evolve.1 = (f32[128,128]{1,0:T(8,128)S(1)}, f32[8,128]{1,0:T(8,128)S(1)}) custom-call(f32[8,128]{1,0:T(8,128)S(1)} %get-tuple-element.20.refs_0_, f32[192,128]{1,0:T(8,128)S(1)} %get-tuple-element.22.refs_1_, f32[192,128]{1,0:T(8,128)S(1)} %collective-permute-done.7.refs_2_, f32[4,128,128]{2,1,0:T(8,128)S(1)} %get-tuple-element.23.refs_3_, ...), custom_call_target="tpu_custom_call" | custom-call | tf_op jit(solution)/shard_map/evolve/pallas_call | solution.py:766
  28.8 0.2 collective-permute-start.14
  29.0 1.0 %collective-permute-done.14 = f32[8,128]{1,0:T(8,128)S(1)} collective-permute-done((f32[8,128]{1,0:T(8,128)S(1)}, f32[8,128]{1,0:T(8,128)S(1)}, u32[]{:S(2)}, u32[]{:S(2)}) %collective-permute-start.14) | collective-permute-done | bytes 4128 | tf_op jit(solution)/shard_map/ppermute | solution.py:642
  30.0 1.1 %collective-permute-start.15 = (f32[8,128]{1,0:T(8,128)S(1)}, f32[8,128]{1,0:T(8,128)S(1)}, u32[]{:S(2)}, u32[]{:S(2)}) collective-permute-start(f32[8,128]{1,0:T(8,128)S(1)} %add.3.refs_0_), channel_id=1, source_target_pairs={{0,8},{1,13},{4,12},{5,9},{8,0},{9,5},{12,4},{13,1},{2,10},{3,15},... | collective-permute-start | bytes 12296 | tf_op jit(solution)/shard_map/ppermute | solution.py:647
  31.1 1.1 %collective-permute-start.16 = (f32[8,128]{1,0:T(8,128)S(1)}, f32[8,128]{1,0:T(8,128)S(1)}, u32[]{:S(2)}, u32[]{:S(2)}) collective-permute-start(f32[8,128]{1,0:T(8,128)S(1)} %add.3.refs_0_), channel_id=1, source_target_pairs={{0,4},{4,0},{8,12},{12,8},{1,5},{5,1},{9,13},{13,9},{2,6},{6,2},{1... | collective-permute-start | bytes 12296 | tf_op jit(solution)/shard_map/ppermute | solution.py:642
  32.2 2.3 %collective-permute-done.15.refs_1_ = f32[8,128]{1,0:T(8,128)S(1)} collective-permute-done((f32[8,128]{1,0:T(8,128)S(1)}, f32[8,128]{1,0:T(8,128)S(1)}, u32[]{:S(2)}, u32[]{:S(2)}) %collective-permute-start.15) | collective-permute-done | bytes 4128 | tf_op jit(solution)/shard_map/ppermute | solution.py:647
  34.5 0.0 collective-permute-start.17
  34.6 0.2 collective-permute-done.16.refs_2_
  34.7 1.0 %collective-permute-done.17.refs_3_ = f32[8,128]{1,0:T(8,128)S(1)} collective-permute-done((f32[8,128]{1,0:T(8,128)S(1)}, f32[8,128]{1,0:T(8,128)S(1)}, u32[]{:S(2)}, u32[]{:S(2)}) %collective-permute-start.17) | collective-permute-done | bytes 4128 | tf_op jit(solution)/shard_map/ppermute | solution.py:642
  35.7 0.0 copy-done
  35.7 0.8 %update.1 = (f32[128,128]{1,0:T(8,128)}, f32[128,128]{1,0:T(8,128)}, f32[128,128]{1,0:T(8,128)}) custom-call(f32[8,128]{1,0:T(8,128)S(1)} %add.3.refs_0_, f32[8,128]{1,0:T(8,128)S(1)} %collective-permute-done.15.refs_1_, f32[8,128]{1,0:T(8,128)S(1)} %collective-permute-done.16.refs_2_, f32[8,128]{1,0:T(8,128)S(1)} %collective-permute-done.17.refs_3_, ...), custom_call_target="tpu_custom_call" | custom-call | tf_op jit(solution)/shard_map/update/pallas_call | solution.py:800
  (6 shorter events, 0.0 us)
Async XLA Ops:
  2.5 12.7 %collective-permute-start.9 = (f32[64,616]{1,0:T(8,128)S(1)}, f32[64,616]{1,0:T(8,128)S(1)}, u32[]{:S(2)}, u32[]{:S(2)}) collective-permute-start(f32[64,616]{1,0:T(8,128)S(1)} %get-tuple-element.25.refs_0_), channel_id=1, source_target_pairs={{0,2},{2,0},{1,3},{3,1},{4,6},{6,4},{5,7},{7,5},{8,10},{10,8},{9,1... | collective-permute-start | bytes 473096 | tf_op jit(solution)/shard_map/ppermute | solution.py:667
  5.5 21.0 %collective-permute-start.8 = (f32[4,128,128]{2,1,0:T(8,128)S(1)}, f32[4,128,128]{2,1,0:T(8,128)S(1)}, u32[]{:S(2)}, u32[]{:S(2)}) collective-permute-start(f32[4,128,128]{2,1,0:T(8,128)S(1)} %get-tuple-element.23.refs_3_), channel_id=1, source_target_pairs={{0,2},{2,0},{1,3},{3,1},{4,6},{6,4},{5,7},{7,5},{8,10},{10,8},{9,1... | collective-permute-start | bytes 786440 | tf_op jit(solution)/shard_map/ppermute | solution.py:667
  5.6 6.7 %collective-permute-start.5 = (f32[96,128]{1,0:T(8,128)S(1)}, f32[96,128]{1,0:T(8,128)S(1)}, u32[]{:S(2)}, u32[]{:S(2)}) collective-permute-start(f32[96,128]{1,0:T(8,128)S(1)} %get-tuple-element.21.refs_2_), channel_id=1, source_target_pairs={{0,12},{4,8},{8,4},{12,0},{1,13},{5,9},{9,5},{13,1},{2,14},{6,10},... | collective-permute-start | bytes 147464 | tf_op jit(solution)/shard_map/ppermute | solution.py:642
  9.6 5.0 %collective-permute-start.3 = (f32[96,128]{1,0:T(8,128)S(1)}, f32[96,128]{1,0:T(8,128)S(1)}, u32[]{:S(2)}, u32[]{:S(2)}) collective-permute-start(f32[96,128]{1,0:T(8,128)S(1)} %get-tuple-element.21.refs_2_), channel_id=1, source_target_pairs={{0,8},{4,12},{8,0},{12,4},{1,9},{5,13},{9,1},{13,5},{2,10},{6,14},... | collective-permute-start | bytes 147464 | tf_op jit(solution)/shard_map/ppermute | solution.py:642
  9.6 5.0 %collective-permute-start.1 = (f32[96,128]{1,0:T(8,128)S(1)}, f32[96,128]{1,0:T(8,128)S(1)}, u32[]{:S(2)}, u32[]{:S(2)}) collective-permute-start(f32[96,128]{1,0:T(8,128)S(1)} %get-tuple-element.21.refs_2_), channel_id=1, source_target_pairs={{0,4},{4,0},{8,12},{12,8},{1,5},{5,1},{9,13},{13,9},{2,6},{6,2},{1... | collective-permute-start | bytes 147464 | tf_op jit(solution)/shard_map/ppermute | solution.py:642
  12.3 3.6 %collective-permute-start = (f32[96,128]{1,0:T(8,128)S(1)}, f32[96,128]{1,0:T(8,128)S(1)}, u32[]{:S(2)}, u32[]{:S(2)}) collective-permute-start(f32[96,128]{1,0:T(8,128)S(1)} %get-tuple-element.21.refs_2_), channel_id=1, source_target_pairs={{0,1},{1,0},{2,3},{3,2},{4,5},{5,4},{6,7},{7,6},{8,9},{9,8},{10,11... | collective-permute-start | bytes 147464 | tf_op jit(solution)/shard_map/ppermute | solution.py:642
  14.6 2.9 %collective-permute-start.6 = (f32[96,128]{1,0:T(8,128)S(1)}, f32[96,128]{1,0:T(8,128)S(1)}, u32[]{:S(2)}, u32[]{:S(2)}) collective-permute-start(f32[96,128]{1,0:T(8,128)S(1)} %collective-permute-done.5.refs_8_), channel_id=1, source_target_pairs={{0,1},{1,0},{2,3},{3,2},{4,5},{5,4},{6,7},{7,6},{8,9},{9,8},{10,11... | collective-permute-start | bytes 147464 | tf_op jit(solution)/shard_map/ppermute | solution.py:642
  14.6 3.3 %collective-permute-start.4 = (f32[96,128]{1,0:T(8,128)S(1)}, f32[96,128]{1,0:T(8,128)S(1)}, u32[]{:S(2)}, u32[]{:S(2)}) collective-permute-start(f32[96,128]{1,0:T(8,128)S(1)} %collective-permute-done.3.refs_6_), channel_id=1, source_target_pairs={{0,1},{1,0},{2,3},{3,2},{4,5},{5,4},{6,7},{7,6},{8,9},{9,8},{10,11... | collective-permute-start | bytes 147464 | tf_op jit(solution)/shard_map/ppermute | solution.py:642
  15.1 5.2 %collective-permute-start.2 = (f32[96,128]{1,0:T(8,128)S(1)}, f32[96,128]{1,0:T(8,128)S(1)}, u32[]{:S(2)}, u32[]{:S(2)}) collective-permute-start(f32[96,128]{1,0:T(8,128)S(1)} %collective-permute-done.1.refs_4_), channel_id=1, source_target_pairs={{0,1},{1,0},{2,3},{3,2},{4,5},{5,4},{6,7},{7,6},{8,9},{9,8},{10,11... | collective-permute-start | bytes 147464 | tf_op jit(solution)/shard_map/ppermute | solution.py:642
  15.2 5.1 %copy-start.4 = (s32[8,4]{0,1:T(4,128)S(1)}, s32[8,4]{0,1:T(4,128)}, u32[]{:S(2)}) copy-start(s32[8,4]{0,1:T(4,128)} %param.24) | copy-start | bytes 388
  15.8 4.5 %copy-start.3 = (s32[8,4]{0,1:T(4,128)S(1)}, s32[8,4]{0,1:T(4,128)}, u32[]{:S(2)}) copy-start(s32[8,4]{0,1:T(4,128)} %param.23) | copy-start | bytes 388
  15.8 7.2 %collective-permute-start.12 = (f32[8,128]{1,0:T(8,128)S(1)}, f32[8,128]{1,0:T(8,128)S(1)}, u32[]{:S(2)}, u32[]{:S(2)}) collective-permute-start(f32[8,128]{1,0:T(8,128)S(1)} %compose.1), channel_id=1, source_target_pairs={{0,12},{4,8},{8,4},{12,0},{1,13},{5,9},{9,5},{13,1},{2,14},{6,10},... | collective-permute-start | bytes 12296 | tf_op jit(solution)/shard_map/ppermute | solution.py:642
  17.5 5.6 %collective-permute-start.11 = (f32[8,128]{1,0:T(8,128)S(1)}, f32[8,128]{1,0:T(8,128)S(1)}, u32[]{:S(2)}, u32[]{:S(2)}) collective-permute-start(f32[8,128]{1,0:T(8,128)S(1)} %compose.1), channel_id=1, source_target_pairs={{0,8},{4,12},{8,0},{12,4},{1,9},{5,13},{9,1},{13,5},{2,10},{6,14},... | collective-permute-start | bytes 12296 | tf_op jit(solution)/shard_map/ppermute | solution.py:642
  17.9 5.1 %collective-permute-start.10 = (f32[8,128]{1,0:T(8,128)S(1)}, f32[8,128]{1,0:T(8,128)S(1)}, u32[]{:S(2)}, u32[]{:S(2)}) collective-permute-start(f32[8,128]{1,0:T(8,128)S(1)} %compose.1), channel_id=1, source_target_pairs={{0,4},{4,0},{8,12},{12,8},{1,5},{5,1},{9,13},{13,9},{2,6},{6,2},{1... | collective-permute-start | bytes 12296 | tf_op jit(solution)/shard_map/ppermute | solution.py:642
  21.5 4.9 %collective-permute-start.7 = (f32[192,128]{1,0:T(8,128)S(1)}, f32[192,128]{1,0:T(8,128)S(1)}, u32[]{:S(2)}, u32[]{:S(2)}) collective-permute-start(f32[192,128]{1,0:T(8,128)S(1)} %get-tuple-element.22.refs_1_), channel_id=1, source_target_pairs={{0,2},{2,0},{1,3},{3,1},{4,6},{6,4},{5,7},{7,5},{8,10},{10,8},{9,1... | collective-permute-start | bytes 294920 | tf_op jit(solution)/shard_map/ppermute | solution.py:667
  23.1 1.2 %collective-permute-start.13 = (f32[32,128]{1,0:T(8,128)S(1)}, f32[32,128]{1,0:T(8,128)S(1)}, u32[]{:S(2)}, u32[]{:S(2)}) collective-permute-start(f32[32,128]{1,0:T(8,128)S(1)} %pad_maximum_fusion.refs_1_), channel_id=1, source_target_pairs={{0,1},{1,0},{2,3},{3,2},{4,5},{5,4},{6,7},{7,6},{8,9},{9,8},{10,11... | collective-permute-start | bytes 49160 | tf_op jit(solution)/shard_map/ppermute | solution.py:642
  26.5 9.2 %copy-start = (f32[1,128,128]{2,1,0:T(8,128)S(1)}, f32[1,128,128]{2,1,0:T(8,128)}, u32[]{:S(2)}) copy-start(f32[1,128,128]{2,1,0:T(8,128)} %param.17) | copy-start | bytes 196612
  26.5 9.2 %copy-start.1 = (f32[1,128,128]{2,1,0:T(8,128)S(1)}, f32[1,128,128]{2,1,0:T(8,128)}, u32[]{:S(2)}) copy-start(f32[1,128,128]{2,1,0:T(8,128)} %param.16) | copy-start | bytes 196612
  26.5 9.2 %copy-start.2 = (f32[1,128,128]{2,1,0:T(8,128)S(1)}, f32[1,128,128]{2,1,0:T(8,128)}, u32[]{:S(2)}) copy-start(f32[1,128,128]{2,1,0:T(8,128)} %param.15) | copy-start | bytes 196612
  28.8 1.2 %collective-permute-start.14 = (f32[8,128]{1,0:T(8,128)S(1)}, f32[8,128]{1,0:T(8,128)S(1)}, u32[]{:S(2)}, u32[]{:S(2)}) collective-permute-start(f32[8,128]{1,0:T(8,128)S(1)} %get-tuple-element.32), channel_id=1, source_target_pairs={{0,1},{1,0},{2,3},{3,2},{4,5},{5,4},{6,7},{7,6},{8,9},{9,8},{10,11... | collective-permute-start | bytes 12296 | tf_op jit(solution)/shard_map/ppermute | solution.py:642
  30.0 4.5 %collective-permute-start.15 = (f32[8,128]{1,0:T(8,128)S(1)}, f32[8,128]{1,0:T(8,128)S(1)}, u32[]{:S(2)}, u32[]{:S(2)}) collective-permute-start(f32[8,128]{1,0:T(8,128)S(1)} %add.3.refs_0_), channel_id=1, source_target_pairs={{0,8},{1,13},{4,12},{5,9},{8,0},{9,5},{12,4},{13,1},{2,10},{3,15},... | collective-permute-start | bytes 12296 | tf_op jit(solution)/shard_map/ppermute | solution.py:647
  31.1 3.6 %collective-permute-start.16 = (f32[8,128]{1,0:T(8,128)S(1)}, f32[8,128]{1,0:T(8,128)S(1)}, u32[]{:S(2)}, u32[]{:S(2)}) collective-permute-start(f32[8,128]{1,0:T(8,128)S(1)} %add.3.refs_0_), channel_id=1, source_target_pairs={{0,4},{4,0},{8,12},{12,8},{1,5},{5,1},{9,13},{13,9},{2,6},{6,2},{1... | collective-permute-start | bytes 12296 | tf_op jit(solution)/shard_map/ppermute | solution.py:642
  34.5 1.2 %collective-permute-start.17 = (f32[8,128]{1,0:T(8,128)S(1)}, f32[8,128]{1,0:T(8,128)S(1)}, u32[]{:S(2)}, u32[]{:S(2)}) collective-permute-start(f32[8,128]{1,0:T(8,128)S(1)} %collective-permute-done.15.refs_1_), channel_id=1, source_target_pairs={{0,1},{1,0},{2,3},{3,2},{4,5},{5,4},{6,7},{7,6},{8,9},{9,8},{10,11... | collective-permute-start | bytes 12296 | tf_op jit(solution)/shard_map/ppermute | solution.py:642

commit v5 on v4

--- a/solution.py
+++ b/solution.py
@@ -101,10 +101,10 @@
     ones = jnp.ones((8, ordered.shape[2]), F32)
     scale = weights[...]
     rows = []
-    for low, high in level_pairs(levels):
-        product = ordered[low] * scale * ordered[high]
-        total = lax.dot_general(ones, product, NT, precision=lax.Precision.HIGHEST, preferred_element_type=F32)
-        rows.append(total[:1])
+    pairs = level_pairs(levels)
+    stacked = jnp.concatenate([ordered[low] * scale * ordered[high] for low, high in pairs], axis=0)
+    totals = lax.dot_general(ones, stacked, NT, precision=lax.Precision.HIGHEST, preferred_element_type=F32)
+    rows += [totals[:1, index * slots : (index + 1) * slots] for index in range(len(pairs))]
     spare = record_rows(levels) - 4 - len(rows)
     if spare:
         rows.append(jnp.zeros((spare, slots), F32))

time: 36.7 us -> 36.8 us (level)
  no operation moved by 1% of the time
where the time goes in v5:
time: 36.8 us; the launch traced here: 36.6 us
  starting transfers between devices  16.8 us (46%)
  waiting for transfers between devices  10.1 us (27%)
  Pallas kernels  8.23 us (22%)
  between operations  1.41 us (4%)
    ppermute x14, starting transfers between devices, exchanged(): return lax.ppermute(value, axis, [(i, i ^ mask) for i in range(count)])  11.1 us
    ppermute x14, waiting for transfers between devices, exchanged(): return lax.ppermute(value, axis, [(i, i ^ mask) for i in range(count)])  7.77 us
    ppermute x3, starting transfers between devices, level_parts(): lax.ppermute(value, 'lev', [(i, (i + k) % count) for i in range(count)])  4.67 us
    ppermute x1, waiting for transfers between devices, split_exchange(): return lax.ppermute(value, ('tile', 'sub'), pairs)  2.32 us
    pallas_call x1, Pallas kernels, body(): pl.pallas_call(functools.partial(evolve, levels), out_shape=(vmem(*shape)...  2.29 us
    pallas_call x1, Pallas kernels, body(): pl.pallas_call(functools.partial(gains, levels, slots, len(records)), out...  2.11 us
    pallas_call x1, Pallas kernels, body(): pl.pallas_call(functools.partial(assemble, len(messages)), out_shape=(vme...  1.2 us
    pallas_call x1, Pallas kernels, body(): pl.pallas_call(functools.partial(prepare, width.bit_length() - 1), out_sh...  1.17 us
  transfers between devices with their start and end apart: 18, of which 7 were waited for; matrix products, arithmetic and copies ran while one was open for 0% of the time, Pallas kernels for 11%

profile of v5, /device:TPU:0, one launch (start us, length us, event | category | flops | bytes accessed | tf_op | source)
XLA Modules:
  0.0 36.6 jit_solution(749770693635458144)
XLA Ops:
  1.3 1.2 %prepare.1 = (f32[96,128]{1,0:T(8,128)S(1)}, f32[4,128,128]{2,1,0:T(8,128)S(1)}, f32[64,616]{1,0:T(8,128)S(1)}, f32[8,128]{1,0:T(8,128)S(1)}, f32[1,616]{1,0:T(1,128)S(1)}, /*index=5*/f32[8,128]{1,0:T(8,128)S(1)}) custom-call(s32[1]{0:T(128)S(6)} %copy.18.count, f32[2]{0:T(128)} %diffusion.1, f32[2]{0:T(128)} %vertical.1, f32[2]{0:T(128)} %prior.1, ...), custom_call_target="tpu_custom_call" | custom-call | tf_op jit(solution)/shard_map/prepare/pallas_call | solution.py:697
  2.5 3.0 %collective-permute-start.9 = (f32[64,616]{1,0:T(8,128)S(1)}, f32[64,616]{1,0:T(8,128)S(1)}, u32[]{:S(2)}, u32[]{:S(2)}) collective-permute-start(f32[64,616]{1,0:T(8,128)S(1)} %get-tuple-element.25.refs_0_), channel_id=1, source_target_pairs={{0,2},{2,0},{1,3},{3,1},{4,6},{6,4},{5,7},{7,5},{8,10},{10,8},{9,1... | collective-permute-start | bytes 473096 | tf_op jit(solution)/shard_map/ppermute | solution.py:667
  5.5 0.1 collective-permute-start.8
  5.6 4.1 %collective-permute-start.5 = (f32[96,128]{1,0:T(8,128)S(1)}, f32[96,128]{1,0:T(8,128)S(1)}, u32[]{:S(2)}, u32[]{:S(2)}) collective-permute-start(f32[96,128]{1,0:T(8,128)S(1)} %get-tuple-element.21.refs_2_), channel_id=1, source_target_pairs={{0,12},{4,8},{8,4},{12,0},{1,13},{5,9},{9,5},{13,1},{2,14},{6,10},... | collective-permute-start | bytes 147464 | tf_op jit(solution)/shard_map/ppermute | solution.py:642
  9.6 0.0 collective-permute-start.3
  9.6 0.6 %collective-permute-start.1 = (f32[96,128]{1,0:T(8,128)S(1)}, f32[96,128]{1,0:T(8,128)S(1)}, u32[]{:S(2)}, u32[]{:S(2)}) collective-permute-start(f32[96,128]{1,0:T(8,128)S(1)} %get-tuple-element.21.refs_2_), channel_id=1, source_target_pairs={{0,4},{4,0},{8,12},{12,8},{1,5},{5,1},{9,13},{13,9},{2,6},{6,2},{1... | collective-permute-start | bytes 147464 | tf_op jit(solution)/shard_map/ppermute | solution.py:642
  10.2 2.1 %collective-permute-done.5.refs_8_ = f32[96,128]{1,0:T(8,128)S(1)} collective-permute-done((f32[96,128]{1,0:T(8,128)S(1)}, f32[96,128]{1,0:T(8,128)S(1)}, u32[]{:S(2)}, u32[]{:S(2)}) %collective-permute-start.5) | collective-permute-done | bytes 49184 | tf_op jit(solution)/shard_map/ppermute | solution.py:642
  12.3 0.0 collective-permute-start
  12.3 2.3 %collective-permute-done.3.refs_6_ = f32[96,128]{1,0:T(8,128)S(1)} collective-permute-done((f32[96,128]{1,0:T(8,128)S(1)}, f32[96,128]{1,0:T(8,128)S(1)}, u32[]{:S(2)}, u32[]{:S(2)}) %collective-permute-start.3) | collective-permute-done | bytes 49184 | tf_op jit(solution)/shard_map/ppermute | solution.py:642
  14.6 0.0 collective-permute-start.6
  14.6 0.0 collective-permute-done.1.refs_4_
  14.6 0.5 %collective-permute-start.4 = (f32[96,128]{1,0:T(8,128)S(1)}, f32[96,128]{1,0:T(8,128)S(1)}, u32[]{:S(2)}, u32[]{:S(2)}) collective-permute-start(f32[96,128]{1,0:T(8,128)S(1)} %collective-permute-done.3.refs_6_), channel_id=1, source_target_pairs={{0,1},{1,0},{2,3},{3,2},{4,5},{5,4},{6,7},{7,6},{8,9},{9,8},{10,11... | collective-permute-start | bytes 147464 | tf_op jit(solution)/shard_map/ppermute | solution.py:642
  15.1 0.0 collective-permute-done.9.refs_1_
  15.1 0.1 collective-permute-start.2
  15.2 0.7 %compose.1 = f32[8,128]{1,0:T(8,128)S(1)} custom-call(f32[64,616]{1,0:T(8,128)S(1)} %get-tuple-element.25.refs_0_, f32[64,616]{1,0:T(8,128)S(1)} %collective-permute-done.9.refs_1_, f32[1,616]{1,0:T(1,128)S(1)} %get-tuple-element.26.refs_2_, f32[8,128]{1,0:T(8,128)S(1)} %get-tuple-element.27.refs_3_), custom_call_target="tpu_custom_call" | custom-call | tf_op jit(solution)/shard_map/compose/pallas_call | solution.py:728
  15.9 0.0 collective-permute-done.refs_3_
  15.9 1.7 %collective-permute-start.12 = (f32[8,128]{1,0:T(8,128)S(1)}, f32[8,128]{1,0:T(8,128)S(1)}, u32[]{:S(2)}, u32[]{:S(2)}) collective-permute-start(f32[8,128]{1,0:T(8,128)S(1)} %compose.1), channel_id=1, source_target_pairs={{0,12},{4,8},{8,4},{12,0},{1,13},{5,9},{9,5},{13,1},{2,14},{6,10},... | collective-permute-start | bytes 12296 | tf_op jit(solution)/shard_map/ppermute | solution.py:642
  17.6 0.0 collective-permute-done.6.refs_9_
  17.6 0.4 %collective-permute-start.11 = (f32[8,128]{1,0:T(8,128)S(1)}, f32[8,128]{1,0:T(8,128)S(1)}, u32[]{:S(2)}, u32[]{:S(2)}) collective-permute-start(f32[8,128]{1,0:T(8,128)S(1)} %compose.1), channel_id=1, source_target_pairs={{0,8},{4,12},{8,0},{12,4},{1,9},{5,13},{9,1},{13,5},{2,10},{6,14},... | collective-permute-start | bytes 12296 | tf_op jit(solution)/shard_map/ppermute | solution.py:642
  18.0 0.0 collective-permute-done.4.refs_7_
  18.0 2.4 %collective-permute-start.10 = (f32[8,128]{1,0:T(8,128)S(1)}, f32[8,128]{1,0:T(8,128)S(1)}, u32[]{:S(2)}, u32[]{:S(2)}) collective-permute-start(f32[8,128]{1,0:T(8,128)S(1)} %compose.1), channel_id=1, source_target_pairs={{0,4},{4,0},{8,12},{12,8},{1,5},{5,1},{9,13},{13,9},{2,6},{6,2},{1... | collective-permute-start | bytes 12296 | tf_op jit(solution)/shard_map/ppermute | solution.py:642
  20.4 0.0 collective-permute-done.2.refs_5_
  20.4 0.0 copy-done.4
  20.4 0.0 copy-done.3
  20.4 1.2 %assemble.1 = (f32[192,128]{1,0:T(8,128)S(1)}, f32[8,128]{1,0:T(8,128)S(1)}) custom-call(s32[4,8]{1,0:T(4,128)S(1)} %bitcast.18, s32[4,8]{1,0:T(4,128)S(1)} %bitcast.19, f32[96,128]{1,0:T(8,128)S(1)} %get-tuple-element.21.refs_2_, f32[96,128]{1,0:T(8,128)S(1)} %collective-permute-done.refs_3_, f32[96,128]{1,0:T(8,128)S(1)} %collective-permute-done.1.refs_4_, ...), custom_call_target="tpu_custom_call" | custom-call | tf_op jit(solution)/shard_map/assemble/pallas_call | solution.py:741
  21.6 1.6 %collective-permute-start.7 = (f32[192,128]{1,0:T(8,128)S(1)}, f32[192,128]{1,0:T(8,128)S(1)}, u32[]{:S(2)}, u32[]{:S(2)}) collective-permute-start(f32[192,128]{1,0:T(8,128)S(1)} %get-tuple-element.22.refs_1_), channel_id=1, source_target_pairs={{0,2},{2,0},{1,3},{3,1},{4,6},{6,4},{5,7},{7,5},{8,10},{10,8},{9,1... | collective-permute-start | bytes 294920 | tf_op jit(solution)/shard_map/ppermute | solution.py:667
  23.1 0.0 collective-permute-done.12
  23.1 0.0 collective-permute-done.11
  23.1 0.0 collective-permute-done.10
  23.2 0.1 collective-permute-start.13
  23.2 1.2 %collective-permute-done.13.refs_2_ = f32[32,128]{1,0:T(8,128)S(1)} collective-permute-done((f32[32,128]{1,0:T(8,128)S(1)}, f32[32,128]{1,0:T(8,128)S(1)}, u32[]{:S(2)}, u32[]{:S(2)}) %collective-permute-start.13) | collective-permute-done | bytes 16416 | tf_op jit(solution)/shard_map/ppermute | solution.py:642
  24.4 2.1 %gains.1 = (f32[12,128,128]{2,1,0:T(8,128)S(1)}, f32[2,12,8,128]{3,2,1,0:T(8,128)S(1)}, f32[12,128,128]{2,1,0:T(8,128)S(1)}, f32[12,32,128]{2,1,0:T(8,128)S(1)}) custom-call(f32[8,128]{1,0:T(8,128)S(1)} %get-tuple-element.24.refs_0_, f32[32,128]{1,0:T(8,128)S(1)} %pad_maximum_fusion.refs_1_, f32[32,128]{1,0:T(8,128)S(1)} %collective-permute-done.13.refs_2_), custom_call_target="tpu_custom_call" | custom-call | tf_op jit(solution)/shard_map/gains/pallas_call | solution.py:756
  26.5 0.0 collective-permute-done.7.refs_2_
  26.5 0.0 collective-permute-done.8.refs_4_
  26.5 0.0 copy-start
  26.6 0.0 copy-start.1
  26.6 0.0 copy-start.2
  26.6 2.3 %evolve.1 = (f32[128,128]{1,0:T(8,128)S(1)}, f32[8,128]{1,0:T(8,128)S(1)}) custom-call(f32[8,128]{1,0:T(8,128)S(1)} %get-tuple-element.20.refs_0_, f32[192,128]{1,0:T(8,128)S(1)} %get-tuple-element.22.refs_1_, f32[192,128]{1,0:T(8,128)S(1)} %collective-permute-done.7.refs_2_, f32[4,128,128]{2,1,0:T(8,128)S(1)} %get-tuple-element.23.refs_3_, ...), custom_call_target="tpu_custom_call" | custom-call | tf_op jit(solution)/shard_map/evolve/pallas_call | solution.py:766
  28.9 0.2 collective-permute-start.14
  29.1 1.0 %collective-permute-done.14 = f32[8,128]{1,0:T(8,128)S(1)} collective-permute-done((f32[8,128]{1,0:T(8,128)S(1)}, f32[8,128]{1,0:T(8,128)S(1)}, u32[]{:S(2)}, u32[]{:S(2)}) %collective-permute-start.14) | collective-permute-done | bytes 4128 | tf_op jit(solution)/shard_map/ppermute | solution.py:642
  30.1 1.1 %collective-permute-start.15 = (f32[8,128]{1,0:T(8,128)S(1)}, f32[8,128]{1,0:T(8,128)S(1)}, u32[]{:S(2)}, u32[]{:S(2)}) collective-permute-start(f32[8,128]{1,0:T(8,128)S(1)} %add.3.refs_0_), channel_id=1, source_target_pairs={{0,8},{1,13},{4,12},{5,9},{8,0},{9,5},{12,4},{13,1},{2,10},{3,15},... | collective-permute-start | bytes 12296 | tf_op jit(solution)/shard_map/ppermute | solution.py:647
  31.2 1.1 %collective-permute-start.16 = (f32[8,128]{1,0:T(8,128)S(1)}, f32[8,128]{1,0:T(8,128)S(1)}, u32[]{:S(2)}, u32[]{:S(2)}) collective-permute-start(f32[8,128]{1,0:T(8,128)S(1)} %add.3.refs_0_), channel_id=1, source_target_pairs={{0,4},{4,0},{8,12},{12,8},{1,5},{5,1},{9,13},{13,9},{2,6},{6,2},{1... | collective-permute-start | bytes 12296 | tf_op jit(solution)/shard_map/ppermute | solution.py:642
  32.3 2.3 %collective-permute-done.15.refs_1_ = f32[8,128]{1,0:T(8,128)S(1)} collective-permute-done((f32[8,128]{1,0:T(8,128)S(1)}, f32[8,128]{1,0:T(8,128)S(1)}, u32[]{:S(2)}, u32[]{:S(2)}) %collective-permute-start.15) | collective-permute-done | bytes 4128 | tf_op jit(solution)/shard_map/ppermute | solution.py:647
  34.6 0.0 collective-permute-start.17
  34.6 0.1 collective-permute-done.16.refs_2_
  34.8 1.0 %collective-permute-done.17.refs_3_ = f32[8,128]{1,0:T(8,128)S(1)} collective-permute-done((f32[8,128]{1,0:T(8,128)S(1)}, f32[8,128]{1,0:T(8,128)S(1)}, u32[]{:S(2)}, u32[]{:S(2)}) %collective-permute-start.17) | collective-permute-done | bytes 4128 | tf_op jit(solution)/shard_map/ppermute | solution.py:642
  35.8 0.0 copy-done
  35.8 0.8 %update.1 = (f32[128,128]{1,0:T(8,128)}, f32[128,128]{1,0:T(8,128)}, f32[128,128]{1,0:T(8,128)}) custom-call(f32[8,128]{1,0:T(8,128)S(1)} %add.3.refs_0_, f32[8,128]{1,0:T(8,128)S(1)} %collective-permute-done.15.refs_1_, f32[8,128]{1,0:T(8,128)S(1)} %collective-permute-done.16.refs_2_, f32[8,128]{1,0:T(8,128)S(1)} %collective-permute-done.17.refs_3_, ...), custom_call_target="tpu_custom_call" | custom-call | tf_op jit(solution)/shard_map/update/pallas_call | solution.py:800
  (6 shorter events, 0.0 us)
Async XLA Ops:
  2.5 12.7 %collective-permute-start.9 = (f32[64,616]{1,0:T(8,128)S(1)}, f32[64,616]{1,0:T(8,128)S(1)}, u32[]{:S(2)}, u32[]{:S(2)}) collective-permute-start(f32[64,616]{1,0:T(8,128)S(1)} %get-tuple-element.25.refs_0_), channel_id=1, source_target_pairs={{0,2},{2,0},{1,3},{3,1},{4,6},{6,4},{5,7},{7,5},{8,10},{10,8},{9,1... | collective-permute-start | bytes 473096 | tf_op jit(solution)/shard_map/ppermute | solution.py:667
  5.5 21.0 %collective-permute-start.8 = (f32[4,128,128]{2,1,0:T(8,128)S(1)}, f32[4,128,128]{2,1,0:T(8,128)S(1)}, u32[]{:S(2)}, u32[]{:S(2)}) collective-permute-start(f32[4,128,128]{2,1,0:T(8,128)S(1)} %get-tuple-element.23.refs_3_), channel_id=1, source_target_pairs={{0,2},{2,0},{1,3},{3,1},{4,6},{6,4},{5,7},{7,5},{8,10},{10,8},{9,1... | collective-permute-start | bytes 786440 | tf_op jit(solution)/shard_map/ppermute | solution.py:667
  5.6 6.7 %collective-permute-start.5 = (f32[96,128]{1,0:T(8,128)S(1)}, f32[96,128]{1,0:T(8,128)S(1)}, u32[]{:S(2)}, u32[]{:S(2)}) collective-permute-start(f32[96,128]{1,0:T(8,128)S(1)} %get-tuple-element.21.refs_2_), channel_id=1, source_target_pairs={{0,12},{4,8},{8,4},{12,0},{1,13},{5,9},{9,5},{13,1},{2,14},{6,10},... | collective-permute-start | bytes 147464 | tf_op jit(solution)/shard_map/ppermute | solution.py:642
  9.6 5.0 %collective-permute-start.3 = (f32[96,128]{1,0:T(8,128)S(1)}, f32[96,128]{1,0:T(8,128)S(1)}, u32[]{:S(2)}, u32[]{:S(2)}) collective-permute-start(f32[96,128]{1,0:T(8,128)S(1)} %get-tuple-element.21.refs_2_), channel_id=1, source_target_pairs={{0,8},{4,12},{8,0},{12,4},{1,9},{5,13},{9,1},{13,5},{2,10},{6,14},... | collective-permute-start | bytes 147464 | tf_op jit(solution)/shard_map/ppermute | solution.py:642
  9.6 5.0 %collective-permute-start.1 = (f32[96,128]{1,0:T(8,128)S(1)}, f32[96,128]{1,0:T(8,128)S(1)}, u32[]{:S(2)}, u32[]{:S(2)}) collective-permute-start(f32[96,128]{1,0:T(8,128)S(1)} %get-tuple-element.21.refs_2_), channel_id=1, source_target_pairs={{0,4},{4,0},{8,12},{12,8},{1,5},{5,1},{9,13},{13,9},{2,6},{6,2},{1... | collective-permute-start | bytes 147464 | tf_op jit(solution)/shard_map/ppermute | solution.py:642
  12.3 3.6 %collective-permute-start = (f32[96,128]{1,0:T(8,128)S(1)}, f32[96,128]{1,0:T(8,128)S(1)}, u32[]{:S(2)}, u32[]{:S(2)}) collective-permute-start(f32[96,128]{1,0:T(8,128)S(1)} %get-tuple-element.21.refs_2_), channel_id=1, source_target_pairs={{0,1},{1,0},{2,3},{3,2},{4,5},{5,4},{6,7},{7,6},{8,9},{9,8},{10,11... | collective-permute-start | bytes 147464 | tf_op jit(solution)/shard_map/ppermute | solution.py:642
  14.6 3.0 %collective-permute-start.6 = (f32[96,128]{1,0:T(8,128)S(1)}, f32[96,128]{1,0:T(8,128)S(1)}, u32[]{:S(2)}, u32[]{:S(2)}) collective-permute-start(f32[96,128]{1,0:T(8,128)S(1)} %collective-permute-done.5.refs_8_), channel_id=1, source_target_pairs={{0,1},{1,0},{2,3},{3,2},{4,5},{5,4},{6,7},{7,6},{8,9},{9,8},{10,11... | collective-permute-start | bytes 147464 | tf_op jit(solution)/shard_map/ppermute | solution.py:642
  14.6 3.4 %collective-permute-start.4 = (f32[96,128]{1,0:T(8,128)S(1)}, f32[96,128]{1,0:T(8,128)S(1)}, u32[]{:S(2)}, u32[]{:S(2)}) collective-permute-start(f32[96,128]{1,0:T(8,128)S(1)} %collective-permute-done.3.refs_6_), channel_id=1, source_target_pairs={{0,1},{1,0},{2,3},{3,2},{4,5},{5,4},{6,7},{7,6},{8,9},{9,8},{10,11... | collective-permute-start | bytes 147464 | tf_op jit(solution)/shard_map/ppermute | solution.py:642
  15.1 5.2 %collective-permute-start.2 = (f32[96,128]{1,0:T(8,128)S(1)}, f32[96,128]{1,0:T(8,128)S(1)}, u32[]{:S(2)}, u32[]{:S(2)}) collective-permute-start(f32[96,128]{1,0:T(8,128)S(1)} %collective-permute-done.1.refs_4_), channel_id=1, source_target_pairs={{0,1},{1,0},{2,3},{3,2},{4,5},{5,4},{6,7},{7,6},{8,9},{9,8},{10,11... | collective-permute-start | bytes 147464 | tf_op jit(solution)/shard_map/ppermute | solution.py:642
  15.2 5.2 %copy-start.4 = (s32[8,4]{0,1:T(4,128)S(1)}, s32[8,4]{0,1:T(4,128)}, u32[]{:S(2)}) copy-start(s32[8,4]{0,1:T(4,128)} %param.24) | copy-start | bytes 388
  15.9 4.5 %copy-start.3 = (s32[8,4]{0,1:T(4,128)S(1)}, s32[8,4]{0,1:T(4,128)}, u32[]{:S(2)}) copy-start(s32[8,4]{0,1:T(4,128)} %param.23) | copy-start | bytes 388
  15.9 7.2 %collective-permute-start.12 = (f32[8,128]{1,0:T(8,128)S(1)}, f32[8,128]{1,0:T(8,128)S(1)}, u32[]{:S(2)}, u32[]{:S(2)}) collective-permute-start(f32[8,128]{1,0:T(8,128)S(1)} %compose.1), channel_id=1, source_target_pairs={{0,12},{4,8},{8,4},{12,0},{1,13},{5,9},{9,5},{13,1},{2,14},{6,10},... | collective-permute-start | bytes 12296 | tf_op jit(solution)/shard_map/ppermute | solution.py:642
  17.6 5.6 %collective-permute-start.11 = (f32[8,128]{1,0:T(8,128)S(1)}, f32[8,128]{1,0:T(8,128)S(1)}, u32[]{:S(2)}, u32[]{:S(2)}) collective-permute-start(f32[8,128]{1,0:T(8,128)S(1)} %compose.1), channel_id=1, source_target_pairs={{0,8},{4,12},{8,0},{12,4},{1,9},{5,13},{9,1},{13,5},{2,10},{6,14},... | collective-permute-start | bytes 12296 | tf_op jit(solution)/shard_map/ppermute | solution.py:642
  18.0 5.1 %collective-permute-start.10 = (f32[8,128]{1,0:T(8,128)S(1)}, f32[8,128]{1,0:T(8,128)S(1)}, u32[]{:S(2)}, u32[]{:S(2)}) collective-permute-start(f32[8,128]{1,0:T(8,128)S(1)} %compose.1), channel_id=1, source_target_pairs={{0,4},{4,0},{8,12},{12,8},{1,5},{5,1},{9,13},{13,9},{2,6},{6,2},{1... | collective-permute-start | bytes 12296 | tf_op jit(solution)/shard_map/ppermute | solution.py:642
  21.6 5.0 %collective-permute-start.7 = (f32[192,128]{1,0:T(8,128)S(1)}, f32[192,128]{1,0:T(8,128)S(1)}, u32[]{:S(2)}, u32[]{:S(2)}) collective-permute-start(f32[192,128]{1,0:T(8,128)S(1)} %get-tuple-element.22.refs_1_), channel_id=1, source_target_pairs={{0,2},{2,0},{1,3},{3,1},{4,6},{6,4},{5,7},{7,5},{8,10},{10,8},{9,1... | collective-permute-start | bytes 294920 | tf_op jit(solution)/shard_map/ppermute | solution.py:667
  23.2 1.2 %collective-permute-start.13 = (f32[32,128]{1,0:T(8,128)S(1)}, f32[32,128]{1,0:T(8,128)S(1)}, u32[]{:S(2)}, u32[]{:S(2)}) collective-permute-start(f32[32,128]{1,0:T(8,128)S(1)} %pad_maximum_fusion.refs_1_), channel_id=1, source_target_pairs={{0,1},{1,0},{2,3},{3,2},{4,5},{5,4},{6,7},{7,6},{8,9},{9,8},{10,11... | collective-permute-start | bytes 49160 | tf_op jit(solution)/shard_map/ppermute | solution.py:642
  26.5 9.2 %copy-start = (f32[1,128,128]{2,1,0:T(8,128)S(1)}, f32[1,128,128]{2,1,0:T(8,128)}, u32[]{:S(2)}) copy-start(f32[1,128,128]{2,1,0:T(8,128)} %param.17) | copy-start | bytes 196612
  26.6 9.2 %copy-start.1 = (f32[1,128,128]{2,1,0:T(8,128)S(1)}, f32[1,128,128]{2,1,0:T(8,128)}, u32[]{:S(2)}) copy-start(f32[1,128,128]{2,1,0:T(8,128)} %param.16) | copy-start | bytes 196612
  26.6 9.2 %copy-start.2 = (f32[1,128,128]{2,1,0:T(8,128)S(1)}, f32[1,128,128]{2,1,0:T(8,128)}, u32[]{:S(2)}) copy-start(f32[1,128,128]{2,1,0:T(8,128)} %param.15) | copy-start | bytes 196612
  28.9 1.2 %collective-permute-start.14 = (f32[8,128]{1,0:T(8,128)S(1)}, f32[8,128]{1,0:T(8,128)S(1)}, u32[]{:S(2)}, u32[]{:S(2)}) collective-permute-start(f32[8,128]{1,0:T(8,128)S(1)} %get-tuple-element.32), channel_id=1, source_target_pairs={{0,1},{1,0},{2,3},{3,2},{4,5},{5,4},{6,7},{7,6},{8,9},{9,8},{10,11... | collective-permute-start | bytes 12296 | tf_op jit(solution)/shard_map/ppermute | solution.py:642
  30.1 4.5 %collective-permute-start.15 = (f32[8,128]{1,0:T(8,128)S(1)}, f32[8,128]{1,0:T(8,128)S(1)}, u32[]{:S(2)}, u32[]{:S(2)}) collective-permute-start(f32[8,128]{1,0:T(8,128)S(1)} %add.3.refs_0_), channel_id=1, source_target_pairs={{0,8},{1,13},{4,12},{5,9},{8,0},{9,5},{12,4},{13,1},{2,10},{3,15},... | collective-permute-start | bytes 12296 | tf_op jit(solution)/shard_map/ppermute | solution.py:647
  31.2 3.6 %collective-permute-start.16 = (f32[8,128]{1,0:T(8,128)S(1)}, f32[8,128]{1,0:T(8,128)S(1)}, u32[]{:S(2)}, u32[]{:S(2)}) collective-permute-start(f32[8,128]{1,0:T(8,128)S(1)} %add.3.refs_0_), channel_id=1, source_target_pairs={{0,4},{4,0},{8,12},{12,8},{1,5},{5,1},{9,13},{13,9},{2,6},{6,2},{1... | collective-permute-start | bytes 12296 | tf_op jit(solution)/shard_map/ppermute | solution.py:642
  34.6 1.2 %collective-permute-start.17 = (f32[8,128]{1,0:T(8,128)S(1)}, f32[8,128]{1,0:T(8,128)S(1)}, u32[]{:S(2)}, u32[]{:S(2)}) collective-permute-start(f32[8,128]{1,0:T(8,128)S(1)} %collective-permute-done.15.refs_1_), channel_id=1, source_target_pairs={{0,1},{1,0},{2,3},{3,2},{4,5},{5,4},{6,7},{7,6},{8,9},{9,8},{10,11... | collective-permute-start | bytes 12296 | tf_op jit(solution)/shard_map/ppermute | solution.py:642
